TPU v7x, 8 devices: a whole 2x2x1 slice. The times are simulated.
8 devices in a mesh: dp: 1 (over z), tp: 2 (over y), sp: 4 (over x, core).
Axes of the slice: x: 2, y: 2, z: 1, core: 2. Of those that a mesh axis runs over, the one named last changes fastest.
Arguments:
- hidden: bfloat16 [4, 128, 4096], P(None, 'dp')
- start_pos: int32 [128], P('dp')
- k_cache: bfloat16 [128, 1024, 8, 128], P('dp', 'sp', 'tp')
- v_cache: bfloat16 [128, 1024, 8, 128], P('dp', 'sp', 'tp')
- w_q: bfloat16 [4096, 4096], P(None, 'tp')
- w_k: bfloat16 [4096, 1024], P(None, 'tp')
- w_v: bfloat16 [4096, 1024], P(None, 'tp')
- w_o: bfloat16 [4096, 4096], P('tp')
- w_gate: bfloat16 [4096, 12288], P(None, 'tp')
- w_up: bfloat16 [4096, 12288], P(None, 'tp')
- w_down: bfloat16 [12288, 4096], P('tp')
- attn_norm: bfloat16 [4096], replicated
- mlp_norm: bfloat16 [4096], replicated
- q_gain: bfloat16 [128], replicated
- k_gain: bfloat16 [128], replicated
Outputs:
- output 1: bfloat16 [4, 128, 4096], P(None, 'dp')
- output 2: bfloat16 [128, 1024, 8, 128], P('dp', 'sp', 'tp')
- output 3: bfloat16 [128, 1024, 8, 128], P('dp', 'sp', 'tp')
All inputs are finite; a program needn't handle non-finite values.
Results may differ from a plain program's by a relative error of at most 0.00856035.
Values sent between devices are 32-bit elements.
A program may use at most 1.5 GiB of HBM per device.

v0:
```python
import jax
import jax.numpy as jnp
from jax import lax
from jax.sharding import PartitionSpec as P

ROPE_BASE = 1000000.0
NORM_EPS = 1e-06
NEG_BIG = -1e30


def rms_scale(values, gain_vec):
    wide_vals = values.astype(jnp.float32)
    inv_rms = lax.rsqrt(jnp.mean(wide_vals * wide_vals, axis=-1, keepdims=True) + NORM_EPS)
    return wide_vals * inv_rms * gain_vec.astype(jnp.float32)


def apply_rope(vector, tok_pos):
    head_dim = vector.shape[-1]
    half_dim = head_dim // 2
    freqs = ROPE_BASE ** (-(jnp.arange(half_dim, dtype=jnp.float32) * (2.0 / head_dim)))
    angles = tok_pos.astype(jnp.float32)[:, None] * freqs[None, :]
    cos_tab = jnp.cos(angles)[:, None, :]
    sin_tab = jnp.sin(angles)[:, None, :]
    lower_half = vector[..., :half_dim]
    upper_half = vector[..., half_dim:]
    return jnp.concatenate([lower_half * cos_tab - upper_half * sin_tab, upper_half * cos_tab + lower_half * sin_tab], axis=-1)


def solution(mesh):
    cache_spec = P('dp', 'sp', 'tp', None)
    col_spec = P(None, 'tp')
    row_spec = P('tp', None)
    in_specs = (P(None, 'dp', None), P('dp'), cache_spec, cache_spec, col_spec, col_spec, col_spec, row_spec,
                col_spec, col_spec, row_spec, P(), P(), P(), P())
    out_specs = (P(None, 'dp', None), cache_spec, cache_spec)

    def shard_body(hidden, start_pos, k_cache, v_cache, w_q, w_k, w_v, w_o, w_gate, w_up, w_down, attn_norm, mlp_norm, q_gain, k_gain):
        n_steps, n_batch = hidden.shape[0], hidden.shape[1]
        seq_blk, kv_loc, head_dim = k_cache.shape[1], k_cache.shape[2], k_cache.shape[3]
        heads_loc = w_q.shape[1] // head_dim
        groups = heads_loc // kv_loc
        score_scale = head_dim ** -0.5
        blk_start = lax.axis_index('sp') * seq_blk
        blk_pos = blk_start + jnp.arange(seq_blk)
        old_mask = (blk_pos[None, :] < start_pos[:, None])[:, None, None, :]
        new_keys = []
        new_vals = []
        owned = []
        outputs = []
        for step_idx in range(n_steps):
            tok_pos = start_pos + step_idx
            x_tok = hidden[step_idx]
            normed = rms_scale(x_tok, attn_norm).astype(jnp.bfloat16)
            q_raw = jnp.dot(normed, w_q, preferred_element_type=jnp.float32).reshape(n_batch, heads_loc, head_dim)
            k_raw = jnp.dot(normed, w_k, preferred_element_type=jnp.float32).reshape(n_batch, kv_loc, head_dim)
            v_new = jnp.dot(normed, w_v, preferred_element_type=jnp.float32).astype(jnp.bfloat16).reshape(n_batch, kv_loc, head_dim)
            q_rot = apply_rope(rms_scale(q_raw, q_gain), tok_pos).astype(jnp.bfloat16).reshape(n_batch, kv_loc, groups, head_dim)
            k_new = apply_rope(rms_scale(k_raw, k_gain), tok_pos).astype(jnp.bfloat16)
            new_keys.append(k_new)
            new_vals.append(v_new)
            owned.append((tok_pos >= blk_start) & (tok_pos < blk_start + seq_blk))
            key_stack = jnp.stack(new_keys, axis=1)
            val_stack = jnp.stack(new_vals, axis=1)
            new_mask = jnp.stack(owned, axis=1)[:, None, None, :]
            old_scores = jnp.einsum('bkgh,bskh->bkgs', q_rot, k_cache, preferred_element_type=jnp.float32) * score_scale
            old_scores = jnp.where(old_mask, old_scores, NEG_BIG)
            new_scores = jnp.einsum('bkgh,bjkh->bkgj', q_rot, key_stack, preferred_element_type=jnp.float32) * score_scale
            new_scores = jnp.where(new_mask, new_scores, NEG_BIG)
            blk_max = jnp.maximum(old_scores.max(axis=-1), new_scores.max(axis=-1))
            old_probs = jnp.where(old_mask, jnp.exp(old_scores - blk_max[..., None]), 0.0)
            new_probs = jnp.where(new_mask, jnp.exp(new_scores - blk_max[..., None]), 0.0)
            blk_sum = old_probs.sum(axis=-1) + new_probs.sum(axis=-1)
            blk_out = (jnp.einsum('bkgs,bskh->bkgh', old_probs.astype(jnp.bfloat16), v_cache, preferred_element_type=jnp.float32)
                       + jnp.einsum('bkgj,bjkh->bkgh', new_probs.astype(jnp.bfloat16), val_stack, preferred_element_type=jnp.float32))
            packed = jnp.concatenate([blk_out, blk_max[..., None], blk_sum[..., None]], axis=-1)
            gathered = lax.all_gather(packed, 'sp')
            shard_max = gathered[..., head_dim]
            top_max = shard_max.max(axis=0)
            weights = jnp.exp(shard_max - top_max)
            total = (weights * gathered[..., head_dim + 1]).sum(axis=0)
            attn_vals = (weights[..., None] * gathered[..., :head_dim]).sum(axis=0) / total[..., None]
            attn_in = attn_vals.reshape(n_batch, heads_loc * head_dim).astype(jnp.bfloat16)
            attn_out = lax.psum(jnp.dot(attn_in, w_o, preferred_element_type=jnp.float32), 'tp')
            residual = (x_tok.astype(jnp.float32) + attn_out).astype(jnp.bfloat16)
            mlp_in = rms_scale(residual, mlp_norm).astype(jnp.bfloat16)
            gate_act = jnp.dot(mlp_in, w_gate, preferred_element_type=jnp.float32)
            up_proj = jnp.dot(mlp_in, w_up, preferred_element_type=jnp.float32)
            mlp_act = (jax.nn.silu(gate_act) * up_proj).astype(jnp.bfloat16)
            down_sum = lax.psum(jnp.dot(mlp_act, w_down, preferred_element_type=jnp.float32), 'tp')
            outputs.append((residual.astype(jnp.float32) + down_sum).astype(jnp.bfloat16))
        offsets = blk_pos[None, :] - start_pos[:, None]
        k_out = k_cache
        v_out = v_cache
        for step_idx in range(n_steps):
            hit = (offsets == step_idx)[:, :, None, None]
            k_out = jnp.where(hit, new_keys[step_idx][:, None], k_out)
            v_out = jnp.where(hit, new_vals[step_idx][:, None], v_out)
        return jnp.stack(outputs), k_out, v_out

    return jax.shard_map(shard_body, mesh=mesh, in_specs=in_specs, out_specs=out_specs, check_vma=False)
```

profile of v0, /device:TPU:0, one launch (start us, length us, event | category | flops | bytes accessed | tf_op | source)
XLA Modules:
  0.0 1102.9 jit_solution(16573914101978064474)
XLA Ops:
  10.3 6.3 copy.561
  16.7 4.7 multiply_reduce_fusion.4
  24.7 21.2 %copy.560 = bf16[2048,4096]{1,0:T(8,128)(2,1)} copy(bf16[2048,4096]{0,1:T(8,128)(2,1)} %bitcast.317) | data formatting | bytes 33554432 | tf_op jit(solution)/shard_map/dot_general | solution.py:54
  45.9 10.8 multiply_reduce_fusion
  57.9 5.2 multiply_reduce_fusion.1
  63.1 4.2 multiply_reduce_fusion.6
  67.3 5.2 multiply_reduce_fusion.2
  72.6 4.2 multiply_reduce_fusion.7
  76.8 6.6 multiply_reduce_fusion.3
  126.3 19.9 %fusion.10 = f32[128,4,4,256]{3,2,1,0:T(4,128)} fusion(bf16[128,256,4,128]{3,2,1,0:T(4,128)(2,1)} %param.17, bf16[128,4,4,64]{3,2,1,0:T(4,128)(2,1)S(1)} %copy.483, bf16[128,4,4,64]{3,2,1,0:T(4,128)(2,1)S(1)} %copy.482), kind=kOutput, calls=%fused_computation.12 | convolution fusion | flops 135266304 | bytes 36175872 | tf_op jit(solution)/shard_map/bkgh,bskh->bkgs/dot_general | solution.py:65
  146.2 18.8 %fusion.8 = f32[128,4,4,256]{3,2,1,0:T(4,128)S(1)} fusion(bf16[128,256,4,128]{3,2,1,0:T(4,128)(2,1)} %param.17, bf16[128,4,4,64]{3,2,1,0:T(4,128)(2,1)S(1)} %copy.507, bf16[128,4,4,64]{3,2,1,0:T(4,128)(2,1)S(1)} %copy.506), kind=kOutput, calls=%fused_computation.10 | convolution fusion | flops 135266304 | bytes 36175872 | tf_op jit(solution)/shard_map/bkgh,bskh->bkgs/dot_general | solution.py:65
  173.6 20.0 %fusion.12 = f32[128,4,4,256]{3,2,1,0:T(4,128)} fusion(bf16[128,256,4,128]{3,2,1,0:T(4,128)(2,1)} %param.17, bf16[128,4,4,64]{3,2,1,0:T(4,128)(2,1)S(1)} %copy-done.18, bf16[128,4,4,64]{3,2,1,0:T(4,128)(2,1)S(1)} %copy-done.19), kind=kOutput, calls=%fused_computation.14 | convolution fusion | flops 135266304 | bytes 36175872 | tf_op jit(solution)/shard_map/bkgh,bskh->bkgs/dot_general | solution.py:65
  196.7 19.5 %fusion.100 = (f32[128,4,4]{2,1,0:T(4,128)}, f32[128,4,4]{2,1,0:T(4,128)S(1)}, f32[128,4,4]{2,1,0:T(4,128)}, f32[128,4,4]{2,1,0:T(4,128)}, f32[128,4,4,256]{3,2,1,0:T(4,128)}) fusion(pred[128,256]{1,0:T(8,128)(4,1)S(1)} %copy-done.73, f32[128,4,4,256]{3,2,1,0:T(4,128)} %fusion.12, f32[128,4,4,256]{3,2,1,0:T(4,128)} %fusion.10, ...), kind=kOutput, calls=%fused_computation.143 | convolution fusion | flops 140500992 | bytes 42532864 | tf_op jit(solution)/shard_map/bkgh,bskh->bkgs/dot_general | solution.py:65
  220.6 9.8 fusion.136
  231.3 4.2 copy.456
  235.5 5.0 copy.455
  240.5 16.8 %fusion.108 = f32[128,4,4,128]{3,2,1,0:T(4,128)} fusion(bf16[128,256,4,128]{3,2,1,0:T(4,128)(2,1)} %param.18, f32[128,4,4,256]{3,2,1,0:T(4,128)} %get-tuple-element.114, f32[128,4,4]{2,1,0:T(4,128)} %copy-done.17, pred[128,256]{1,0:T(8,128)(4,1)S(1)} %copy-done.73, f32[128,4,128]{2,1,0:T(4,128)} %convert.87, f32[128,4,4]{2,1,0:T(4,128)} %get-tuple-element.31), kind=kOutput, calls=%fused_computation.154 | convolution fusion | flops 137363456 | bytes 37011456 | tf_op jit(solution)/shard_map/bkgs,bskh->bkgh/dot_general | solution.py:73
  261.0 4.0 copy.457
  272.8 4.2 copy.475
  277.0 5.0 copy.474
  282.0 16.8 %fusion.4 = f32[128,4,4,128]{3,2,1,0:T(4,128)} fusion(bf16[128,256,4,128]{3,2,1,0:T(4,128)(2,1)} %param.18, f32[128,4,4,256]{3,2,1,0:T(4,128)} %fusion.12, f32[128,4,4]{2,1,0:T(4,128)} %copy-done.14, pred[128,256]{1,0:T(8,128)(4,1)} %get-tuple-element.67), kind=kOutput, calls=%fused_computation.6 | convolution fusion | flops 136839168 | bytes 36741120 | tf_op jit(solution)/shard_map/bkgs,bskh->bkgh/dot_general | solution.py:73
  304.3 4.0 copy.476
  314.9 4.2 copy.499
  319.0 5.0 copy.498
  324.1 17.0 %fusion.2 = f32[128,4,4,128]{3,2,1,0:T(4,128)} fusion(bf16[128,256,4,128]{3,2,1,0:T(4,128)(2,1)} %param.18, f32[128,4,4,256]{3,2,1,0:T(4,128)} %fusion.10, f32[128,4,4]{2,1,0:T(4,128)} %copy-done.9, pred[128,256]{1,0:T(8,128)(4,1)} %get-tuple-element.67), kind=kOutput, calls=%fused_computation.4 | convolution fusion | flops 136839168 | bytes 36741120 | tf_op jit(solution)/shard_map/bkgs,bskh->bkgh/dot_general | solution.py:73
  356.6 4.2 copy.524
  360.7 4.1 copy.523
  364.8 16.0 %fusion = f32[128,4,4,128]{3,2,1,0:T(4,128)} fusion(bf16[128,256,4,128]{3,2,1,0:T(4,128)(2,1)} %param.18, f32[128,4,4,256]{3,2,1,0:T(4,128)S(1)} %fusion.8, f32[128,4,4]{2,1,0:T(4,128)S(1)} %max.55, pred[128,256]{1,0:T(8,128)(4,1)} %get-tuple-element.67), kind=kOutput, calls=%fused_computation.2 | convolution fusion | flops 136839168 | bytes 36741120 | tf_op jit(solution)/shard_map/bkgs,bskh->bkgh/dot_general | solution.py:73
  387.3 5.9 reshape.896
  393.1 5.9 reshape.897
  399.0 5.9 reshape.898
  412.0 10.6 all-gather.15.cloned.1.call-done
  422.6 6.1 reshape.899
  431.1 5.2 fusion.23
  436.4 5.1 fusion.22
  447.9 9.6 fusion.251
  475.0 186.3 %all-reduce.7.cloned.1.call-done = (f32[128,4096]{1,0:T(8,128)}, f32[128,4096]{1,0:T(8,128)}, f32[128,4096]{1,0:T(8,128)}, f32[128,4096]{1,0:T(8,128)}) async-done(((f32[128,4096]{1,0:T(8,128)}, f32[128,4096]{1,0:T(8,128)}, f32[128,4096]{1,0:T(8,128)}, f32[128,4096]{1,0:T(8,128)}), (f32[128,4096]{1,0:T(8,128)}, f32[128,4096]{1,0:T(8,128)}, f32[128,4096]{1,0:T(8,128)}, ...) | async-done | bytes 8388624 | tf_op jit(solution)/shard_map/psum | solution.py:83
  661.3 6.3 fusion.84
  668.3 20.5 %fusion.158 = f32[128,6144]{1,0:T(8,128)} fusion(bf16[4096,6144]{1,0:T(8,128)(2,1)} %param.23, bf16[128,4096]{1,0:T(8,128)(2,1)S(1)} %get-tuple-element.38, f32[128]{0:T(128)S(1)} %add_rsqrt_fusion.8, f32[4096]{0:T(1024)S(1)} %convert_element_type.307), kind=kOutput, calls=%fused_computation.232 | convolution fusion | flops 6444548096 | bytes 54542848 | tf_op jit(solution)/shard_map/dot_general | solution.py:86
  688.8 20.5 %fusion.162 = f32[128,6144]{1,0:T(8,128)} fusion(bf16[4096,6144]{1,0:T(8,128)(2,1)} %param.23, bf16[128,4096]{1,0:T(8,128)(2,1)S(1)} %get-tuple-element.36, f32[128]{0:T(128)S(1)} %add_rsqrt_fusion.10, f32[4096]{0:T(1024)S(1)} %convert_element_type.307), kind=kOutput, calls=%fused_computation.233 | convolution fusion | flops 6444548096 | bytes 54542848 | tf_op jit(solution)/shard_map/dot_general | solution.py:86
  709.3 35.9 %fusion.24 = f32[128,4096]{1,0:T(8,128)} fusion(bf16[6144,4096]{1,0:T(8,128)(2,1)} %param.25, bf16[4096,6144]{1,0:T(8,128)(2,1)} %param.24, f32[128,6144]{1,0:T(8,128)} %fusion.158, bf16[128,4096]{1,0:T(8,128)(2,1)S(1)} %get-tuple-element.38, f32[128]{0:T(128)S(1)} %add_rsqrt_fusion.8, f32[4096]{0:T(1024)S(1)} %convert_element_type.307), kind=kOutput, calls=%fused_computation.35 | convolution fusion | flops 12891717632 | bytes 106971648 | tf_op jit(solution)/shard_map/dot_general | solution.py:89
  745.2 36.2 %fusion.25 = f32[128,4096]{1,0:T(8,128)} fusion(bf16[6144,4096]{1,0:T(8,128)(2,1)} %param.25, bf16[4096,6144]{1,0:T(8,128)(2,1)} %param.24, f32[128,6144]{1,0:T(8,128)} %fusion.162, bf16[128,4096]{1,0:T(8,128)(2,1)S(1)} %get-tuple-element.36, f32[128]{0:T(128)S(1)} %add_rsqrt_fusion.10, f32[4096]{0:T(1024)S(1)} %convert_element_type.307), kind=kOutput, calls=%fused_computation.36 | convolution fusion | flops 12891717632 | bytes 106971648 | tf_op jit(solution)/shard_map/dot_general | solution.py:89
  781.4 20.5 %fusion.166 = f32[128,6144]{1,0:T(8,128)} fusion(bf16[4096,6144]{1,0:T(8,128)(2,1)} %param.23, bf16[128,4096]{1,0:T(8,128)(2,1)S(1)} %get-tuple-element.34, f32[128]{0:T(128)S(1)} %add_rsqrt_fusion.12, f32[4096]{0:T(1024)S(1)} %convert_element_type.307), kind=kOutput, calls=%fused_computation.234 | convolution fusion | flops 6444548096 | bytes 54542848 | tf_op jit(solution)/shard_map/dot_general | solution.py:86
  801.9 36.0 %fusion.26 = f32[128,4096]{1,0:T(8,128)} fusion(bf16[6144,4096]{1,0:T(8,128)(2,1)} %param.25, bf16[4096,6144]{1,0:T(8,128)(2,1)} %param.24, f32[128,6144]{1,0:T(8,128)} %fusion.166, bf16[128,4096]{1,0:T(8,128)(2,1)S(1)} %get-tuple-element.34, f32[128]{0:T(128)S(1)} %add_rsqrt_fusion.12, f32[4096]{0:T(1024)S(1)} %convert_element_type.307), kind=kOutput, calls=%fused_computation.37 | convolution fusion | flops 12891717632 | bytes 106971648 | tf_op jit(solution)/shard_map/dot_general | solution.py:89
  837.9 20.8 %fusion.170 = f32[128,6144]{1,0:T(8,128)} fusion(bf16[4096,6144]{1,0:T(8,128)(2,1)} %param.23, bf16[128,4096]{1,0:T(8,128)(2,1)S(1)} %copy-done.4, f32[4096]{0:T(1024)S(1)} %convert_element_type.307, f32[128]{0:T(128)S(1)} %copy-done.89), kind=kOutput, calls=%fused_computation.235 | convolution fusion | flops 6444548096 | bytes 54542848 | tf_op jit(solution)/shard_map/dot_general | solution.py:86
  858.7 35.8 %fusion.27 = f32[128,4096]{1,0:T(8,128)} fusion(bf16[6144,4096]{1,0:T(8,128)(2,1)} %param.25, bf16[4096,6144]{1,0:T(8,128)(2,1)} %param.24, f32[128,6144]{1,0:T(8,128)} %fusion.170, bf16[128,4096]{1,0:T(8,128)(2,1)S(1)} %copy-done.4, f32[4096]{0:T(1024)S(1)} %convert_element_type.307, f32[128]{0:T(128)S(1)} %copy-done.89), kind=kOutput, calls=%fused_computation.38 | convolution fusion | flops 12891717632 | bytes 106971648 | tf_op jit(solution)/shard_map/dot_general | solution.py:89
  895.6 161.6 %select_select_fusion = (bf16[128,256,4,128]{3,2,1,0:T(4,128)(2,1)}, bf16[128,256,4,128]{3,2,1,0:T(4,128)(2,1)}) fusion(bf16[128,256,4,128]{3,2,1,0:T(4,128)(2,1)} %param.18, pred[128,256]{1,0:T(8,128)(4,1)} %get-tuple-element.64, pred[128,256]{1,0:T(8,128)(4,1)} %get-tuple-element.65, pred[128,256]{1,0:T(8,128)(4,1)} %get-tuple-element.66, ...), kind=kLoop, calls=%fused_computation | loop fusion | flops 134217728 | bytes 135397376 | tf_op jit(solution)/shard_map/jit(_where)/select_n | solution.py:97
  1057.2 30.1 %all-reduce.5.cloned.1.call-done = (f32[128,4096]{1,0:T(8,128)}, f32[128,4096]{1,0:T(8,128)}, f32[128,4096]{1,0:T(8,128)}, f32[128,4096]{1,0:T(8,128)}) async-done(((f32[128,4096]{1,0:T(8,128)}, f32[128,4096]{1,0:T(8,128)}, f32[128,4096]{1,0:T(8,128)}, f32[128,4096]{1,0:T(8,128)}), (f32[128,4096]{1,0:T(8,128)}, f32[128,4096]{1,0:T(8,128)}, f32[128,4096]{1,0:T(8,128)}, ...) | async-done | bytes 8388624 | tf_op jit(solution)/shard_map/psum | solution.py:89
  (371 shorter events, 155.7 us)
Async XLA Ops:
  7.2 380.1 %all-gather.9.cloned.1.call-start = ((), (), s32[]{:S(2)}) async-start(), calls=%async_computation | async-start | bytes 5324800 | tf_op jit(solution)/shard_map/all_gather | solution.py:76
  16.7 29.2 %copy-start.90 = (f32[128]{0:T(128)}, f32[128]{0:T(128)S(1)}, u32[]{:S(2)}) copy-start(f32[128]{0:T(128)S(1)} %get-tuple-element.117) | copy-start | bytes 1540
  16.7 40.0 %copy-start.92 = (f32[128]{0:T(128)}, f32[128]{0:T(128)S(1)}, u32[]{:S(2)}) copy-start(f32[128]{0:T(128)S(1)} %get-tuple-element.118) | copy-start | bytes 1540
  45.9 10.8 copy-start
  45.9 12.0 %copy-start.1 = (bf16[4,128,4096]{2,1,0:T(8,128)(2,1)S(1)}, bf16[4,128,4096]{2,1,0:T(8,128)(2,1)}, u32[]{:S(2)}) copy-start(bf16[4,128,4096]{2,1,0:T(8,128)(2,1)} %param.15) | copy-start | bytes 12582916
  76.8 6.6 copy-start.97
  76.8 7.1 copy-start.98
  76.8 7.1 copy-start.86
  89.2 5.7 copy-start.28
  95.0 7.8 copy-start.24
  95.0 7.8 copy-start.26
  99.4 7.7 copy-start.76
  99.4 7.7 copy-start.77
  99.5 7.8 copy-start.79
  99.5 7.8 copy-start.78
  99.5 7.8 copy-start.96
  125.4 20.8 %copy-start.71 = (f32[128,4,4,3]{0,2,3,1:T(4,128)}, f32[128,4,4,3]{0,2,3,1:T(4,128)S(1)}, u32[]{:S(2)}) copy-start(f32[128,4,4,3]{0,2,3,1:T(4,128)S(1)} %copy.487) | copy-start | bytes 73732
  146.2 18.8 %copy-start.20 = (bf16[128,4,4,128]{3,1,2,0:T(4,128)(2,1)S(1)}, bf16[128,4,4,128]{3,1,2,0:T(4,128)(2,1)}, u32[]{:S(2)}) copy-start(bf16[128,4,4,128]{3,1,2,0:T(4,128)(2,1)} %copy.510) | copy-start | bytes 1572868
  166.9 5.3 copy-start.69
  168.5 25.0 %copy-start.66 = (f32[128,4,4,4]{0,3,2,1:T(4,128)}, f32[128,4,4,4]{0,3,2,1:T(4,128)S(1)}, u32[]{:S(2)}) copy-start(f32[128,4,4,4]{0,3,2,1:T(4,128)S(1)} %copy.511) | copy-start | bytes 98308
  173.6 20.0 %copy-start.70 = (bf16[128,2,4,128]{3,1,2,0:T(2,128)(2,1)S(1)}, bf16[128,2,4,128]{3,1,2,0:T(2,128)(2,1)}, u32[]{:S(2)}) copy-start(bf16[128,2,4,128]{3,1,2,0:T(2,128)(2,1)} %copy.468) | copy-start | bytes 786436
  173.6 20.0 %copy-start.74 = (pred[128,2]{1,0:T(8,128)(4,1)S(1)}, pred[128,2]{1,0:T(8,128)(4,1)}, u32[]{:S(2)}) copy-start(pred[128,2]{1,0:T(8,128)(4,1)} %copy.466) | copy-start | bytes 772
  196.7 19.5 %copy-start.34 = (f32[128,4,4]{2,1,0:T(4,128)S(1)}, f32[128,4,4]{2,1,0:T(4,128)}, u32[]{:S(2)}) copy-start(f32[128,4,4]{2,1,0:T(4,128)} %copy.567) | copy-start | bytes 24580
  196.7 20.7 %copy-start.33 = (f32[128,4,4]{2,1,0:T(4,128)S(1)}, f32[128,4,4]{2,1,0:T(4,128)}, u32[]{:S(2)}) copy-start(f32[128,4,4]{2,1,0:T(4,128)} %copy.564) | copy-start | bytes 24580
  196.7 21.7 %copy-start.68 = (f32[128,4,4]{2,1,0:T(4,128)S(1)}, f32[128,4,4]{2,1,0:T(4,128)}, u32[]{:S(2)}) copy-start(f32[128,4,4]{2,1,0:T(4,128)} %get-tuple-element.115) | copy-start | bytes 24580
  218.4 11.9 %copy-start.9 = (f32[128,4,4]{2,1,0:T(4,128)}, f32[128,4,4]{2,1,0:T(4,128)S(1)}, u32[]{:S(2)}) copy-start(f32[128,4,4]{2,1,0:T(4,128)S(1)} %max.53) | copy-start | bytes 24580
  218.5 11.8 %copy-start.14 = (f32[128,4,4]{2,1,0:T(4,128)}, f32[128,4,4]{2,1,0:T(4,128)S(1)}, u32[]{:S(2)}) copy-start(f32[128,4,4]{2,1,0:T(4,128)S(1)} %max.51) | copy-start | bytes 24580
  220.6 9.8 copy-start.17
  265.0 128.1 %all-gather.11.cloned.1.call-start = ((), (), s32[]{:S(2)}) async-start(), calls=%async_computation.1 | async-start | bytes 5324800 | tf_op jit(solution)/shard_map/all_gather | solution.py:76
  265.8 6.2 copy-start.32
  308.3 90.6 %all-gather.13.cloned.1.call-start = ((), (), s32[]{:S(2)}) async-start(), calls=%async_computation.2 | async-start | bytes 5324800 | tf_op jit(solution)/shard_map/all_gather | solution.py:76
  308.5 5.6 copy-start.31
  350.0 72.6 %all-gather.15.cloned.1.call-start = ((), (), s32[]{:S(2)}) async-start(), calls=%async_computation.3 | async-start | bytes 5324800 | tf_op jit(solution)/shard_map/all_gather | solution.py:76
  350.2 5.6 copy-start.30
  387.2 274.1 %all-reduce.7.cloned.1.call-start = ((), (), s32[]{:S(2)}) async-start(), calls=%async_computation.5 | async-start | bytes 16777216 | tf_op jit(solution)/shard_map/psum | solution.py:83
  422.6 18.8 %slice-start.4 = ((s8[4259840]{0:T(1024)(128)(4,1)}), s8[65536]{0:T(1024)(128)(4,1)S(1)}, s32[]{:S(2)}) async-start(s8[4259840]{0:T(1024)(128)(4,1)} %bitcast.313), calls=%async_computation.10 | async-start | bytes 131072
  431.1 10.3 slice-start.5
  431.1 13.2 %slice-start.6 = ((s8[4259840]{0:T(1024)(128)(4,1)}), s8[4194304]{0:T(1024)(128)(4,1)S(1)}, s32[]{:S(2)}) async-start(s8[4259840]{0:T(1024)(128)(4,1)} %bitcast.315), calls=%async_computation.12 | async-start | bytes 8388608
  436.3 8.0 slice-start.7
  444.3 13.2 %slice-start = ((s8[16777216]{0:T(1024)(128)(4,1)}), s8[4194304]{0:T(1024)(128)(4,1)S(1)}, s32[]{:S(2)}) async-start(s8[16777216]{0:T(1024)(128)(4,1)} %bitcast.311), calls=%async_computation.6 | async-start | bytes 8388608
  447.7 9.8 slice-start.1
  447.8 9.7 slice-start.2
  447.8 9.6 slice-start.3
  469.0 5.3 copy-start.47
  469.0 618.3 %all-reduce.5.cloned.1.call-start = ((), (), s32[]{:S(2)}) async-start(), calls=%async_computation.4 | async-start | bytes 16777216 | tf_op jit(solution)/shard_map/psum | solution.py:89
  667.7 41.6 %copy-start.2 = (bf16[128,4096]{1,0:T(8,128)(2,1)}, bf16[128,4096]{1,0:T(8,128)(2,1)S(1)}, u32[]{:S(2)}) copy-start(bf16[128,4096]{1,0:T(8,128)(2,1)S(1)} %get-tuple-element.38) | copy-start | bytes 3145732
  801.9 36.0 %copy-start.4 = (bf16[128,4096]{1,0:T(8,128)(2,1)S(1)}, bf16[128,4096]{1,0:T(8,128)(2,1)}, u32[]{:S(2)}) copy-start(bf16[128,4096]{1,0:T(8,128)(2,1)} %get-tuple-element.24) | copy-start | bytes 3145732
  801.9 36.0 %copy-start.89 = (f32[128]{0:T(128)S(1)}, f32[128]{0:T(128)}, u32[]{:S(2)}) copy-start(f32[128]{0:T(128)} %add_rsqrt_fusion.14) | copy-start | bytes 1540
  (65 other events, 196.1 us)
Sparse Core Ops, SparseCore 0:
  265.1 35.2 all-gather.8
  308.5 35.2 all-gather.10
  350.1 35.2 all-gather.12
  387.4 35.1 all-gather.14
  469.1 192.2 all-reduce.6
  894.7 192.5 all-reduce.4
where the time goes:
time: 1110 us; the launch traced here: 1100 us
  matrix products  467 us (42%)
  other arithmetic  251 us (23%)
  waiting for transfers between devices  227 us (20%)
  local copies, waits for them, and re-layouts  142 us (13%)
  between operations  15.7 us (1%)
    psum x1, waiting for transfers between devices, shard_body(): lax.psum(jnp.dot(attn_in, w_o, preferred_element_type=jnp.float32), 'tp')  186 us
    select_n x1, other arithmetic, shard_body(): v_out = jnp.where(hit, new_vals[step_idx][:, None], v_out)  162 us
    dot_general x4, matrix products, shard_body(): jnp.dot(mlp_act, w_down, preferred_element_type=jnp.float32)  144 us
    dot_general x4, matrix products, shard_body(): gate_act = jnp.dot(mlp_in, w_gate, preferred_element_type=jnp.float32)  82.3 us
    dot_general x4, matrix products, shard_body(): jnp.einsum('bkgh,bskh->bkgs', q_rot, k_cache, preferred_element_type=jnp....  78.2 us
    dot_general x4, matrix products, shard_body(): jnp.einsum('bkgs,bskh->bkgh', old_probs.astype(jnp.bfloat16), v_cache, pr...  66.6 us
    psum x1, waiting for transfers between devices, shard_body(): lax.psum(jnp.dot(mlp_act, w_down, preferred_element_type=jnp.float32), 'tp')  30.1 us
    dot_general x4, matrix products, shard_body(): jnp.dot(normed, w_q, preferred_element_type=jnp.float32)  27.9 us
  transfers between devices with their start and end apart: 6, of which 3 were waited for; matrix products, arithmetic and copies ran while one was open for 28% of the time, Pallas kernels for 0%

commit v1 on v0

v1 whole, which is shorter than its diff:
```python
import functools
import math

import jax
import jax.numpy as jnp
from jax import lax
from jax.experimental import pallas as pl
from jax.experimental.pallas import tpu as pltpu
from jax.sharding import PartitionSpec as P

ROPE_BASE = 1000000.0
NORM_EPS = 1e-06
MASKED = -3e38
FLOOR = -1e38


def rms_scale(values, gain_vec):
    wide_vals = values.astype(jnp.float32)
    inv_rms = lax.rsqrt(jnp.mean(wide_vals * wide_vals, axis=-1, keepdims=True) + NORM_EPS)
    return wide_vals * inv_rms * gain_vec.astype(jnp.float32)


def apply_rope(vector, tok_pos):
    head_dim = vector.shape[-1]
    half_dim = head_dim // 2
    freqs = ROPE_BASE ** (-(jnp.arange(half_dim, dtype=jnp.float32) * (2.0 / head_dim)))
    angles = tok_pos.astype(jnp.float32)[..., None] * freqs
    cos_tab = jnp.cos(angles)[..., None, :]
    sin_tab = jnp.sin(angles)[..., None, :]
    lower_half = vector[..., :half_dim]
    upper_half = vector[..., half_dim:]
    return jnp.concatenate([lower_half * cos_tab - upper_half * sin_tab, upper_half * cos_tab + lower_half * sin_tab], axis=-1)


def attn_kernel(dims, order_ref, rel_ref, q_ref, kn_ref, vn_ref, k_ref, v_ref, ko_ref, vo_ref, o_ref, ml_ref):
    n_req, n_steps, heads, kv_heads, groups, rows_c, hd, exp_scale = dims
    rows_q = n_steps * heads
    new_rows = n_steps * kv_heads
    blk = order_ref[pl.program_id(0)]

    col = lax.broadcasted_iota(jnp.int32, (rows_q, rows_c), 1)
    row = lax.broadcasted_iota(jnp.int32, (rows_q, rows_c), 0)
    same_head = (col % kv_heads) == ((row % heads) // groups)
    lag = jnp.where(same_head, col // kv_heads - row // heads, jnp.int32(1 << 30))
    win_row = lax.broadcasted_iota(jnp.int32, (2 * new_rows, hd), 0)
    ml_lane = lax.broadcasted_iota(jnp.int32, (rows_q, 2 * rows_q), 1)
    ml_row = lax.broadcasted_iota(jnp.int32, (rows_q, 2 * rows_q), 0)
    pad = jnp.zeros((new_rows, hd), jnp.float32)

    for j in range(n_req):
        rel = rel_ref[blk * n_req + j]
        first = rel * kv_heads
        base = pl.multiple_of(jnp.clip((first >> 4) << 4, 0, rows_c - 2 * new_rows), 16)
        off = first - base
        inside = (win_row >= off) & (win_row < off + new_rows)
        for src, new, dst in ((k_ref, kn_ref, ko_ref), (v_ref, vn_ref, vo_ref)):
            dst[j] = src[j]
            rolled = pltpu.roll(jnp.concatenate([new[j].astype(jnp.float32), pad], axis=0), off & (2 * new_rows - 1), 0)
            window = src[j, pl.ds(base, 2 * new_rows), :].astype(jnp.float32)
            dst[j, pl.ds(base, 2 * new_rows), :] = jnp.where(inside, rolled, window).astype(dst.dtype)
        query = q_ref[:, j].reshape(rows_q, hd)
        scores = lax.dot_general(query, ko_ref[j], (((1,), (1,)), ((), ())), preferred_element_type=jnp.float32)
        scores = jnp.where(lag <= rel, scores, MASKED)
        top = jnp.maximum(jnp.max(scores, axis=1, keepdims=True), FLOOR)
        probs = jnp.exp2((scores - top) * exp_scale)
        total = jnp.sum(probs, axis=1, keepdims=True)
        o_ref[j] = lax.dot_general(probs.astype(jnp.bfloat16), vo_ref[j], (((1,), (0,)), ((), ())), preferred_element_type=jnp.float32)
        packed = jnp.where(ml_lane == ml_row, top, jnp.where(ml_lane == ml_row + rows_q, total, 0.0))
        ml_ref[j] = jnp.sum(packed, axis=0, keepdims=True)


def attention(order, rel, q, k_new, v_new, k_cache, v_cache, kv_heads, exp_scale, n_req=4):
    n_steps, n_batch, heads, hd = q.shape
    rows_c = k_cache.shape[1]
    new_rows = n_steps * kv_heads
    rows_q = n_steps * heads
    dims = (n_req, n_steps, heads, kv_heads, heads // kv_heads, rows_c, hd, exp_scale)
    cache_blk = pl.BlockSpec((n_req, rows_c, hd), lambda i, order, rel: (order[i], 0, 0))
    new_blk = pl.BlockSpec((n_req, new_rows, hd), lambda i, order, rel: (order[i], 0, 0))
    cache_shape = jax.ShapeDtypeStruct(k_cache.shape, k_cache.dtype)
    return pl.pallas_call(
        functools.partial(attn_kernel, dims),
        grid_spec=pltpu.PrefetchScalarGridSpec(
            num_scalar_prefetch=2,
            grid=(n_batch // n_req,),
            in_specs=[pl.BlockSpec((n_steps, n_req, heads, hd), lambda i, order, rel: (0, order[i], 0, 0)),
                      new_blk, new_blk, cache_blk, cache_blk],
            out_specs=[cache_blk, cache_blk,
                       pl.BlockSpec((n_req, rows_q, hd), lambda i, order, rel: (i, 0, 0)),
                       pl.BlockSpec((n_req, 1, 2 * rows_q), lambda i, order, rel: (i, 0, 0))],
        ),
        out_shape=[cache_shape, cache_shape,
                   jax.ShapeDtypeStruct((n_batch, rows_q, hd), jnp.float32),
                   jax.ShapeDtypeStruct((n_batch, 1, 2 * rows_q), jnp.float32)],
        compiler_params=pltpu.CompilerParams(dimension_semantics=("arbitrary",), vmem_limit_bytes=40 * 2**20),
        cost_estimate=pl.CostEstimate(flops=4 * n_batch * rows_q * rows_c * hd, bytes_accessed=8 * n_batch * rows_c * hd,
                                      transcendentals=n_batch * rows_q * rows_c),
        name="decode_attention",
    )(order, rel, q, k_new, v_new, k_cache, v_cache)


def assemble_kernel(own, cw, sp_ref, *refs):
    out_ref = refs[-1]
    sp = sp_ref[0]
    for c in range(len(refs) // 4):
        for flip in range(4):
            start = pl.multiple_of((sp ^ flip) * own, own)
            out_ref[0, pl.ds(start, own), c * cw:(c + 1) * cw] = refs[c * 4 + flip][0].astype(out_ref.dtype)


def assemble(sp, pieces):
    n_steps, own, cw = pieces[0][0].shape
    n_chunks = len(pieces)
    piece_blk = pl.BlockSpec((1, own, cw), lambda i, sp: (i, 0, 0))
    return pl.pallas_call(
        functools.partial(assemble_kernel, own, cw),
        grid_spec=pltpu.PrefetchScalarGridSpec(
            num_scalar_prefetch=1,
            grid=(n_steps,),
            in_specs=[piece_blk] * (4 * n_chunks),
            out_specs=pl.BlockSpec((1, 4 * own, cw * n_chunks), lambda i, sp: (i, 0, 0)),
        ),
        out_shape=jax.ShapeDtypeStruct((n_steps, 4 * own, cw * n_chunks), jnp.bfloat16),
        compiler_params=pltpu.CompilerParams(dimension_semantics=("arbitrary",)),
        name="assemble_hidden",
    )(sp.reshape(1), *[piece for chunk in pieces for piece in chunk])


def merge(mine, other, exp_scale):
    out_a, max_a, sum_a = mine
    out_b, max_b, sum_b = other
    top = jnp.maximum(max_a, max_b)
    wt_a = jnp.exp2((max_a - top) * exp_scale)
    wt_b = jnp.exp2((max_b - top) * exp_scale)
    return wt_a[..., None] * out_a + wt_b[..., None] * out_b, top, wt_a * sum_a + wt_b * sum_b


def solution(mesh):
    cache_spec = P('dp', 'sp', 'tp', None)
    col_spec = P(None, 'tp')
    row_spec = P('tp', None)
    in_specs = (P(None, 'dp', None), P('dp'), cache_spec, cache_spec, col_spec, col_spec, col_spec, row_spec,
                col_spec, col_spec, row_spec, P(), P(), P(), P())
    out_specs = (P(None, 'dp', None), cache_spec, cache_spec)
    core_perm = [(0, 1), (1, 0), (2, 3), (3, 2)]
    chip_perm = [(0, 2), (2, 0), (1, 3), (3, 1)]
    tp_perm = [(0, 1), (1, 0)]

    def shard_body(hidden, start_pos, k_cache, v_cache, w_q, w_k, w_v, w_o, w_gate, w_up, w_down, attn_norm, mlp_norm, q_gain, k_gain):
        n_steps, n_batch, width = hidden.shape
        seq_blk, kv_heads, hd = k_cache.shape[1], k_cache.shape[2], k_cache.shape[3]
        heads = w_q.shape[1] // hd
        rows_q = n_steps * heads
        exp_scale = hd ** -0.5 * math.log2(math.e)
        sp = lax.axis_index('sp')
        core, chip = sp % 2, sp // 2
        own = n_batch // 4

        tok_pos = start_pos[None, :] + jnp.arange(n_steps, dtype=jnp.int32)[:, None]
        normed = rms_scale(hidden, attn_norm).astype(jnp.bfloat16).reshape(n_steps * n_batch, width)
        q_raw = jnp.dot(normed, w_q, preferred_element_type=jnp.float32).reshape(n_steps, n_batch, heads, hd)
        k_raw = jnp.dot(normed, w_k, preferred_element_type=jnp.float32).reshape(n_steps, n_batch, kv_heads, hd)
        v_new = jnp.dot(normed, w_v, preferred_element_type=jnp.float32).astype(jnp.bfloat16).reshape(n_steps, n_batch, kv_heads, hd)
        q_rot = apply_rope(rms_scale(q_raw, q_gain), tok_pos).astype(jnp.bfloat16)
        k_new = apply_rope(rms_scale(k_raw, k_gain), tok_pos).astype(jnp.bfloat16)
        k_rows = k_new.transpose(1, 0, 2, 3).reshape(n_batch, n_steps * kv_heads, hd)
        v_rows = v_new.transpose(1, 0, 2, 3).reshape(n_batch, n_steps * kv_heads, hd)

        n_req = 4
        per = own // n_req
        part = jnp.stack([(1 - chip) * 2 + (1 - core), chip * 2 + (1 - core), (1 - chip) * 2 + core, chip * 2 + core])
        order = (part[:, None] * per + jnp.arange(per)[None, :]).reshape(-1).astype(jnp.int32)
        rel = start_pos - sp * seq_blk
        flat = (n_batch, seq_blk * kv_heads, hd)
        k_out, v_out, o_part, ml = attention(order, rel, q_rot, k_rows, v_rows, k_cache.reshape(flat), v_cache.reshape(flat),
                                             kv_heads, exp_scale, n_req)

        half = n_batch // 2
        ml = ml.reshape(n_batch, 2 * rows_q)
        o_recv = lax.ppermute(o_part[:half], 'sp', core_perm)
        ml_recv = lax.ppermute(ml[:half], 'sp', core_perm)
        both = merge((o_part[half:], ml[half:, :rows_q], ml[half:, rows_q:]),
                     (o_recv, ml_recv[:, :rows_q], ml_recv[:, rows_q:]), exp_scale)
        far = [lax.ppermute(part_[:own], 'sp', chip_perm) for part_ in both]
        o_sum, _, l_sum = merge([part_[own:] for part_ in both], far, exp_scale)
        attn_in = (o_sum / l_sum[..., None]).astype(jnp.bfloat16).reshape(own, n_steps, heads * hd)
        attn_in = attn_in.transpose(1, 0, 2).reshape(n_steps * own, heads * hd)

        x_own = lax.dynamic_slice_in_dim(hidden, sp * own, own, axis=1).reshape(n_steps * own, width)
        o_mine = jnp.dot(attn_in, w_o, preferred_element_type=jnp.float32)
        attn_out = o_mine + lax.ppermute(o_mine, 'tp', tp_perm)
        residual = (x_own.astype(jnp.float32) + attn_out).astype(jnp.bfloat16)
        mlp_in = rms_scale(residual, mlp_norm).astype(jnp.bfloat16)
        gate_act = jnp.dot(mlp_in, w_gate, preferred_element_type=jnp.float32)
        up_proj = jnp.dot(mlp_in, w_up, preferred_element_type=jnp.float32)
        mlp_act = (jax.nn.silu(gate_act) * up_proj).astype(jnp.bfloat16)
        n_chunks = 4
        cw = width // n_chunks
        pieces = []
        for c in range(n_chunks):
            sl = slice(c * cw, (c + 1) * cw)
            mine = jnp.dot(mlp_act, w_down[:, sl], preferred_element_type=jnp.float32)
            mine = residual[:, sl].astype(jnp.float32) + (mine + lax.ppermute(mine, 'tp', tp_perm))
            near = lax.ppermute(mine, 'sp', core_perm)
            across = lax.ppermute(mine, 'sp', chip_perm)
            diag = lax.ppermute(across, 'sp', core_perm)
            pieces.append([piece.reshape(n_steps, own, cw) for piece in (mine, near, across, diag)])
        hid_out = assemble(sp, pieces)
        return hid_out, k_out.reshape(k_cache.shape), v_out.reshape(v_cache.shape)

    return jax.shard_map(shard_body, mesh=mesh, in_specs=in_specs, out_specs=out_specs, check_vma=False)
```

time: 1110 us -> 395 us (0.36)
  matrix products: 467 us -> 92.8 us
  other arithmetic: 251 us -> 23.1 us
  local copies, waits for them, and re-layouts: 142 us -> 39.1 us
  waiting for transfers between devices: 227 us -> 154 us
  Pallas kernels: 0 us -> 64.8 us
  starting transfers between devices: 0.25 us -> 17.4 us
  between operations: 15.7 us -> 1.39 us
    dot_general x23 -> x6, matrix products: 327 us -> 50.3 us  [the longest x4 23.2 us: shard_body(): mine = jnp.dot(mlp_act, w_down[:, sl], preferred_element_type=jnp.float32)]
    psum x2 -> x0, waiting for transfers between devices: 216 us -> none  [the longest x1 186 us: shard_body(): lax.psum(jnp.dot(attn_in, w_o, preferred_element_type=jnp.float32), 'tp')]
    select_n x1 -> x0, other arithmetic: 162 us -> none  [shard_body(): v_out = jnp.where(hit, new_vals[step_idx][:, None], v_out)]
    ppermute x0 -> x22, waiting for transfers between devices: none -> 154 us  [the longest x1 44 us: shard_body(): attn_out = o_mine + lax.ppermute(o_mine, 'tp', tp_perm)]
    pallas_call x0 -> x2, Pallas kernels: none -> 64.8 us  [the longest x1 59 us: attention(): pl.pallas_call(functools.partial(attn_kernel, dims), grid_spec=pltpu.Pref...]
    dot_general x4 -> x1, matrix products: 82.3 us -> 20.5 us  [shard_body(): gate_act = jnp.dot(mlp_in, w_gate, preferred_element_type=jnp.float32)]
    reduce_sum x10 -> x0, other arithmetic: 31.1 us -> none  [the longest x4 16 us: shard_body(): (weights[..., None] * gathered[..., :head_dim]).sum(axis=0)]
    concatenate x17 -> x0, local copies, waits for them, and re-layouts: 27.5 us -> none  [the longest x4 14.2 us: shard_body(): jnp.concatenate([blk_out, blk_max[..., None], blk_sum[..., None]], axis=-1)]
  transfers between devices with their start and end apart: 6 -> 22, of which waited for: 3 -> 13; matrix products, arithmetic and copies ran while one was open for 28% -> 0% of each run, Pallas kernels for 0% -> 0%
where the time goes in v1:
time: 395 us; the launch traced here: 392 us
  waiting for transfers between devices  154 us (39%)
  matrix products  92.8 us (23%)
  Pallas kernels  64.8 us (16%)
  local copies, waits for them, and re-layouts  39.1 us (10%)
  other arithmetic  23.1 us (6%)
  starting transfers between devices  17.4 us (4%)
    pallas_call x1, Pallas kernels, attention(): pl.pallas_call(functools.partial(attn_kernel, dims), grid_spec=pltpu.Pref...  59 us
    ppermute x1, waiting for transfers between devices, shard_body(): attn_out = o_mine + lax.ppermute(o_mine, 'tp', tp_perm)  44 us
    ppermute x4, waiting for transfers between devices, shard_body(): lax.ppermute(mine, 'tp', tp_perm)  42.3 us
    ppermute x4, waiting for transfers between devices, shard_body(): across = lax.ppermute(mine, 'sp', chip_perm)  39.8 us
    dot_general x2, local copies, waits for them, and re-layouts, shard_body(): jnp.dot(normed, w_q, preferred_element_type=jnp.float32)  26.6 us
    dot_general x4, matrix products, shard_body(): mine = jnp.dot(mlp_act, w_down[:, sl], preferred_element_type=jnp.float32)  23.2 us
    ppermute x3, waiting for transfers between devices, shard_body(): far = [lax.ppermute(part_[:own], 'sp', chip_perm) for part_ in both]  22.1 us
    dot_general x1, matrix products, shard_body(): gate_act = jnp.dot(mlp_in, w_gate, preferred_element_type=jnp.float32)  20.5 us
  transfers between devices with their start and end apart: 22, of which 13 were waited for; matrix products, arithmetic and copies ran while one was open for 0% of the time, Pallas kernels for 0%

profile of v1, /device:TPU:0, one launch (start us, length us, event | category | flops | bytes accessed | tf_op | source)
XLA Modules:
  0.0 392.5 jit_solution(4262653387009649704)
XLA Ops:
  3.6 3.1 fusion.8
  6.7 1.0 multiply_cosine_fusion
  7.9 4.0 %fusion.10 = bf16[4,128,4096]{2,1,0:T(8,128)(2,1)S(1)} fusion(bf16[4,128,4096]{2,1,0:T(8,128)(2,1)} %param.15, f32[4096]{0:T(1024)S(1)} %convert_element_type.67, f32[4,128]{1,0:T(4,128)S(1)} %add_rsqrt_fusion.2), kind=kLoop, calls=%fused_computation.12 | loop fusion | flops 8388608 | bytes 8407040 | tf_op jit(solution)/shard_map/convert_element_type | solution.py:160
  11.9 2.0 copy-done
  13.9 2.3 convolution_convert_fusion
  16.6 6.5 %copy.44 = bf16[512,4096]{1,0:T(8,128)(2,1)} copy(bf16[512,4096]{0,1:T(8,128)(2,1)} %bitcast.80) | data formatting | bytes 8388608 | tf_op jit(solution)/shard_map/dot_general | solution.py:162
  23.1 5.5 %multiply_reduce_fusion.1 = (f32[4,128,4]{1,2,0:T(4,128)S(1)}, f32[4,128,4,128]{1,3,2,0:T(8,128)S(1)}) fusion(bf16[4,128,4096,1]{2,1,0,3:T(8,128)(2,1)} %bitcast.81, bf16[4,128,4096]{2,1,0:T(8,128)(2,1)} %copy-done), kind=kOutput, calls=%fused_computation.37 | convolution fusion | flops 2148005888 | bytes 9445376 | tf_op jit(solution)/shard_map/dot_general | solution.py:162
  29.4 21.2 %copy.43 = bf16[2048,4096]{1,0:T(8,128)(2,1)} copy(bf16[2048,4096]{0,1:T(8,128)(2,1)} %bitcast.77) | data formatting | bytes 33554432 | tf_op jit(solution)/shard_map/dot_general | solution.py:161
  50.6 14.3 %multiply_reduce_fusion = (f32[4,128,16]{1,2,0:T(8,128)S(1)}, f32[4,128,16,128]{1,3,2,0:T(8,128)}) fusion(bf16[16,128,4096,1]{2,1,0,3:T(8,128)(2,1)} %bitcast.78, bf16[4,128,4096]{2,1,0:T(8,128)(2,1)} %copy-done), kind=kOutput, calls=%fused_computation.22 | convolution fusion | flops 8592023552 | bytes 25198592 | tf_op jit(solution)/shard_map/dot_general | solution.py:161
  65.1 5.4 %copy.35 = f32[4,128,16,128]{3,2,1,0:T(8,128)} copy(f32[4,128,16,128]{1,3,2,0:T(8,128)} %get-tuple-element.31) | data formatting | bytes 8388608 | tf_op jit(solution)/shard_map/dot_general | solution.py:161
  70.5 3.6 multiply_multiply_fusion
  74.1 1.8 subtract_convert_fusion
  75.9 1.2 pad_maximum_fusion.q_ref
  77.1 59.0 %decode_attention.1 = (bf16[128,1024,128]{2,1,0:T(8,128)(2,1)}, bf16[128,1024,128]{2,1,0:T(8,128)(2,1)}, f32[128,64,128]{2,1,0:T(8,128)S(1)}, f32[128,1,128]{2,1,0:T(1,128)S(1)}) custom-call(s32[32]{0:T(128)S(1)} %add.159.order_ref, s32[128]{0:T(128)S(1)} %broadcast_subtract_fusion.rel_ref, bf16[4,128,16,128]{3,2,1,0:T(8,128)(2,1)S(1)} %pad_maximum_fusion.q_ref, ...), custom_call_target="tpu_custom_call" | custom-call | flops 4294967296 | bytes 134217728 | tf_op jit(solution)/shard_map/decode_attention/pallas_call | solution.py:81
  136.3 0.9 collective-permute-start.2
  137.2 3.8 collective-permute-done
  141.1 1.3 multiply_add_fusion
  142.4 2.9 collective-permute-start.3
  145.4 2.0 collective-permute-start.4
  147.3 22.0 %collective-permute-done.1 = f32[32,64]{1,0:T(8,128)S(1)} collective-permute-done((f32[32,64]{1,0:T(8,128)S(1)}, f32[32,64]{1,0:T(8,128)S(1)}, u32[]{:S(2)}, u32[]{:S(2)}) %collective-permute-start.1) | collective-permute-done | bytes 8224 | tf_op jit(solution)/shard_map/ppermute | solution.py:184
  169.5 1.2 fusion.22
  171.2 8.1 %fusion.35 = f32[128,4096]{1,0:T(8,128)S(1)} fusion(bf16[128,2048]{1,0:T(8,128)(2,1)S(1)} %bitcast.82, bf16[2048,4096]{1,0:T(8,128)(2,1)} %param.22), kind=kOutput, calls=%fused_computation.73 | convolution fusion | flops 2147483648 | bytes 19398656 | tf_op jit(solution)/shard_map/dot_general | solution.py:190
  179.3 1.8 collective-permute-start.5
  181.1 1.3 constant_dynamic-slice_fusion
  182.4 44.0 %collective-permute-done.5 = f32[128,4096]{1,0:T(8,128)} collective-permute-done((f32[128,4096]{1,0:T(8,128)S(1)}, f32[128,4096]{1,0:T(8,128)}, u32[]{:S(2)}, u32[]{:S(2)}) %collective-permute-start.5) | collective-permute-done | bytes 2097184 | tf_op jit(solution)/shard_map/ppermute | solution.py:191
  226.4 2.1 fusion.16
  228.5 20.5 %fusion.24 = f32[128,6144]{1,0:T(8,128)} fusion(bf16[4096,6144]{1,0:T(8,128)(2,1)} %param.23, bf16[128,4096]{1,0:T(8,128)(2,1)S(1)} %get-tuple-element.12, f32[4096]{0:T(1024)S(1)} %convert_element_type.77, f32[128]{0:T(128)S(1)} %add_rsqrt_fusion.3), kind=kOutput, calls=%fused_computation.48 | convolution fusion | flops 6444548096 | bytes 54542848 | tf_op jit(solution)/shard_map/dot_general | solution.py:194
  249.0 19.0 %fusion.11 = bf16[128,6144]{1,0:T(8,128)(2,1)S(1)} fusion(bf16[4096,6144]{1,0:T(8,128)(2,1)} %param.24, f32[128,6144]{1,0:T(8,128)} %fusion.24, bf16[128,4096]{1,0:T(8,128)(2,1)S(1)} %get-tuple-element.12, f32[4096]{0:T(1024)S(1)} %convert_element_type.77, f32[128]{0:T(128)S(1)} %add_rsqrt_fusion.3), kind=kOutput, calls=%fused_computation.14 | convolution fusion | flops 6449266688 | bytes 56115712 | tf_op jit(solution)/shard_map/dot_general | solution.py:195
  268.0 5.7 %fusion = f32[128,1024]{1,0:T(8,128)S(1)} fusion(bf16[128,6144]{1,0:T(8,128)(2,1)S(1)} %fusion.11, bf16[6144,4096]{1,0:T(8,128)(2,1)} %param.25), kind=kOutput, calls=%fused_computation | convolution fusion | flops 1610612736 | bytes 14680064 | tf_op jit(solution)/shard_map/dot_general | solution.py:202
  273.7 5.7 %fusion.2 = f32[128,1024]{1,0:T(8,128)S(1)} fusion(bf16[128,6144]{1,0:T(8,128)(2,1)S(1)} %fusion.11, bf16[6144,4096]{1,0:T(8,128)(2,1)} %param.25), kind=kOutput, calls=%fused_computation.2 | convolution fusion | flops 1610612736 | bytes 14680064 | tf_op jit(solution)/shard_map/dot_general | solution.py:202
  279.5 6.0 %fusion.4 = f32[128,1024]{1,0:T(8,128)S(1)} fusion(bf16[128,6144]{1,0:T(8,128)(2,1)S(1)} %fusion.11, bf16[6144,4096]{1,0:T(8,128)(2,1)} %param.25), kind=kOutput, calls=%fused_computation.4 | convolution fusion | flops 1610612736 | bytes 14680064 | tf_op jit(solution)/shard_map/dot_general | solution.py:202
  285.5 5.7 %fusion.6 = f32[128,1024]{1,0:T(8,128)S(1)} fusion(bf16[128,6144]{1,0:T(8,128)(2,1)S(1)} %fusion.11, bf16[6144,4096]{1,0:T(8,128)(2,1)} %param.25), kind=kOutput, calls=%fused_computation.6 | convolution fusion | flops 1610612736 | bytes 14680064 | tf_op jit(solution)/shard_map/dot_general | solution.py:202
  291.2 1.5 collective-permute-start.6
  293.2 1.5 collective-permute-start.14
  295.3 10.7 %collective-permute-done.6 = f32[128,1024]{1,0:T(8,128)S(1)} collective-permute-done((f32[128,1024]{1,0:T(8,128)S(1)}, f32[128,1024]{1,0:T(8,128)S(1)}, u32[]{:S(2)}, u32[]{:S(2)}) %collective-permute-start.6) | collective-permute-done | bytes 524320 | tf_op jit(solution)/shard_map/ppermute | solution.py:203
  306.0 11.2 %collective-permute-done.10 = f32[128,1024]{1,0:T(8,128)S(1)} collective-permute-done((f32[128,1024]{1,0:T(8,128)S(1)}, f32[128,1024]{1,0:T(8,128)S(1)}, u32[]{:S(2)}, u32[]{:S(2)}) %collective-permute-start.10) | collective-permute-done | bytes 524320 | tf_op jit(solution)/shard_map/ppermute | solution.py:203
  317.3 11.2 %collective-permute-done.14 = f32[128,1024]{1,0:T(8,128)S(1)} collective-permute-done((f32[128,1024]{1,0:T(8,128)S(1)}, f32[128,1024]{1,0:T(8,128)S(1)}, u32[]{:S(2)}, u32[]{:S(2)}) %collective-permute-start.14) | collective-permute-done | bytes 524320 | tf_op jit(solution)/shard_map/ppermute | solution.py:203
  328.5 9.1 %collective-permute-done.18 = f32[128,1024]{1,0:T(8,128)S(1)} collective-permute-done((f32[128,1024]{1,0:T(8,128)S(1)}, f32[128,1024]{1,0:T(8,128)S(1)}, u32[]{:S(2)}, u32[]{:S(2)}) %collective-permute-start.18) | collective-permute-done | bytes 524320 | tf_op jit(solution)/shard_map/ppermute | solution.py:203
  338.2 1.2 collective-permute-start.20
  339.4 0.8 collective-permute-start.16
  340.5 1.2 collective-permute-start.12
  341.7 11.4 %collective-permute-done.20 = f32[128,1024]{1,0:T(8,128)S(1)} collective-permute-done((f32[128,1024]{1,0:T(8,128)S(1)}, f32[128,1024]{1,0:T(8,128)S(1)}, u32[]{:S(2)}, u32[]{:S(2)}) %collective-permute-start.20) | collective-permute-done | bytes 524320 | tf_op jit(solution)/shard_map/ppermute | solution.py:205
  353.1 1.2 collective-permute-start.8
  354.3 10.0 %collective-permute-done.16 = f32[128,1024]{1,0:T(8,128)S(1)} collective-permute-done((f32[128,1024]{1,0:T(8,128)S(1)}, f32[128,1024]{1,0:T(8,128)S(1)}, u32[]{:S(2)}, u32[]{:S(2)}) %collective-permute-start.16) | collective-permute-done | bytes 524320 | tf_op jit(solution)/shard_map/ppermute | solution.py:205
  364.8 10.7 %collective-permute-done.12 = f32[128,1024]{1,0:T(8,128)S(1)} collective-permute-done((f32[128,1024]{1,0:T(8,128)S(1)}, f32[128,1024]{1,0:T(8,128)S(1)}, u32[]{:S(2)}, u32[]{:S(2)}) %collective-permute-start.12) | collective-permute-done | bytes 524320 | tf_op jit(solution)/shard_map/ppermute | solution.py:205
  376.0 7.7 %collective-permute-done.8 = f32[128,1024]{1,0:T(8,128)S(1)} collective-permute-done((f32[128,1024]{1,0:T(8,128)S(1)}, f32[128,1024]{1,0:T(8,128)S(1)}, u32[]{:S(2)}, u32[]{:S(2)}) %collective-permute-start.8) | collective-permute-done | bytes 524320 | tf_op jit(solution)/shard_map/ppermute | solution.py:205
  383.8 1.8 collective-permute-done.9
  386.5 5.8 %assemble_hidden.1 = bf16[4,128,4096]{2,1,0:T(8,128)(2,1)} custom-call(s32[1]{0:T(128)} %bitcast.sp_ref, f32[4,32,1024]{2,1,0:T(8,128)} %bitcast.86, f32[4,32,1024]{2,1,0:T(8,128)} %bitcast.94, f32[4,32,1024]{2,1,0:T(8,128)} %bitcast.93, f32[4,32,1024]{2,1,0:T(8,128)} %bitcast.98, f32[4,32,1024]{2,1,0:T(8,128)} %bitcast.85, f32[4,32,1024]{2,1,0:T(8,128)} %bitcast.92, ...), custom_call_target="tpu_custom_call" | custom-call | tf_op jit(solution)/shard_map/assemble_hidden/pallas_call | solution.py:115
  (94 shorter events, 9.2 us)
Async XLA Ops:
  0.6 6.0 %copy-start.17 = (bf16[4096]{0:T(1024)(128)(2,1)S(1)}, bf16[4096]{0:T(1024)(128)(2,1)}, u32[]{:S(2)}) copy-start(bf16[4096]{0:T(1024)(128)(2,1)} %param.26) | copy-start | bytes 24580
  7.9 6.0 %copy-start.19 = (bf16[4096,512]{1,0:T(8,128)(2,1)S(1)}, bf16[4096,512]{1,0:T(8,128)(2,1)}, u32[]{:S(2)}) copy-start(bf16[4096,512]{1,0:T(8,128)(2,1)} %param.21) | copy-start | bytes 12582916
  11.9 2.0 copy-start
  136.3 4.8 %collective-permute-start.2 = (f32[64,64,128]{2,1,0:T(8,128)S(1)}, f32[64,64,128]{2,1,0:T(8,128)S(1)}, u32[]{:S(2)}, u32[]{:S(2)}) collective-permute-start(f32[64,64,128]{2,1,0:T(8,128)S(1)} %slice.89), channel_id=1, source_target_pairs={{0,1},{1,0},{2,3},{3,2},{4,5},{5,4},{6,7},{7,6}} | collective-permute-start | bytes 6291464 | tf_op jit(solution)/shard_map/ppermute | solution.py:180
  137.2 3.8 collective-permute-start
  142.4 27.1 %collective-permute-start.3 = (f32[32,64,128]{2,1,0:T(8,128)S(1)}, f32[32,64,128]{2,1,0:T(8,128)S(1)}, u32[]{:S(2)}, u32[]{:S(2)}) collective-permute-start(f32[32,64,128]{2,1,0:T(8,128)S(1)} %slice.113), channel_id=1, source_target_pairs={{0,2},{2,0},{1,3},{3,1},{4,6},{6,4},{5,7},{7,5}} | collective-permute-start | bytes 3145736 | tf_op jit(solution)/shard_map/ppermute | solution.py:184
  145.3 24.0 %collective-permute-start.1 = (f32[32,64]{1,0:T(8,128)S(1)}, f32[32,64]{1,0:T(8,128)S(1)}, u32[]{:S(2)}, u32[]{:S(2)}) collective-permute-start(f32[32,64]{1,0:T(8,128)S(1)} %slice.111), channel_id=1, source_target_pairs={{0,2},{2,0},{1,3},{3,1},{4,6},{6,4},{5,7},{7,5}} | collective-permute-start | bytes 24584 | tf_op jit(solution)/shard_map/ppermute | solution.py:184
  145.4 24.1 %collective-permute-start.4 = (f32[32,64]{1,0:T(8,128)S(1)}, f32[32,64]{1,0:T(8,128)S(1)}, u32[]{:S(2)}, u32[]{:S(2)}) collective-permute-start(f32[32,64]{1,0:T(8,128)S(1)} %slice.117), channel_id=1, source_target_pairs={{0,2},{2,0},{1,3},{3,1},{4,6},{6,4},{5,7},{7,5}} | collective-permute-start | bytes 24584 | tf_op jit(solution)/shard_map/ppermute | solution.py:184
  171.2 9.9 %copy-start.18 = (bf16[4096]{0:T(1024)(128)(2,1)S(1)}, bf16[4096]{0:T(1024)(128)(2,1)}, u32[]{:S(2)}) copy-start(bf16[4096]{0:T(1024)(128)(2,1)} %param.27) | copy-start | bytes 24580
  179.3 47.1 %collective-permute-start.5 = (f32[128,4096]{1,0:T(8,128)S(1)}, f32[128,4096]{1,0:T(8,128)}, u32[]{:S(2)}, u32[]{:S(2)}) collective-permute-start(f32[128,4096]{1,0:T(8,128)S(1)} %fusion.35), channel_id=1, source_target_pairs={{0,4},{4,0},{1,5},{5,1},{2,6},{6,2},{3,7},{7,3}} | collective-permute-start | bytes 6291464 | tf_op jit(solution)/shard_map/ppermute | solution.py:191
  291.2 14.8 %collective-permute-start.6 = (f32[128,1024]{1,0:T(8,128)S(1)}, f32[128,1024]{1,0:T(8,128)S(1)}, u32[]{:S(2)}, u32[]{:S(2)}) collective-permute-start(f32[128,1024]{1,0:T(8,128)S(1)} %fusion.6), channel_id=1, source_target_pairs={{0,4},{4,0},{1,5},{5,1},{2,6},{6,2},{3,7},{7,3}} | collective-permute-start | bytes 1572872 | tf_op jit(solution)/shard_map/ppermute | solution.py:203
  292.7 24.6 %collective-permute-start.10 = (f32[128,1024]{1,0:T(8,128)S(1)}, f32[128,1024]{1,0:T(8,128)S(1)}, u32[]{:S(2)}, u32[]{:S(2)}) collective-permute-start(f32[128,1024]{1,0:T(8,128)S(1)} %fusion.4), channel_id=1, source_target_pairs={{0,4},{4,0},{1,5},{5,1},{2,6},{6,2},{3,7},{7,3}} | collective-permute-start | bytes 1572872 | tf_op jit(solution)/shard_map/ppermute | solution.py:203
  293.2 35.2 %collective-permute-start.14 = (f32[128,1024]{1,0:T(8,128)S(1)}, f32[128,1024]{1,0:T(8,128)S(1)}, u32[]{:S(2)}, u32[]{:S(2)}) collective-permute-start(f32[128,1024]{1,0:T(8,128)S(1)} %fusion.2), channel_id=1, source_target_pairs={{0,4},{4,0},{1,5},{5,1},{2,6},{6,2},{3,7},{7,3}} | collective-permute-start | bytes 1572872 | tf_op jit(solution)/shard_map/ppermute | solution.py:203
  294.7 42.8 %collective-permute-start.18 = (f32[128,1024]{1,0:T(8,128)S(1)}, f32[128,1024]{1,0:T(8,128)S(1)}, u32[]{:S(2)}, u32[]{:S(2)}) collective-permute-start(f32[128,1024]{1,0:T(8,128)S(1)} %fusion), channel_id=1, source_target_pairs={{0,4},{4,0},{1,5},{5,1},{2,6},{6,2},{3,7},{7,3}} | collective-permute-start | bytes 1572872 | tf_op jit(solution)/shard_map/ppermute | solution.py:203
  338.2 48.3 %copy-start.1 = (f32[128,1024]{1,0:T(8,128)}, f32[128,1024]{1,0:T(8,128)S(1)}, u32[]{:S(2)}) copy-start(f32[128,1024]{1,0:T(8,128)S(1)} %get-tuple-element.24) | copy-start | bytes 1572868
  338.2 48.3 %copy-start.2 = (f32[128,1024]{1,0:T(8,128)}, f32[128,1024]{1,0:T(8,128)S(1)}, u32[]{:S(2)}) copy-start(f32[128,1024]{1,0:T(8,128)S(1)} %get-tuple-element.25) | copy-start | bytes 1572868
  338.2 48.3 %copy-start.3 = (f32[128,1024]{1,0:T(8,128)}, f32[128,1024]{1,0:T(8,128)S(1)}, u32[]{:S(2)}) copy-start(f32[128,1024]{1,0:T(8,128)S(1)} %get-tuple-element.26) | copy-start | bytes 1572868
  338.2 48.3 %copy-start.4 = (f32[128,1024]{1,0:T(8,128)}, f32[128,1024]{1,0:T(8,128)S(1)}, u32[]{:S(2)}) copy-start(f32[128,1024]{1,0:T(8,128)S(1)} %get-tuple-element.27) | copy-start | bytes 1572868
  338.2 14.8 %collective-permute-start.20 = (f32[128,1024]{1,0:T(8,128)S(1)}, f32[128,1024]{1,0:T(8,128)S(1)}, u32[]{:S(2)}, u32[]{:S(2)}) collective-permute-start(f32[128,1024]{1,0:T(8,128)S(1)} %get-tuple-element.24), channel_id=1, source_target_pairs={{0,2},{2,0},{1,3},{3,1},{4,6},{6,4},{5,7},{7,5}} | collective-permute-start | bytes 1572872 | tf_op jit(solution)/shard_map/ppermute | solution.py:205
  339.4 13.6 %collective-permute-start.19 = (f32[128,1024]{1,0:T(8,128)S(1)}, f32[128,1024]{1,0:T(8,128)S(1)}, u32[]{:S(2)}, u32[]{:S(2)}) collective-permute-start(f32[128,1024]{1,0:T(8,128)S(1)} %get-tuple-element.24), channel_id=1, source_target_pairs={{0,1},{1,0},{2,3},{3,2},{4,5},{5,4},{6,7},{7,6}} | collective-permute-start | bytes 1572872 | tf_op jit(solution)/shard_map/ppermute | solution.py:204
  339.4 24.9 %collective-permute-start.16 = (f32[128,1024]{1,0:T(8,128)S(1)}, f32[128,1024]{1,0:T(8,128)S(1)}, u32[]{:S(2)}, u32[]{:S(2)}) collective-permute-start(f32[128,1024]{1,0:T(8,128)S(1)} %get-tuple-element.25), channel_id=1, source_target_pairs={{0,2},{2,0},{1,3},{3,1},{4,6},{6,4},{5,7},{7,5}} | collective-permute-start | bytes 1572872 | tf_op jit(solution)/shard_map/ppermute | solution.py:205
  340.3 24.0 %collective-permute-start.15 = (f32[128,1024]{1,0:T(8,128)S(1)}, f32[128,1024]{1,0:T(8,128)S(1)}, u32[]{:S(2)}, u32[]{:S(2)}) collective-permute-start(f32[128,1024]{1,0:T(8,128)S(1)} %get-tuple-element.25), channel_id=1, source_target_pairs={{0,1},{1,0},{2,3},{3,2},{4,5},{5,4},{6,7},{7,6}} | collective-permute-start | bytes 1572872 | tf_op jit(solution)/shard_map/ppermute | solution.py:204
  340.5 35.0 %collective-permute-start.12 = (f32[128,1024]{1,0:T(8,128)S(1)}, f32[128,1024]{1,0:T(8,128)S(1)}, u32[]{:S(2)}, u32[]{:S(2)}) collective-permute-start(f32[128,1024]{1,0:T(8,128)S(1)} %get-tuple-element.26), channel_id=1, source_target_pairs={{0,2},{2,0},{1,3},{3,1},{4,6},{6,4},{5,7},{7,5}} | collective-permute-start | bytes 1572872 | tf_op jit(solution)/shard_map/ppermute | solution.py:205
  353.0 33.4 %copy-start.5 = (f32[128,1024]{1,0:T(8,128)}, f32[128,1024]{1,0:T(8,128)S(1)}, u32[]{:S(2)}) copy-start(f32[128,1024]{1,0:T(8,128)S(1)} %collective-permute-done.20) | copy-start | bytes 1572868
  353.0 22.5 %collective-permute-start.11 = (f32[128,1024]{1,0:T(8,128)S(1)}, f32[128,1024]{1,0:T(8,128)S(1)}, u32[]{:S(2)}, u32[]{:S(2)}) collective-permute-start(f32[128,1024]{1,0:T(8,128)S(1)} %get-tuple-element.26), channel_id=1, source_target_pairs={{0,1},{1,0},{2,3},{3,2},{4,5},{5,4},{6,7},{7,6}} | collective-permute-start | bytes 1572872 | tf_op jit(solution)/shard_map/ppermute | solution.py:204
  353.0 33.4 %copy-start.6 = (f32[128,1024]{1,0:T(8,128)}, f32[128,1024]{1,0:T(8,128)S(1)}, u32[]{:S(2)}) copy-start(f32[128,1024]{1,0:T(8,128)S(1)} %collective-permute-done.19) | copy-start | bytes 1572868
  353.1 30.7 %collective-permute-start.8 = (f32[128,1024]{1,0:T(8,128)S(1)}, f32[128,1024]{1,0:T(8,128)S(1)}, u32[]{:S(2)}, u32[]{:S(2)}) collective-permute-start(f32[128,1024]{1,0:T(8,128)S(1)} %get-tuple-element.27), channel_id=1, source_target_pairs={{0,2},{2,0},{1,3},{3,1},{4,6},{6,4},{5,7},{7,5}} | collective-permute-start | bytes 1572872 | tf_op jit(solution)/shard_map/ppermute | solution.py:205
  364.3 19.5 %copy-start.7 = (f32[128,1024]{1,0:T(8,128)}, f32[128,1024]{1,0:T(8,128)S(1)}, u32[]{:S(2)}) copy-start(f32[128,1024]{1,0:T(8,128)S(1)} %collective-permute-done.16) | copy-start | bytes 1572868
  364.3 19.5 %collective-permute-start.7 = (f32[128,1024]{1,0:T(8,128)S(1)}, f32[128,1024]{1,0:T(8,128)S(1)}, u32[]{:S(2)}, u32[]{:S(2)}) collective-permute-start(f32[128,1024]{1,0:T(8,128)S(1)} %get-tuple-element.27), channel_id=1, source_target_pairs={{0,1},{1,0},{2,3},{3,2},{4,5},{5,4},{6,7},{7,6}} | collective-permute-start | bytes 1572872 | tf_op jit(solution)/shard_map/ppermute | solution.py:204
  364.3 19.5 %copy-start.8 = (f32[128,1024]{1,0:T(8,128)}, f32[128,1024]{1,0:T(8,128)S(1)}, u32[]{:S(2)}) copy-start(f32[128,1024]{1,0:T(8,128)S(1)} %collective-permute-done.15) | copy-start | bytes 1572868
  364.3 19.5 %collective-permute-start.21 = (f32[128,1024]{1,0:T(8,128)S(1)}, f32[128,1024]{1,0:T(8,128)S(1)}, u32[]{:S(2)}, u32[]{:S(2)}) collective-permute-start(f32[128,1024]{1,0:T(8,128)S(1)} %collective-permute-done.20), channel_id=1, source_target_pairs={{0,1},{1,0},{2,3},{3,2},{4,5},{5,4},{6,7},{7,6}} | collective-permute-start | bytes 1572872 | tf_op jit(solution)/shard_map/ppermute | solution.py:206
  375.5 8.3 %copy-start.9 = (f32[128,1024]{1,0:T(8,128)}, f32[128,1024]{1,0:T(8,128)S(1)}, u32[]{:S(2)}) copy-start(f32[128,1024]{1,0:T(8,128)S(1)} %collective-permute-done.12) | copy-start | bytes 1572868
  375.5 8.3 %collective-permute-start.17 = (f32[128,1024]{1,0:T(8,128)S(1)}, f32[128,1024]{1,0:T(8,128)S(1)}, u32[]{:S(2)}, u32[]{:S(2)}) collective-permute-start(f32[128,1024]{1,0:T(8,128)S(1)} %collective-permute-done.16), channel_id=1, source_target_pairs={{0,1},{1,0},{2,3},{3,2},{4,5},{5,4},{6,7},{7,6}} | collective-permute-start | bytes 1572872 | tf_op jit(solution)/shard_map/ppermute | solution.py:206
  375.5 10.1 %copy-start.10 = (f32[128,1024]{1,0:T(8,128)}, f32[128,1024]{1,0:T(8,128)S(1)}, u32[]{:S(2)}) copy-start(f32[128,1024]{1,0:T(8,128)S(1)} %collective-permute-done.11) | copy-start | bytes 1572868
  375.5 8.3 %collective-permute-start.13 = (f32[128,1024]{1,0:T(8,128)S(1)}, f32[128,1024]{1,0:T(8,128)S(1)}, u32[]{:S(2)}, u32[]{:S(2)}) collective-permute-start(f32[128,1024]{1,0:T(8,128)S(1)} %collective-permute-done.12), channel_id=1, source_target_pairs={{0,1},{1,0},{2,3},{3,2},{4,5},{5,4},{6,7},{7,6}} | collective-permute-start | bytes 1572872 | tf_op jit(solution)/shard_map/ppermute | solution.py:206
  383.7 1.9 copy-start.11
  383.7 1.9 collective-permute-start.9
  383.7 1.9 copy-start.12
  383.8 1.9 copy-start.13
  383.8 1.9 copy-start.14
  383.8 1.8 copy-start.15
  385.6 0.8 copy-start.16

commit v2 on v1

--- a/solution.py
+++ b/solution.py
@@ -20,16 +20,123 @@
     return wide_vals * inv_rms * gain_vec.astype(jnp.float32)
 
 
-def apply_rope(vector, tok_pos):
-    head_dim = vector.shape[-1]
+def rope_tables(tok_pos, head_dim):
     half_dim = head_dim // 2
     freqs = ROPE_BASE ** (-(jnp.arange(half_dim, dtype=jnp.float32) * (2.0 / head_dim)))
-    angles = tok_pos.astype(jnp.float32)[..., None] * freqs
-    cos_tab = jnp.cos(angles)[..., None, :]
-    sin_tab = jnp.sin(angles)[..., None, :]
-    lower_half = vector[..., :half_dim]
-    upper_half = vector[..., half_dim:]
-    return jnp.concatenate([lower_half * cos_tab - upper_half * sin_tab, upper_half * cos_tab + lower_half * sin_tab], axis=-1)
+    angles = tok_pos.astype(jnp.float32)[:, None] * freqs[None, :]
+    cos_tab = jnp.cos(angles)
+    sin_tab = jnp.sin(angles)
+    return jnp.concatenate([cos_tab, cos_tab], axis=-1), jnp.concatenate([-sin_tab, sin_tab], axis=-1)
+
+
+def qkv_kernel(dims, x_ref, norm_ref, cos_ref, sin_ref, qg_ref, kg_ref, wq_hbm, wk_hbm, wv_hbm, q_ref, k_ref, v_ref,
+               n_ref, y_ref, qf_ref, wbuf, sems):
+    heads, kv_heads, hd, unit, n_buf = dims
+    tokens = x_ref.shape[0]
+    rows_blk = 64
+    per = unit // hd
+    n_q, n_kv = heads // per, kv_heads // per
+    total = n_q + 2 * n_kv
+
+    def fetch(hbm, col, slot):
+        return pltpu.make_async_copy(hbm.at[:, pl.ds(pl.multiple_of(col * unit, unit), unit)], wbuf.at[slot], sems.at[slot])
+
+    def start(g):
+        slot = lax.rem(g, n_buf)
+
+        @pl.when(g < n_q)
+        def _():
+            fetch(wq_hbm, g, slot).start()
+
+        @pl.when((g >= n_q) & (g < n_q + n_kv))
+        def _():
+            fetch(wk_hbm, g - n_q, slot).start()
+
+        @pl.when((g >= n_q + n_kv) & (g < total))
+        def _():
+            fetch(wv_hbm, g - n_q - n_kv, slot).start()
+
+    for g in range(n_buf - 1):
+        start(jnp.int32(g))
+
+    def norm_rows(i, carry):
+        rows = pl.ds(pl.multiple_of(i * rows_blk, rows_blk), rows_blk)
+        wide = x_ref[rows, :].astype(jnp.float32)
+        inv = lax.rsqrt(jnp.mean(wide * wide, axis=-1, keepdims=True) + NORM_EPS)
+        n_ref[rows, :] = (wide * inv * norm_ref[...].astype(jnp.float32)).astype(n_ref.dtype)
+        return carry
+
+    lax.fori_loop(0, tokens // rows_blk, norm_rows, 0)
+
+    def project(g):
+        slot = lax.rem(g, n_buf)
+        start(g + n_buf - 1)
+        fetch(wq_hbm, 0, slot).wait()
+        y_ref[...] = jnp.dot(n_ref[...], wbuf[slot], preferred_element_type=jnp.float32)
+
+    def rotate(vec, gain_ref):
+        inv = lax.rsqrt(jnp.mean(vec * vec, axis=-1, keepdims=True) + NORM_EPS)
+        vec = vec * inv * gain_ref[...].astype(jnp.float32)
+        return vec * cos_ref[...] + pltpu.roll(vec, hd // 2, 1) * sin_ref[...]
+
+    def q_unit(g, carry):
+        project(g)
+        for h in range(per):
+            qf_ref[pl.ds(g * per + h, tokens, stride=heads), :] = rotate(y_ref[:, h * hd:(h + 1) * hd], qg_ref)
+        return carry
+
+    lax.fori_loop(0, n_q, q_unit, 0)
+
+    def k_unit(g, carry):
+        project(n_q + g)
+        for h in range(per):
+            row = rotate(y_ref[:, h * hd:(h + 1) * hd], kg_ref).astype(jnp.bfloat16)
+            k_ref[pl.ds(g * per + h, tokens, stride=kv_heads), :] = row.astype(jnp.float32)
+        return carry
+
+    lax.fori_loop(0, n_kv, k_unit, 0)
+
+    def v_unit(g, carry):
+        project(n_q + n_kv + g)
+        for h in range(per):
+            row = y_ref[:, h * hd:(h + 1) * hd].astype(jnp.bfloat16)
+            v_ref[pl.ds(g * per + h, tokens, stride=kv_heads), :] = row.astype(jnp.float32)
+        return carry
+
+    lax.fori_loop(0, n_kv, v_unit, 0)
+
+    def cast_rows(i, carry):
+        rows = pl.ds(pl.multiple_of(i * 512, 512), 512)
+        q_ref[rows, :] = qf_ref[rows, :].astype(q_ref.dtype)
+        return carry
+
+    lax.fori_loop(0, tokens * heads // 512, cast_rows, 0)
+
+
+def project_qkv(x, norm, cos_tab, sin_tab, q_gain, k_gain, w_q, w_k, w_v):
+    tokens, width = x.shape
+    hd = q_gain.shape[0]
+    heads, kv_heads = w_q.shape[1] // hd, w_k.shape[1] // hd
+    unit, n_buf = 2 * hd, 4
+    vmem = pl.BlockSpec(memory_space=pltpu.VMEM)
+    hbm = pl.BlockSpec(memory_space=pl.ANY)
+    cols = (heads + 2 * kv_heads) * hd
+    return pl.pallas_call(
+        functools.partial(qkv_kernel, (heads, kv_heads, hd, unit, n_buf)),
+        in_specs=[vmem] * 6 + [hbm] * 3,
+        out_specs=[vmem] * 3,
+        out_shape=[jax.ShapeDtypeStruct((tokens * heads, hd), jnp.bfloat16),
+                   jax.ShapeDtypeStruct((tokens * kv_heads, hd), jnp.float32),
+                   jax.ShapeDtypeStruct((tokens * kv_heads, hd), jnp.float32)],
+        scratch_shapes=[pltpu.VMEM((tokens, width), jnp.bfloat16),
+                        pltpu.VMEM((tokens, unit), jnp.float32),
+                        pltpu.VMEM((tokens * heads, hd), jnp.float32),
+                        pltpu.VMEM((n_buf, width, unit), jnp.bfloat16),
+                        pltpu.SemaphoreType.DMA((n_buf,))],
+        compiler_params=pltpu.CompilerParams(vmem_limit_bytes=48 * 2**20),
+        cost_estimate=pl.CostEstimate(flops=2 * tokens * width * cols, bytes_accessed=2 * width * cols, transcendentals=0),
+        name="project_qkv",
+    )(x, norm.reshape(1, width), cos_tab, sin_tab, q_gain.reshape(1, hd), k_gain.reshape(1, hd), w_q, w_k, w_v)
 
 
 def attn_kernel(dims, order_ref, rel_ref, q_ref, kn_ref, vn_ref, k_ref, v_ref, ko_ref, vo_ref, o_ref, ml_ref):
@@ -55,7 +162,8 @@
         inside = (win_row >= off) & (win_row < off + new_rows)
         for src, new, dst in ((k_ref, kn_ref, ko_ref), (v_ref, vn_ref, vo_ref)):
             dst[j] = src[j]
-            rolled = pltpu.roll(jnp.concatenate([new[j].astype(jnp.float32), pad], axis=0), off & (2 * new_rows - 1), 0)
+            fresh = [new[t, j * kv_heads:(j + 1) * kv_heads, :] for t in range(n_steps)]
+            rolled = pltpu.roll(jnp.concatenate(fresh + [pad], axis=0), off & (2 * new_rows - 1), 0)
             window = src[j, pl.ds(base, 2 * new_rows), :].astype(jnp.float32)
             dst[j, pl.ds(base, 2 * new_rows), :] = jnp.where(inside, rolled, window).astype(dst.dtype)
         query = q_ref[:, j].reshape(rows_q, hd)
@@ -72,11 +180,10 @@
 def attention(order, rel, q, k_new, v_new, k_cache, v_cache, kv_heads, exp_scale, n_req=4):
     n_steps, n_batch, heads, hd = q.shape
     rows_c = k_cache.shape[1]
-    new_rows = n_steps * kv_heads
     rows_q = n_steps * heads
     dims = (n_req, n_steps, heads, kv_heads, heads // kv_heads, rows_c, hd, exp_scale)
     cache_blk = pl.BlockSpec((n_req, rows_c, hd), lambda i, order, rel: (order[i], 0, 0))
-    new_blk = pl.BlockSpec((n_req, new_rows, hd), lambda i, order, rel: (order[i], 0, 0))
+    new_blk = pl.BlockSpec((n_steps, n_req * kv_heads, hd), lambda i, order, rel: (0, order[i], 0))
     cache_shape = jax.ShapeDtypeStruct(k_cache.shape, k_cache.dtype)
     return pl.pallas_call(
         functools.partial(attn_kernel, dims),
@@ -156,15 +263,13 @@
         core, chip = sp % 2, sp // 2
         own = n_batch // 4
 
-        tok_pos = start_pos[None, :] + jnp.arange(n_steps, dtype=jnp.int32)[:, None]
-        normed = rms_scale(hidden, attn_norm).astype(jnp.bfloat16).reshape(n_steps * n_batch, width)
-        q_raw = jnp.dot(normed, w_q, preferred_element_type=jnp.float32).reshape(n_steps, n_batch, heads, hd)
-        k_raw = jnp.dot(normed, w_k, preferred_element_type=jnp.float32).reshape(n_steps, n_batch, kv_heads, hd)
-        v_new = jnp.dot(normed, w_v, preferred_element_type=jnp.float32).astype(jnp.bfloat16).reshape(n_steps, n_batch, kv_heads, hd)
-        q_rot = apply_rope(rms_scale(q_raw, q_gain), tok_pos).astype(jnp.bfloat16)
-        k_new = apply_rope(rms_scale(k_raw, k_gain), tok_pos).astype(jnp.bfloat16)
-        k_rows = k_new.transpose(1, 0, 2, 3).reshape(n_batch, n_steps * kv_heads, hd)
-        v_rows = v_new.transpose(1, 0, 2, 3).reshape(n_batch, n_steps * kv_heads, hd)
+        tok_pos = (start_pos[None, :] + jnp.arange(n_steps, dtype=jnp.int32)[:, None]).reshape(-1)
+        cos_tab, sin_tab = rope_tables(tok_pos, hd)
+        q_rows, k_rows, v_rows = project_qkv(hidden.reshape(n_steps * n_batch, width), attn_norm, cos_tab, sin_tab,
+                                             q_gain, k_gain, w_q, w_k, w_v)
+        q_rot = q_rows.reshape(n_steps, n_batch, heads, hd)
+        k_rows = k_rows.reshape(n_steps, n_batch * kv_heads, hd)
+        v_rows = v_rows.reshape(n_steps, n_batch * kv_heads, hd)
 
         n_req = 4
         per = own // n_req

time: 395 us -> 347 us (0.88)
  local copies, waits for them, and re-layouts: 39.1 us -> 4.87 us
  Pallas kernels: 64.8 us -> 89.6 us
  matrix products: 92.8 us -> 70.7 us
  other arithmetic: 23.1 us -> 7.71 us
    dot_general x3 -> x0, local copies, waits for them, and re-layouts: 33.1 us -> none  [the longest x2 26.6 us: shard_body(): jnp.dot(normed, w_q, preferred_element_type=jnp.float32)]
    pallas_call x0 -> x1, Pallas kernels: none -> 27.7 us  [project_qkv(): pl.pallas_call(functools.partial(qkv_kernel, (heads, kv_heads, hd, unit,...]
    dot_general x3 -> x0, matrix products: 22 us -> none  [the longest x1 14.3 us: shard_body(): jnp.dot(normed, w_q, preferred_element_type=jnp.float32)]
    convert_element_type x2 -> x1, other arithmetic: 4.64 us -> 0.66 us  [rope_tables(): angles = tok_pos.astype(jnp.float32)[:, None] * freqs[None, :]]
where the time goes in v2:
time: 347 us; the launch traced here: 345 us
  waiting for transfers between devices  154 us (44%)
  Pallas kernels  89.6 us (26%)
  matrix products  70.7 us (20%)
  starting transfers between devices  17.4 us (5%)
  other arithmetic  7.71 us (2%)
  local copies, waits for them, and re-layouts  4.87 us (1%)
    pallas_call x1, Pallas kernels, attention(): pl.pallas_call(functools.partial(attn_kernel, dims), grid_spec=pltpu.Pref...  56.1 us
    ppermute x1, waiting for transfers between devices, shard_body(): attn_out = o_mine + lax.ppermute(o_mine, 'tp', tp_perm)  44 us
    ppermute x4, waiting for transfers between devices, shard_body(): lax.ppermute(mine, 'tp', tp_perm)  42.3 us
    ppermute x4, waiting for transfers between devices, shard_body(): across = lax.ppermute(mine, 'sp', chip_perm)  39.8 us
    pallas_call x1, Pallas kernels, project_qkv(): pl.pallas_call(functools.partial(qkv_kernel, (heads, kv_heads, hd, unit,...  27.7 us
    dot_general x4, matrix products, shard_body(): mine = jnp.dot(mlp_act, w_down[:, sl], preferred_element_type=jnp.float32)  22.9 us
    ppermute x3, waiting for transfers between devices, shard_body(): far = [lax.ppermute(part_[:own], 'sp', chip_perm) for part_ in both]  22.1 us
    dot_general x1, matrix products, shard_body(): gate_act = jnp.dot(mlp_in, w_gate, preferred_element_type=jnp.float32)  20.7 us
  transfers between devices with their start and end apart: 22, of which 13 were waited for; matrix products, arithmetic and copies ran while one was open for 0% of the time, Pallas kernels for 0%

profile of v2, /device:TPU:0, one launch (start us, length us, event | category | flops | bytes accessed | tf_op | source)
XLA Modules:
  0.0 345.3 jit_solution(11719260399163591692)
XLA Ops:
  0.7 0.7 convert_bitcast_fusion
  1.3 0.7 broadcast_subtract_fusion.rel_ref
  2.2 0.7 reshape.179.norm_ref
  2.9 1.0 fusion.19
  4.2 0.6 copy-done
  4.8 0.7 copy-done.1
  5.5 27.7 %project_qkv.1 = (bf16[8192,128]{1,0:T(8,128)(2,1)S(1)}, f32[2048,128]{1,0:T(8,128)S(1)}, f32[2048,128]{1,0:T(8,128)S(1)}) custom-call(bf16[512,4096]{1,0:T(8,128)(2,1)} %bitcast.75, bf16[1,4096]{1,0:T(2,128)(2,1)S(1)} %reshape.179.norm_ref, f32[512,128]{1,0:T(8,128)S(1)} %get-tuple-element.33.cos_ref, f32[512,128]{1,0:T(8,128)S(1)} %get-tuple-element.34.sin_ref, ...), custom_call_target="tpu_custom_call" | custom-call | flops 12884901888 | bytes 25165824 | tf_op jit(solution)/shard_map/project_qkv/pallas_call | solution.py:124
  33.2 56.1 %decode_attention.1 = (bf16[128,1024,128]{2,1,0:T(8,128)(2,1)}, bf16[128,1024,128]{2,1,0:T(8,128)(2,1)}, f32[128,64,128]{2,1,0:T(8,128)S(1)}, f32[128,1,128]{2,1,0:T(1,128)S(1)}) custom-call(s32[32]{0:T(128)S(1)} %add.122.order_ref, s32[128]{0:T(128)S(1)} %broadcast_subtract_fusion.rel_ref, bf16[4,128,16,128]{3,2,1,0:T(8,128)(2,1)S(1)} %bitcast.50, ...), custom_call_target="tpu_custom_call" | custom-call | flops 4294967296 | bytes 134217728 | tf_op jit(solution)/shard_map/decode_attention/pallas_call | solution.py:188
  89.5 0.9 collective-permute-start.2
  90.4 3.8 %collective-permute-done = f32[64,128]{1,0:T(8,128)S(1)} collective-permute-done((f32[64,128]{1,0:T(8,128)S(1)}, f32[64,128]{1,0:T(8,128)S(1)}, u32[]{:S(2)}, u32[]{:S(2)}) %collective-permute-start) | collective-permute-done | bytes 32800 | tf_op jit(solution)/shard_map/ppermute | solution.py:286
  94.3 1.3 multiply_add_fusion
  95.6 2.9 collective-permute-start.3
  98.5 2.0 collective-permute-start.4
  100.5 22.0 %collective-permute-done.1 = f32[32,64]{1,0:T(8,128)S(1)} collective-permute-done((f32[32,64]{1,0:T(8,128)S(1)}, f32[32,64]{1,0:T(8,128)S(1)}, u32[]{:S(2)}, u32[]{:S(2)}) %collective-permute-start.1) | collective-permute-done | bytes 8224 | tf_op jit(solution)/shard_map/ppermute | solution.py:289
  122.7 1.0 fusion.15
  124.1 8.1 %fusion.29 = f32[128,4096]{1,0:T(8,128)S(1)} fusion(bf16[128,2048]{1,0:T(8,128)(2,1)S(1)} %bitcast.58, bf16[2048,4096]{1,0:T(8,128)(2,1)} %param.22), kind=kOutput, calls=%fused_computation.53 | convolution fusion | flops 2147483648 | bytes 19398656 | tf_op jit(solution)/shard_map/dot_general | solution.py:295
  132.3 1.8 collective-permute-start.5
  134.1 1.3 constant_dynamic-slice_fusion
  135.4 44.0 %collective-permute-done.5 = f32[128,4096]{1,0:T(8,128)} collective-permute-done((f32[128,4096]{1,0:T(8,128)S(1)}, f32[128,4096]{1,0:T(8,128)}, u32[]{:S(2)}, u32[]{:S(2)}) %collective-permute-start.5) | collective-permute-done | bytes 2097184 | tf_op jit(solution)/shard_map/ppermute | solution.py:296
  179.4 2.1 fusion.9
  181.5 20.7 %fusion.17 = f32[128,6144]{1,0:T(8,128)} fusion(bf16[4096,6144]{1,0:T(8,128)(2,1)} %param.23, bf16[128,4096]{1,0:T(8,128)(2,1)S(1)} %get-tuple-element.18, f32[4096]{0:T(1024)S(1)} %convert_element_type.54, f32[128]{0:T(128)S(1)} %add_rsqrt_fusion), kind=kOutput, calls=%fused_computation.28 | convolution fusion | flops 6444548096 | bytes 54542848 | tf_op jit(solution)/shard_map/dot_general | solution.py:299
  202.1 19.0 %fusion.8 = bf16[128,6144]{1,0:T(8,128)(2,1)S(1)} fusion(bf16[4096,6144]{1,0:T(8,128)(2,1)} %param.24, f32[128,6144]{1,0:T(8,128)} %fusion.17, bf16[128,4096]{1,0:T(8,128)(2,1)S(1)} %get-tuple-element.18, f32[4096]{0:T(1024)S(1)} %convert_element_type.54, f32[128]{0:T(128)S(1)} %add_rsqrt_fusion), kind=kOutput, calls=%fused_computation.9 | convolution fusion | flops 6449266688 | bytes 56115712 | tf_op jit(solution)/shard_map/dot_general | solution.py:300
  221.1 5.7 %fusion = f32[128,1024]{1,0:T(8,128)S(1)} fusion(bf16[128,6144]{1,0:T(8,128)(2,1)S(1)} %fusion.8, bf16[6144,4096]{1,0:T(8,128)(2,1)} %param.25), kind=kOutput, calls=%fused_computation | convolution fusion | flops 1610612736 | bytes 14680064 | tf_op jit(solution)/shard_map/dot_general | solution.py:307
  226.9 5.7 %fusion.2 = f32[128,1024]{1,0:T(8,128)S(1)} fusion(bf16[128,6144]{1,0:T(8,128)(2,1)S(1)} %fusion.8, bf16[6144,4096]{1,0:T(8,128)(2,1)} %param.25), kind=kOutput, calls=%fused_computation.2 | convolution fusion | flops 1610612736 | bytes 14680064 | tf_op jit(solution)/shard_map/dot_general | solution.py:307
  232.6 5.7 %fusion.4 = f32[128,1024]{1,0:T(8,128)S(1)} fusion(bf16[128,6144]{1,0:T(8,128)(2,1)S(1)} %fusion.8, bf16[6144,4096]{1,0:T(8,128)(2,1)} %param.25), kind=kOutput, calls=%fused_computation.4 | convolution fusion | flops 1610612736 | bytes 14680064 | tf_op jit(solution)/shard_map/dot_general | solution.py:307
  238.3 5.7 %fusion.6 = f32[128,1024]{1,0:T(8,128)S(1)} fusion(bf16[128,6144]{1,0:T(8,128)(2,1)S(1)} %fusion.8, bf16[6144,4096]{1,0:T(8,128)(2,1)} %param.25), kind=kOutput, calls=%fused_computation.6 | convolution fusion | flops 1610612736 | bytes 14680064 | tf_op jit(solution)/shard_map/dot_general | solution.py:307
  244.1 1.5 collective-permute-start.6
  245.6 0.5 collective-permute-start.10
  246.1 1.5 collective-permute-start.14
  247.6 0.5 collective-permute-start.18
  248.2 10.7 %collective-permute-done.6 = f32[128,1024]{1,0:T(8,128)S(1)} collective-permute-done((f32[128,1024]{1,0:T(8,128)S(1)}, f32[128,1024]{1,0:T(8,128)S(1)}, u32[]{:S(2)}, u32[]{:S(2)}) %collective-permute-start.6) | collective-permute-done | bytes 524320 | tf_op jit(solution)/shard_map/ppermute | solution.py:308
  258.9 11.2 %collective-permute-done.10 = f32[128,1024]{1,0:T(8,128)S(1)} collective-permute-done((f32[128,1024]{1,0:T(8,128)S(1)}, f32[128,1024]{1,0:T(8,128)S(1)}, u32[]{:S(2)}, u32[]{:S(2)}) %collective-permute-start.10) | collective-permute-done | bytes 524320 | tf_op jit(solution)/shard_map/ppermute | solution.py:308
  270.1 11.2 %collective-permute-done.14 = f32[128,1024]{1,0:T(8,128)S(1)} collective-permute-done((f32[128,1024]{1,0:T(8,128)S(1)}, f32[128,1024]{1,0:T(8,128)S(1)}, u32[]{:S(2)}, u32[]{:S(2)}) %collective-permute-start.14) | collective-permute-done | bytes 524320 | tf_op jit(solution)/shard_map/ppermute | solution.py:308
  281.4 9.1 %collective-permute-done.18 = f32[128,1024]{1,0:T(8,128)S(1)} collective-permute-done((f32[128,1024]{1,0:T(8,128)S(1)}, f32[128,1024]{1,0:T(8,128)S(1)}, u32[]{:S(2)}, u32[]{:S(2)}) %collective-permute-start.18) | collective-permute-done | bytes 524320 | tf_op jit(solution)/shard_map/ppermute | solution.py:308
  290.4 0.6 add_add_fusion
  291.1 1.2 collective-permute-start.20
  292.3 0.8 collective-permute-start.16
  293.4 1.2 collective-permute-start.12
  294.6 11.4 %collective-permute-done.20 = f32[128,1024]{1,0:T(8,128)S(1)} collective-permute-done((f32[128,1024]{1,0:T(8,128)S(1)}, f32[128,1024]{1,0:T(8,128)S(1)}, u32[]{:S(2)}, u32[]{:S(2)}) %collective-permute-start.20) | collective-permute-done | bytes 524320 | tf_op jit(solution)/shard_map/ppermute | solution.py:310
  305.9 1.2 collective-permute-start.8
  307.1 10.0 %collective-permute-done.16 = f32[128,1024]{1,0:T(8,128)S(1)} collective-permute-done((f32[128,1024]{1,0:T(8,128)S(1)}, f32[128,1024]{1,0:T(8,128)S(1)}, u32[]{:S(2)}, u32[]{:S(2)}) %collective-permute-start.16) | collective-permute-done | bytes 524320 | tf_op jit(solution)/shard_map/ppermute | solution.py:310
  317.2 0.5 collective-permute-start.21
  317.7 10.7 %collective-permute-done.12 = f32[128,1024]{1,0:T(8,128)S(1)} collective-permute-done((f32[128,1024]{1,0:T(8,128)S(1)}, f32[128,1024]{1,0:T(8,128)S(1)}, u32[]{:S(2)}, u32[]{:S(2)}) %collective-permute-start.12) | collective-permute-done | bytes 524320 | tf_op jit(solution)/shard_map/ppermute | solution.py:310
  328.4 0.5 collective-permute-start.13
  328.9 7.7 %collective-permute-done.8 = f32[128,1024]{1,0:T(8,128)S(1)} collective-permute-done((f32[128,1024]{1,0:T(8,128)S(1)}, f32[128,1024]{1,0:T(8,128)S(1)}, u32[]{:S(2)}, u32[]{:S(2)}) %collective-permute-start.8) | collective-permute-done | bytes 524320 | tf_op jit(solution)/shard_map/ppermute | solution.py:310
  336.7 1.8 collective-permute-done.9
  338.6 0.8 copy-done.17
  339.3 5.8 %assemble_hidden.1 = bf16[4,128,4096]{2,1,0:T(8,128)(2,1)} custom-call(s32[1]{0:T(128)} %bitcast.sp_ref, f32[4,32,1024]{2,1,0:T(8,128)} %bitcast.62, f32[4,32,1024]{2,1,0:T(8,128)} %bitcast.70, f32[4,32,1024]{2,1,0:T(8,128)} %bitcast.69, f32[4,32,1024]{2,1,0:T(8,128)} %bitcast.74, f32[4,32,1024]{2,1,0:T(8,128)} %bitcast.61, f32[4,32,1024]{2,1,0:T(8,128)} %bitcast.68, ...), custom_call_target="tpu_custom_call" | custom-call | tf_op jit(solution)/shard_map/assemble_hidden/pallas_call | solution.py:222
  (69 shorter events, 1.8 us)
Async XLA Ops:
  4.2 0.7 copy-start
  4.8 0.7 copy-start.1
  89.5 4.8 %collective-permute-start.2 = (f32[64,64,128]{2,1,0:T(8,128)S(1)}, f32[64,64,128]{2,1,0:T(8,128)S(1)}, u32[]{:S(2)}, u32[]{:S(2)}) collective-permute-start(f32[64,64,128]{2,1,0:T(8,128)S(1)} %slice.73), channel_id=1, source_target_pairs={{0,1},{1,0},{2,3},{3,2},{4,5},{5,4},{6,7},{7,6}} | collective-permute-start | bytes 6291464 | tf_op jit(solution)/shard_map/ppermute | solution.py:285
  90.4 3.8 %collective-permute-start = (f32[64,128]{1,0:T(8,128)S(1)}, f32[64,128]{1,0:T(8,128)S(1)}, u32[]{:S(2)}, u32[]{:S(2)}) collective-permute-start(f32[64,128]{1,0:T(8,128)S(1)} %bitcast.76), channel_id=1, source_target_pairs={{0,1},{1,0},{2,3},{3,2},{4,5},{5,4},{6,7},{7,6}} | collective-permute-start | bytes 98312 | tf_op jit(solution)/shard_map/ppermute | solution.py:286
  95.6 27.0 %collective-permute-start.3 = (f32[32,64,128]{2,1,0:T(8,128)S(1)}, f32[32,64,128]{2,1,0:T(8,128)S(1)}, u32[]{:S(2)}, u32[]{:S(2)}) collective-permute-start(f32[32,64,128]{2,1,0:T(8,128)S(1)} %slice.93), channel_id=1, source_target_pairs={{0,2},{2,0},{1,3},{3,1},{4,6},{6,4},{5,7},{7,5}} | collective-permute-start | bytes 3145736 | tf_op jit(solution)/shard_map/ppermute | solution.py:289
  98.5 24.0 %collective-permute-start.1 = (f32[32,64]{1,0:T(8,128)S(1)}, f32[32,64]{1,0:T(8,128)S(1)}, u32[]{:S(2)}, u32[]{:S(2)}) collective-permute-start(f32[32,64]{1,0:T(8,128)S(1)} %slice.91), channel_id=1, source_target_pairs={{0,2},{2,0},{1,3},{3,1},{4,6},{6,4},{5,7},{7,5}} | collective-permute-start | bytes 24584 | tf_op jit(solution)/shard_map/ppermute | solution.py:289
  98.5 24.1 %collective-permute-start.4 = (f32[32,64]{1,0:T(8,128)S(1)}, f32[32,64]{1,0:T(8,128)S(1)}, u32[]{:S(2)}, u32[]{:S(2)}) collective-permute-start(f32[32,64]{1,0:T(8,128)S(1)} %slice.97), channel_id=1, source_target_pairs={{0,2},{2,0},{1,3},{3,1},{4,6},{6,4},{5,7},{7,5}} | collective-permute-start | bytes 24584 | tf_op jit(solution)/shard_map/ppermute | solution.py:289
  124.1 10.0 %copy-start.18 = (bf16[4096]{0:T(1024)(128)(2,1)S(1)}, bf16[4096]{0:T(1024)(128)(2,1)}, u32[]{:S(2)}) copy-start(bf16[4096]{0:T(1024)(128)(2,1)} %param.27) | copy-start | bytes 24580
  132.3 47.1 %collective-permute-start.5 = (f32[128,4096]{1,0:T(8,128)S(1)}, f32[128,4096]{1,0:T(8,128)}, u32[]{:S(2)}, u32[]{:S(2)}) collective-permute-start(f32[128,4096]{1,0:T(8,128)S(1)} %fusion.29), channel_id=1, source_target_pairs={{0,4},{4,0},{1,5},{5,1},{2,6},{6,2},{3,7},{7,3}} | collective-permute-start | bytes 6291464 | tf_op jit(solution)/shard_map/ppermute | solution.py:296
  244.1 14.8 %collective-permute-start.6 = (f32[128,1024]{1,0:T(8,128)S(1)}, f32[128,1024]{1,0:T(8,128)S(1)}, u32[]{:S(2)}, u32[]{:S(2)}) collective-permute-start(f32[128,1024]{1,0:T(8,128)S(1)} %fusion.6), channel_id=1, source_target_pairs={{0,4},{4,0},{1,5},{5,1},{2,6},{6,2},{3,7},{7,3}} | collective-permute-start | bytes 1572872 | tf_op jit(solution)/shard_map/ppermute | solution.py:308
  245.6 24.5 %collective-permute-start.10 = (f32[128,1024]{1,0:T(8,128)S(1)}, f32[128,1024]{1,0:T(8,128)S(1)}, u32[]{:S(2)}, u32[]{:S(2)}) collective-permute-start(f32[128,1024]{1,0:T(8,128)S(1)} %fusion.4), channel_id=1, source_target_pairs={{0,4},{4,0},{1,5},{5,1},{2,6},{6,2},{3,7},{7,3}} | collective-permute-start | bytes 1572872 | tf_op jit(solution)/shard_map/ppermute | solution.py:308
  246.1 35.2 %collective-permute-start.14 = (f32[128,1024]{1,0:T(8,128)S(1)}, f32[128,1024]{1,0:T(8,128)S(1)}, u32[]{:S(2)}, u32[]{:S(2)}) collective-permute-start(f32[128,1024]{1,0:T(8,128)S(1)} %fusion.2), channel_id=1, source_target_pairs={{0,4},{4,0},{1,5},{5,1},{2,6},{6,2},{3,7},{7,3}} | collective-permute-start | bytes 1572872 | tf_op jit(solution)/shard_map/ppermute | solution.py:308
  247.6 42.8 %collective-permute-start.18 = (f32[128,1024]{1,0:T(8,128)S(1)}, f32[128,1024]{1,0:T(8,128)S(1)}, u32[]{:S(2)}, u32[]{:S(2)}) collective-permute-start(f32[128,1024]{1,0:T(8,128)S(1)} %fusion), channel_id=1, source_target_pairs={{0,4},{4,0},{1,5},{5,1},{2,6},{6,2},{3,7},{7,3}} | collective-permute-start | bytes 1572872 | tf_op jit(solution)/shard_map/ppermute | solution.py:308
  291.1 48.3 %copy-start.2 = (f32[128,1024]{1,0:T(8,128)}, f32[128,1024]{1,0:T(8,128)S(1)}, u32[]{:S(2)}) copy-start(f32[128,1024]{1,0:T(8,128)S(1)} %get-tuple-element.26) | copy-start | bytes 1572868
  291.1 48.3 %copy-start.3 = (f32[128,1024]{1,0:T(8,128)}, f32[128,1024]{1,0:T(8,128)S(1)}, u32[]{:S(2)}) copy-start(f32[128,1024]{1,0:T(8,128)S(1)} %get-tuple-element.27) | copy-start | bytes 1572868
  291.1 48.2 %copy-start.4 = (f32[128,1024]{1,0:T(8,128)}, f32[128,1024]{1,0:T(8,128)S(1)}, u32[]{:S(2)}) copy-start(f32[128,1024]{1,0:T(8,128)S(1)} %get-tuple-element.28) | copy-start | bytes 1572868
  291.1 48.2 %copy-start.5 = (f32[128,1024]{1,0:T(8,128)}, f32[128,1024]{1,0:T(8,128)S(1)}, u32[]{:S(2)}) copy-start(f32[128,1024]{1,0:T(8,128)S(1)} %get-tuple-element.29) | copy-start | bytes 1572868
  291.1 14.8 %collective-permute-start.20 = (f32[128,1024]{1,0:T(8,128)S(1)}, f32[128,1024]{1,0:T(8,128)S(1)}, u32[]{:S(2)}, u32[]{:S(2)}) collective-permute-start(f32[128,1024]{1,0:T(8,128)S(1)} %get-tuple-element.26), channel_id=1, source_target_pairs={{0,2},{2,0},{1,3},{3,1},{4,6},{6,4},{5,7},{7,5}} | collective-permute-start | bytes 1572872 | tf_op jit(solution)/shard_map/ppermute | solution.py:310
  292.3 13.6 %collective-permute-start.19 = (f32[128,1024]{1,0:T(8,128)S(1)}, f32[128,1024]{1,0:T(8,128)S(1)}, u32[]{:S(2)}, u32[]{:S(2)}) collective-permute-start(f32[128,1024]{1,0:T(8,128)S(1)} %get-tuple-element.26), channel_id=1, source_target_pairs={{0,1},{1,0},{2,3},{3,2},{4,5},{5,4},{6,7},{7,6}} | collective-permute-start | bytes 1572872 | tf_op jit(solution)/shard_map/ppermute | solution.py:309
  292.3 24.8 %collective-permute-start.16 = (f32[128,1024]{1,0:T(8,128)S(1)}, f32[128,1024]{1,0:T(8,128)S(1)}, u32[]{:S(2)}, u32[]{:S(2)}) collective-permute-start(f32[128,1024]{1,0:T(8,128)S(1)} %get-tuple-element.27), channel_id=1, source_target_pairs={{0,2},{2,0},{1,3},{3,1},{4,6},{6,4},{5,7},{7,5}} | collective-permute-start | bytes 1572872 | tf_op jit(solution)/shard_map/ppermute | solution.py:310
  293.1 24.0 %collective-permute-start.15 = (f32[128,1024]{1,0:T(8,128)S(1)}, f32[128,1024]{1,0:T(8,128)S(1)}, u32[]{:S(2)}, u32[]{:S(2)}) collective-permute-start(f32[128,1024]{1,0:T(8,128)S(1)} %get-tuple-element.27), channel_id=1, source_target_pairs={{0,1},{1,0},{2,3},{3,2},{4,5},{5,4},{6,7},{7,6}} | collective-permute-start | bytes 1572872 | tf_op jit(solution)/shard_map/ppermute | solution.py:309
  293.4 35.0 %collective-permute-start.12 = (f32[128,1024]{1,0:T(8,128)S(1)}, f32[128,1024]{1,0:T(8,128)S(1)}, u32[]{:S(2)}, u32[]{:S(2)}) collective-permute-start(f32[128,1024]{1,0:T(8,128)S(1)} %get-tuple-element.28), channel_id=1, source_target_pairs={{0,2},{2,0},{1,3},{3,1},{4,6},{6,4},{5,7},{7,5}} | collective-permute-start | bytes 1572872 | tf_op jit(solution)/shard_map/ppermute | solution.py:310
  305.9 33.4 %copy-start.6 = (f32[128,1024]{1,0:T(8,128)}, f32[128,1024]{1,0:T(8,128)S(1)}, u32[]{:S(2)}) copy-start(f32[128,1024]{1,0:T(8,128)S(1)} %collective-permute-done.20) | copy-start | bytes 1572868
  305.9 22.5 %collective-permute-start.11 = (f32[128,1024]{1,0:T(8,128)S(1)}, f32[128,1024]{1,0:T(8,128)S(1)}, u32[]{:S(2)}, u32[]{:S(2)}) collective-permute-start(f32[128,1024]{1,0:T(8,128)S(1)} %get-tuple-element.28), channel_id=1, source_target_pairs={{0,1},{1,0},{2,3},{3,2},{4,5},{5,4},{6,7},{7,6}} | collective-permute-start | bytes 1572872 | tf_op jit(solution)/shard_map/ppermute | solution.py:309
  305.9 33.4 %copy-start.7 = (f32[128,1024]{1,0:T(8,128)}, f32[128,1024]{1,0:T(8,128)S(1)}, u32[]{:S(2)}) copy-start(f32[128,1024]{1,0:T(8,128)S(1)} %collective-permute-done.19) | copy-start | bytes 1572868
  305.9 30.7 %collective-permute-start.8 = (f32[128,1024]{1,0:T(8,128)S(1)}, f32[128,1024]{1,0:T(8,128)S(1)}, u32[]{:S(2)}, u32[]{:S(2)}) collective-permute-start(f32[128,1024]{1,0:T(8,128)S(1)} %get-tuple-element.29), channel_id=1, source_target_pairs={{0,2},{2,0},{1,3},{3,1},{4,6},{6,4},{5,7},{7,5}} | collective-permute-start | bytes 1572872 | tf_op jit(solution)/shard_map/ppermute | solution.py:310
  317.1 19.5 %copy-start.8 = (f32[128,1024]{1,0:T(8,128)}, f32[128,1024]{1,0:T(8,128)S(1)}, u32[]{:S(2)}) copy-start(f32[128,1024]{1,0:T(8,128)S(1)} %collective-permute-done.16) | copy-start | bytes 1572868
  317.2 19.5 %collective-permute-start.7 = (f32[128,1024]{1,0:T(8,128)S(1)}, f32[128,1024]{1,0:T(8,128)S(1)}, u32[]{:S(2)}, u32[]{:S(2)}) collective-permute-start(f32[128,1024]{1,0:T(8,128)S(1)} %get-tuple-element.29), channel_id=1, source_target_pairs={{0,1},{1,0},{2,3},{3,2},{4,5},{5,4},{6,7},{7,6}} | collective-permute-start | bytes 1572872 | tf_op jit(solution)/shard_map/ppermute | solution.py:309
  317.2 19.5 %copy-start.9 = (f32[128,1024]{1,0:T(8,128)}, f32[128,1024]{1,0:T(8,128)S(1)}, u32[]{:S(2)}) copy-start(f32[128,1024]{1,0:T(8,128)S(1)} %collective-permute-done.15) | copy-start | bytes 1572868
  317.2 19.5 %collective-permute-start.21 = (f32[128,1024]{1,0:T(8,128)S(1)}, f32[128,1024]{1,0:T(8,128)S(1)}, u32[]{:S(2)}, u32[]{:S(2)}) collective-permute-start(f32[128,1024]{1,0:T(8,128)S(1)} %collective-permute-done.20), channel_id=1, source_target_pairs={{0,1},{1,0},{2,3},{3,2},{4,5},{5,4},{6,7},{7,6}} | collective-permute-start | bytes 1572872 | tf_op jit(solution)/shard_map/ppermute | solution.py:311
  328.4 8.3 %copy-start.10 = (f32[128,1024]{1,0:T(8,128)}, f32[128,1024]{1,0:T(8,128)S(1)}, u32[]{:S(2)}) copy-start(f32[128,1024]{1,0:T(8,128)S(1)} %collective-permute-done.12) | copy-start | bytes 1572868
  328.4 8.3 %collective-permute-start.17 = (f32[128,1024]{1,0:T(8,128)S(1)}, f32[128,1024]{1,0:T(8,128)S(1)}, u32[]{:S(2)}, u32[]{:S(2)}) collective-permute-start(f32[128,1024]{1,0:T(8,128)S(1)} %collective-permute-done.16), channel_id=1, source_target_pairs={{0,1},{1,0},{2,3},{3,2},{4,5},{5,4},{6,7},{7,6}} | collective-permute-start | bytes 1572872 | tf_op jit(solution)/shard_map/ppermute | solution.py:311
  328.4 10.1 %copy-start.11 = (f32[128,1024]{1,0:T(8,128)}, f32[128,1024]{1,0:T(8,128)S(1)}, u32[]{:S(2)}) copy-start(f32[128,1024]{1,0:T(8,128)S(1)} %collective-permute-done.11) | copy-start | bytes 1572868
  328.4 8.3 %collective-permute-start.13 = (f32[128,1024]{1,0:T(8,128)S(1)}, f32[128,1024]{1,0:T(8,128)S(1)}, u32[]{:S(2)}, u32[]{:S(2)}) collective-permute-start(f32[128,1024]{1,0:T(8,128)S(1)} %collective-permute-done.12), channel_id=1, source_target_pairs={{0,1},{1,0},{2,3},{3,2},{4,5},{5,4},{6,7},{7,6}} | collective-permute-start | bytes 1572872 | tf_op jit(solution)/shard_map/ppermute | solution.py:311
  336.6 1.9 copy-start.12
  336.6 1.9 collective-permute-start.9
  336.6 1.9 copy-start.13
  336.6 1.9 copy-start.14
  336.7 1.9 copy-start.15
  336.7 1.8 copy-start.16
  338.5 0.8 copy-start.17

commit v3 on v2

--- a/solution.py
+++ b/solution.py
@@ -206,40 +206,282 @@
     )(order, rel, q, k_new, v_new, k_cache, v_cache)
 
 
-def assemble_kernel(own, cw, sp_ref, *refs):
-    out_ref = refs[-1]
-    sp = sp_ref[0]
-    for c in range(len(refs) // 4):
-        for flip in range(4):
-            start = pl.multiple_of((sp ^ flip) * own, own)
-            out_ref[0, pl.ds(start, own), c * cw:(c + 1) * cw] = refs[c * 4 + flip][0].astype(out_ref.dtype)
-
-
-def assemble(sp, pieces):
-    n_steps, own, cw = pieces[0][0].shape
-    n_chunks = len(pieces)
-    piece_blk = pl.BlockSpec((1, own, cw), lambda i, sp: (i, 0, 0))
+def tail_kernel(dims, o_ref, ml_ref, x_ref, gain_ref, wo_hbm, wg_hbm, wu_hbm, wd_hbm, out_ref,
+                ring, near1, nml, far1, fml, wts, comb, attn, part_o, recv_o, res, mid, act, part_d, recv_d, fin, across, near, diag,
+                ring_sem, n1s, n1r, nms, nmr, f1s, f1r, fms, fmr, os_, or_, ds_, dr_, xs_, xr_, cs_, cr_, gs_, gr_):
+    n_steps, heads, hd, n_chunks, exp_scale, n_slots = dims
+    rows_q = n_steps * heads
+    own = far1.shape[0]
+    per = own // n_chunks
+    tok = per * n_steps
+    width = x_ref.shape[1]
+    kt, nt = ring.shape[1], ring.shape[2]
+    n_o = width // nt
+    n_up = act.shape[1] // nt
+    k_up, k_dn = width // kt, act.shape[1] // kt
+    n_dn = width // nt
+    first_up = n_o
+    first_dn = n_o + 2 * k_up * n_up
+    n_loads = first_dn + k_dn * n_dn
+
+    sp = lax.axis_index('sp')
+    tp = lax.axis_index('tp')
+    sp_core = sp + 1 - 2 * lax.rem(sp, 2)
+    sp_chip = lax.rem(sp + 2, 4)
+    sp_diag = lax.rem(sp_core + 2, 4)
+    to_core = {'sp': sp_core}
+    to_chip = {'sp': sp_chip}
+    to_tp = {'tp': 1 - tp}
+
+    def send(src, dst, s_sem, r_sem, dev):
+        return pltpu.make_async_remote_copy(src_ref=src, dst_ref=dst, send_sem=s_sem, recv_sem=r_sem, device_id=dev,
+                                            device_id_type=pl.DeviceIdType.MESH)
+
+    barrier = pltpu.get_barrier_semaphore()
+    for dev in (to_core, to_chip, to_tp):
+        pl.semaphore_signal(barrier, inc=1, device_id=dev, device_id_type=pl.DeviceIdType.MESH)
+    pl.semaphore_wait(barrier, 3)
+
+    near_ml = send(ml_ref.at[pl.ds(0, 2 * own)], nml, nms.at[0], nmr.at[0], to_core)
+    near_ml.start()
+    near_o = []
+    for piece in (0, 1):
+        for j in range(n_chunks):
+            rows = pl.ds(piece * own + j * per, per)
+            near_o.append(send(o_ref.at[rows], near1.at[rows], n1s.at[piece * n_chunks + j], n1r.at[piece * n_chunks + j], to_core))
+    for copy in near_o:
+        copy.start()
+
+    def load(src, row, col, slot):
+        return pltpu.make_async_copy(src.at[pl.ds(pl.multiple_of(row * kt, kt), kt), pl.ds(pl.multiple_of(col * nt, nt), nt)],
+                                     ring.at[slot], ring_sem.at[slot])
+
+    def start(idx):
+        slot = lax.rem(idx, n_slots)
+
+        @pl.when(idx < first_up)
+        def _():
+            load(wo_hbm, 0, idx, slot).start()
+
+        up = idx - first_up
+        sub = lax.rem(up + 2 * k_up, 2 * k_up)
+        col = (up - sub) // (2 * k_up)
+
+        @pl.when((idx >= first_up) & (idx < first_dn) & (sub < k_up))
+        def _():
+            load(wg_hbm, sub, col, slot).start()
+
+        @pl.when((idx >= first_up) & (idx < first_dn) & (sub >= k_up))
+        def _():
+            load(wu_hbm, sub - k_up, col, slot).start()
+
+        dn = idx - first_dn
+        dsub = lax.rem(dn, k_dn)
+
+        @pl.when((idx >= first_dn) & (idx < n_loads))
+        def _():
+            load(wd_hbm, dsub, (dn - dsub) // k_dn, slot).start()
+
+    def arrived(idx):
+        slot = lax.rem(idx, n_slots)
+        load(wo_hbm, 0, 0, slot).wait()
+        return slot
+
+    def start_many(lo, hi):
+        def one(i, carry):
+            start(i)
+            return carry
+        lax.fori_loop(lo, hi, one, 0)
+
+    start_many(0, n_slots)
+
+    diag_mask = lax.broadcasted_iota(jnp.int32, (rows_q, 2 * rows_q), 0) == lax.broadcasted_iota(jnp.int32, (rows_q, 2 * rows_q), 1)
+    left = lax.broadcasted_iota(jnp.int32, (per, 2 * rows_q), 1) < rows_q
+
+    def column(row):
+        return jnp.sum(jnp.where(diag_mask, row, 0.0), axis=1, keepdims=True)
+
+    def weights(stat_a, stat_b):
+        top = jnp.maximum(stat_a, stat_b)
+        wt_a = jnp.exp2((stat_a - top) * exp_scale)
+        wt_b = jnp.exp2((stat_b - top) * exp_scale)
+        total = pltpu.roll(wt_a, rows_q, 1) * stat_a + pltpu.roll(wt_b, rows_q, 1) * stat_b
+        return wt_a, wt_b, jnp.where(left, top, total)
+
+    def merge_near(piece, j):
+        base = piece * own + j * per
+        near_o[piece * n_chunks + j].wait_recv()
+        wt_a, wt_b, stat = weights(nml[base:base + per, :], ml_ref[2 * own + base:2 * own + base + per, :])
+        wts[0] = wt_a
+        wts[1] = wt_b
+        nml[base:base + per, :] = stat
+
+        def one(i, carry):
+            near1[base + i] = column(wts[0, pl.ds(i, 1), :]) * near1[base + i] + column(wts[1, pl.ds(i, 1), :]) * o_ref[2 * own + base + i]
+            return carry
+        lax.fori_loop(0, per, one, 0)
+
+    near_ml.wait_recv()
+    far_o, far_ml = [], []
+    for j in range(n_chunks):
+        rows = pl.ds(j * per, per)
+        merge_near(0, j)
+        far_ml.append(send(nml.at[rows], fml.at[rows], fms.at[j], fmr.at[j], to_chip))
+        far_o.append(send(near1.at[rows], far1.at[rows], f1s.at[j], f1r.at[j], to_chip))
+        far_ml[j].start()
+        far_o[j].start()
+    for j in range(n_chunks):
+        merge_near(1, j)
+
+    tp_o = []
+    for j in range(n_chunks):
+        base = j * per
+        far_ml[j].wait_recv()
+        far_o[j].wait_recv()
+        wt_a, wt_b, stat = weights(nml[own + base:own + base + per, :], fml[base:base + per, :])
+        inv = pltpu.roll(1.0 / stat, rows_q, 1)
+        wts[0] = wt_a * inv
+        wts[1] = wt_b * inv
+
+        def one(i, carry, base=base):
+            rows = pl.ds(pl.multiple_of(i * rows_q, rows_q), rows_q)
+            comb[rows, :] = column(wts[0, pl.ds(i, 1), :]) * near1[own + base + i] + column(wts[1, pl.ds(i, 1), :]) * far1[base + i]
+            return carry
+        lax.fori_loop(0, per, one, 0)
+        for step in range(n_steps):
+            for h in range(heads):
+                attn[step * per:(step + 1) * per, h * hd:(h + 1) * hd] = comb[pl.ds(step * heads + h, per, stride=rows_q), :]
+        attn_in = attn[...].astype(jnp.bfloat16)
+
+        def o_tile(n, carry, j=j, attn_in=attn_in):
+            if j == 0:
+                arrived(n)
+            part_o[j, :, pl.ds(pl.multiple_of(n * nt, nt), nt)] = jnp.dot(attn_in, ring[n], preferred_element_type=jnp.float32)
+            return carry
+        lax.fori_loop(0, n_o, o_tile, 0)
+        tp_o.append(send(part_o.at[j], recv_o.at[j], os_.at[j], or_.at[j], to_tp))
+        tp_o[j].start()
+    start_many(n_slots, n_slots + n_o)
+
+    half = 16
+    for j in range(n_chunks):
+        tp_o[j].wait_recv()
+
+        def norm_rows(i, carry, j=j):
+            sub = pl.ds(pl.multiple_of(i * half, half), half)
+            rows = pl.ds(pl.multiple_of(j * tok + i * half, half), half)
+            summed = x_ref[rows, :].astype(jnp.float32) + (part_o[j, sub, :] + recv_o[j, sub, :])
+            resid = summed.astype(jnp.bfloat16)
+            res[rows, :] = resid
+            wide = resid.astype(jnp.float32)
+            inv = lax.rsqrt(jnp.mean(wide * wide, axis=-1, keepdims=True) + NORM_EPS)
+            mid[rows, :] = (wide * inv * gain_ref[...].astype(jnp.float32)).astype(jnp.bfloat16)
+            return carry
+        lax.fori_loop(0, tok // half, norm_rows, 0)
+
+    def up_tile(t, carry):
+        idx = first_up + 2 * k_up * t
+        total = []
+        for side in (0, 1):
+            acc = None
+            for k in range(k_up):
+                slot = arrived(idx + side * k_up + k)
+                prod = jnp.dot(mid[:, k * kt:(k + 1) * kt], ring[slot], preferred_element_type=jnp.float32)
+                acc = prod if acc is None else acc + prod
+            total.append(acc)
+        gate, up = total
+        act[:, pl.ds(pl.multiple_of(t * nt, nt), nt)] = (jax.nn.silu(gate) * up).astype(jnp.bfloat16)
+        for k in range(2 * k_up):
+            start(idx + k + n_slots)
+        return carry
+
+    lax.fori_loop(0, n_up, up_tile, 0)
+
+    tp_d, chip_d, core_d, diag_d = [], [], [], []
+    for t in range(n_dn):
+        tp_d.append(send(part_d.at[t], recv_d.at[t], ds_.at[t], dr_.at[t], to_tp))
+        chip_d.append(send(fin.at[t], across.at[t], xs_.at[t], xr_.at[t], to_chip))
+        core_d.append(send(fin.at[t], near.at[t], cs_.at[t], cr_.at[t], to_core))
+        diag_d.append(send(across.at[t], diag.at[t], gs_.at[t], gr_.at[t], to_core))
+
+    n_tok = res.shape[0]
+
+    def emit(who, t, value):
+        rows = pl.ds(pl.multiple_of(who * n_tok, n_tok), n_tok)
+        out_ref[rows, t * nt:(t + 1) * nt] = value.astype(out_ref.dtype)
+
+    def down(t):
+        acc = None
+        for k in range(k_dn):
+            slot = arrived(first_dn + k_dn * t + k)
+            prod = jnp.dot(act[:, k * kt:(k + 1) * kt], ring[slot], preferred_element_type=jnp.float32)
+            acc = prod if acc is None else acc + prod
+        part_d[t] = acc
+        tp_d[t].start()
+        for k in range(k_dn):
+            start(jnp.int32(first_dn + k_dn * t + k + n_slots))
+
+    def finish(t):
+        tp_d[t].wait_recv()
+        fin[t] = res[:, t * nt:(t + 1) * nt].astype(jnp.float32) + (part_d[t] + recv_d[t])
+        chip_d[t].start()
+        core_d[t].start()
+        emit(sp, t, fin[t])
+
+    def forward(t):
+        chip_d[t].wait_recv()
+        diag_d[t].start()
+        emit(sp_chip, t, across[t])
+        core_d[t].wait_recv()
+        emit(sp_core, t, near[t])
+
+    for t in range(n_dn):
+        down(t)
+        if t == 5:
+            finish(0)
+    for t in range(1, n_dn):
+        finish(t)
+        forward(t - 1)
+    forward(n_dn - 1)
+    for t in range(n_dn):
+        diag_d[t].wait_recv()
+        emit(sp_diag, t, diag[t])
+    for copy in near_o + [near_ml] + far_o + far_ml + tp_o + tp_d + chip_d + core_d + diag_d:
+        copy.wait_send()
+
+
+def finish_layer(o_part, ml, x_own, norm, w_o, w_gate, w_up, w_down, n_steps, heads, exp_scale):
+    n_batch, rows_q, hd = o_part.shape
+    tokens, width = x_own.shape
+    own = tokens // n_steps
+    inner = w_gate.shape[1]
+    n_chunks, n_slots, kt, nt = 4, 12, 2048, 512
+    per = own // n_chunks
+    n_dn = width // nt
+    vmem = pl.BlockSpec(memory_space=pltpu.VMEM)
+    hbm = pl.BlockSpec(memory_space=pl.ANY)
+    f32, bf16 = jnp.float32, jnp.bfloat16
+    tiles = pltpu.VMEM((n_dn, tokens, nt), f32)
+    dma = pltpu.SemaphoreType.DMA
     return pl.pallas_call(
-        functools.partial(assemble_kernel, own, cw),
-        grid_spec=pltpu.PrefetchScalarGridSpec(
-            num_scalar_prefetch=1,
-            grid=(n_steps,),
-            in_specs=[piece_blk] * (4 * n_chunks),
-            out_specs=pl.BlockSpec((1, 4 * own, cw * n_chunks), lambda i, sp: (i, 0, 0)),
-        ),
-        out_shape=jax.ShapeDtypeStruct((n_steps, 4 * own, cw * n_chunks), jnp.bfloat16),
-        compiler_params=pltpu.CompilerParams(dimension_semantics=("arbitrary",)),
-        name="assemble_hidden",
-    )(sp.reshape(1), *[piece for chunk in pieces for piece in chunk])
-
-
-def merge(mine, other, exp_scale):
-    out_a, max_a, sum_a = mine
-    out_b, max_b, sum_b = other
-    top = jnp.maximum(max_a, max_b)
-    wt_a = jnp.exp2((max_a - top) * exp_scale)
-    wt_b = jnp.exp2((max_b - top) * exp_scale)
-    return wt_a[..., None] * out_a + wt_b[..., None] * out_b, top, wt_a * sum_a + wt_b * sum_b
+        functools.partial(tail_kernel, (n_steps, heads, hd, n_chunks, exp_scale, n_slots)),
+        in_specs=[vmem] * 4 + [hbm] * 4,
+        out_specs=vmem,
+        out_shape=jax.ShapeDtypeStruct((4 * tokens, width), bf16),
+        scratch_shapes=[pltpu.VMEM((n_slots, kt, nt), bf16),
+                        pltpu.VMEM((2 * own, rows_q, hd), f32), pltpu.VMEM((2 * own, 2 * rows_q), f32),
+                        pltpu.VMEM((own, rows_q, hd), f32), pltpu.VMEM((own, 2 * rows_q), f32),
+                        pltpu.VMEM((2, per, 2 * rows_q), f32), pltpu.VMEM((per * rows_q, hd), f32),
+                        pltpu.VMEM((per * n_steps, heads * hd), f32),
+                        pltpu.VMEM((n_chunks, per * n_steps, width), f32), pltpu.VMEM((n_chunks, per * n_steps, width), f32),
+                        pltpu.VMEM((tokens, width), bf16), pltpu.VMEM((tokens, width), bf16), pltpu.VMEM((tokens, inner), bf16),
+                        tiles, tiles, tiles, tiles, tiles, tiles,
+                        dma((n_slots,)), dma((2 * n_chunks,)), dma((2 * n_chunks,)), dma((1,)), dma((1,)),
+                        dma((n_chunks,)), dma((n_chunks,)), dma((n_chunks,)), dma((n_chunks,)), dma((n_chunks,)), dma((n_chunks,)),
+                        dma((n_dn,)), dma((n_dn,)), dma((n_dn,)), dma((n_dn,)), dma((n_dn,)), dma((n_dn,)), dma((n_dn,)), dma((n_dn,))],
+        compiler_params=pltpu.CompilerParams(collective_id=0, has_side_effects=True, vmem_limit_bytes=63 * 2**20),
+        name="finish_layer",
+    )(o_part, ml, x_own, norm.reshape(1, width), w_o, w_gate, w_up, w_down)
 
 
 def solution(mesh):
@@ -249,9 +491,6 @@
     in_specs = (P(None, 'dp', None), P('dp'), cache_spec, cache_spec, col_spec, col_spec, col_spec, row_spec,
                 col_spec, col_spec, row_spec, P(), P(), P(), P())
     out_specs = (P(None, 'dp', None), cache_spec, cache_spec)
-    core_perm = [(0, 1), (1, 0), (2, 3), (3, 2)]
-    chip_perm = [(0, 2), (2, 0), (1, 3), (3, 1)]
-    tp_perm = [(0, 1), (1, 0)]
 
     def shard_body(hidden, start_pos, k_cache, v_cache, w_q, w_k, w_v, w_o, w_gate, w_up, w_down, attn_norm, mlp_norm, q_gain, k_gain):
         n_steps, n_batch, width = hidden.shape
@@ -280,37 +519,13 @@
         k_out, v_out, o_part, ml = attention(order, rel, q_rot, k_rows, v_rows, k_cache.reshape(flat), v_cache.reshape(flat),
                                              kv_heads, exp_scale, n_req)
 
-        half = n_batch // 2
-        ml = ml.reshape(n_batch, 2 * rows_q)
-        o_recv = lax.ppermute(o_part[:half], 'sp', core_perm)
-        ml_recv = lax.ppermute(ml[:half], 'sp', core_perm)
-        both = merge((o_part[half:], ml[half:, :rows_q], ml[half:, rows_q:]),
-                     (o_recv, ml_recv[:, :rows_q], ml_recv[:, rows_q:]), exp_scale)
-        far = [lax.ppermute(part_[:own], 'sp', chip_perm) for part_ in both]
-        o_sum, _, l_sum = merge([part_[own:] for part_ in both], far, exp_scale)
-        attn_in = (o_sum / l_sum[..., None]).astype(jnp.bfloat16).reshape(own, n_steps, heads * hd)
-        attn_in = attn_in.transpose(1, 0, 2).reshape(n_steps * own, heads * hd)
-
-        x_own = lax.dynamic_slice_in_dim(hidden, sp * own, own, axis=1).reshape(n_steps * own, width)
-        o_mine = jnp.dot(attn_in, w_o, preferred_element_type=jnp.float32)
-        attn_out = o_mine + lax.ppermute(o_mine, 'tp', tp_perm)
-        residual = (x_own.astype(jnp.float32) + attn_out).astype(jnp.bfloat16)
-        mlp_in = rms_scale(residual, mlp_norm).astype(jnp.bfloat16)
-        gate_act = jnp.dot(mlp_in, w_gate, preferred_element_type=jnp.float32)
-        up_proj = jnp.dot(mlp_in, w_up, preferred_element_type=jnp.float32)
-        mlp_act = (jax.nn.silu(gate_act) * up_proj).astype(jnp.bfloat16)
         n_chunks = 4
-        cw = width // n_chunks
-        pieces = []
-        for c in range(n_chunks):
-            sl = slice(c * cw, (c + 1) * cw)
-            mine = jnp.dot(mlp_act, w_down[:, sl], preferred_element_type=jnp.float32)
-            mine = residual[:, sl].astype(jnp.float32) + (mine + lax.ppermute(mine, 'tp', tp_perm))
-            near = lax.ppermute(mine, 'sp', core_perm)
-            across = lax.ppermute(mine, 'sp', chip_perm)
-            diag = lax.ppermute(across, 'sp', core_perm)
-            pieces.append([piece.reshape(n_steps, own, cw) for piece in (mine, near, across, diag)])
-        hid_out = assemble(sp, pieces)
+        per_chunk = own // n_chunks
+        x_own = lax.dynamic_slice_in_dim(hidden, sp * own, own, axis=1).reshape(n_steps, n_chunks, per_chunk, width)
+        x_own = x_own.transpose(1, 0, 2, 3).reshape(n_steps * own, width)
+        flat_out = finish_layer(o_part, ml.reshape(n_batch, 2 * rows_q), x_own, mlp_norm, w_o, w_gate, w_up, w_down,
+                                n_steps, heads, exp_scale)
+        hid_out = flat_out.reshape(4 * n_chunks, n_steps, per_chunk, width).transpose(1, 0, 2, 3).reshape(n_steps, n_batch, width)
         return hid_out, k_out.reshape(k_cache.shape), v_out.reshape(v_cache.shape)
 
     return jax.shard_map(shard_body, mesh=mesh, in_specs=in_specs, out_specs=out_specs, check_vma=False)

time: 347 us -> 258 us (0.74)
  waiting for transfers between devices: 154 us -> 0 us
  Pallas kernels: 89.6 us -> 240 us
  matrix products: 70.7 us -> 0 us
  starting transfers between devices: 17.4 us -> 0 us
  local copies, waits for them, and re-layouts: 4.87 us -> 14.6 us
  other arithmetic: 7.71 us -> 2.03 us
    ppermute x22 -> x0, waiting for transfers between devices: 154 us -> none  [the longest x1 44 us: shard_body(): attn_out = o_mine + lax.ppermute(o_mine, 'tp', tp_perm)]
    pallas_call x1, Pallas kernels: 5.78 us -> 156 us  [finish_layer(): pl.pallas_call(functools.partial(tail_kernel, (n_steps, heads, hd, n_chun...]
    dot_general x7 -> x0, matrix products: 70.7 us -> none  [the longest x4 22.9 us: shard_body(): mine = jnp.dot(mlp_act, w_down[:, sl], preferred_element_type=jnp.float32)]
    ppermute x22 -> x0, starting transfers between devices: 17.4 us -> none  [the longest x3 4.88 us: shard_body(): far = [lax.ppermute(part_[:own], 'sp', chip_perm) for part_ in both]]
    transpose x0 -> x3, local copies, waits for them, and re-layouts: none -> 7.03 us  [the longest x1 4.7 us: shard_body(): flat_out.reshape(4 * n_chunks, n_steps, per_chunk, width)]
    unnamed x38 -> x16, local copies, waits for them, and re-layouts: 2.13 us -> 6.13 us
  transfers between devices with their start and end apart: 22 -> 0, of which waited for: 13 -> 0; matrix products, arithmetic and copies ran while one was open for 0% -> 0% of each run, Pallas kernels for 0% -> 0%
where the time goes in v3:
time: 258 us; the launch traced here: 257 us
  Pallas kernels  240 us (93%)
  local copies, waits for them, and re-layouts  14.6 us (6%)
    pallas_call x1, Pallas kernels, finish_layer(): pl.pallas_call(functools.partial(tail_kernel, (n_steps, heads, hd, n_chun...  156 us
    pallas_call x1, Pallas kernels, attention(): pl.pallas_call(functools.partial(attn_kernel, dims), grid_spec=pltpu.Pref...  56.1 us
    pallas_call x1, Pallas kernels, project_qkv(): pl.pallas_call(functools.partial(qkv_kernel, (heads, kv_heads, hd, unit,...  27.7 us
    unnamed x16, local copies, waits for them, and re-layouts  6.13 us

profile of v3, /device:TPU:0, one launch (start us, length us, event | category | flops | bytes accessed | tf_op | source)
XLA Modules:
  0.0 256.9 jit_solution(11769427732918993318)
XLA Ops:
  0.7 0.1 add_multiply_fusion
  0.7 0.1 iota_add_fusion
  0.8 0.1 add.64.order_ref
  0.9 0.7 convert_bitcast_fusion
  1.6 1.0 fusion
  2.6 0.2 pad_maximum_fusion
  2.8 0.7 reshape.118.norm_ref
  3.5 0.0 copy-start.4
  3.5 0.6 copy-done.4
  4.2 0.0 copy-start.5
  4.2 0.7 copy-done.5
  4.8 0.0 copy-start.7
  4.8 27.7 %project_qkv.1 = (bf16[8192,128]{1,0:T(8,128)(2,1)S(1)}, f32[2048,128]{1,0:T(8,128)S(1)}, f32[2048,128]{1,0:T(8,128)S(1)}) custom-call(bf16[512,4096]{1,0:T(8,128)(2,1)} %bitcast.39, bf16[1,4096]{1,0:T(2,128)(2,1)S(1)} %reshape.118.norm_ref, f32[512,128]{1,0:T(8,128)S(1)} %get-tuple-element.20.cos_ref, f32[512,128]{1,0:T(8,128)S(1)} %get-tuple-element.21.sin_ref, ...), custom_call_target="tpu_custom_call" | custom-call | flops 12884901888 | bytes 25165824 | tf_op jit(solution)/shard_map/project_qkv/pallas_call | solution.py:124
  32.6 0.0 copy-start.1
  32.6 1.0 copy-done.1
  33.5 0.0 copy-done.7
  33.5 0.0 copy-start.2
  33.5 1.2 copy-done.2
  34.8 0.0 copy-start.6
  34.8 56.1 %decode_attention.1 = (bf16[128,1024,128]{2,1,0:T(8,128)(2,1)}, bf16[128,1024,128]{2,1,0:T(8,128)(2,1)}, f32[128,64,128]{2,1,0:T(8,128)S(1)}, f32[128,1,128]{2,1,0:T(1,128)S(1)}) custom-call(s32[32]{0:T(128)S(1)} %add.64.order_ref, s32[128]{0:T(128)S(1)} %broadcast_subtract_fusion.rel_ref, bf16[4,128,16,128]{3,2,1,0:T(8,128)(2,1)S(1)} %bitcast.28, ...), custom_call_target="tpu_custom_call" | custom-call | flops 4294967296 | bytes 134217728 | tf_op jit(solution)/shard_map/decode_attention/pallas_call | solution.py:188
  90.9 0.0 copy-start
  90.9 2.0 copy-done
  92.9 0.0 copy-start.3
  92.9 0.6 copy-done.3
  93.5 1.3 dynamic-slice_bitcast_fusion
  94.8 1.0 copy.19
  95.8 0.0 copy-done.6
  95.8 0.6 reshape.129.gain_ref
  96.5 155.7 %finish_layer.1 = bf16[512,4096]{1,0:T(8,128)(2,1)} custom-call(f32[128,64,128]{2,1,0:T(8,128)} %copy-done, f32[128,128]{1,0:T(8,128)} %bitcast.31, bf16[128,4096]{1,0:T(8,128)(2,1)} %bitcast.37, bf16[1,4096]{1,0:T(2,128)(2,1)} %reshape.129.gain_ref, bf16[2048,4096]{1,0:T(8,128)(2,1)} %wo_hbm.1, bf16[4096,6144]{1,0:T(8,128)(2,1)} %wg_hbm.1, ...), custom_call_target="tpu_custom_call" | custom-call | tf_op jit(solution)/shard_map/finish_layer/pallas_call | solution.py:466
  252.2 4.7 %copy.22 = bf16[4,16,8,4096]{3,2,1,0:T(8,128)(2,1)} copy(bf16[4,16,8,4096]{3,2,0,1:T(8,128)(2,1)} %bitcast.36) | data formatting | bytes 8388608 | tf_op jit(solution)/shard_map/transpose | solution.py:528
  (2 shorter events, 0.0 us)
Async XLA Ops:
  3.5 0.7 copy-start.4
  4.2 0.7 copy-start.5
  4.8 28.7 %copy-start.7 = (s32[128]{0:T(128)S(1)}, s32[128]{0:T(128)}, u32[]{:S(2)}) copy-start(s32[128]{0:T(128)} %param.16) | copy-start | bytes 1540
  32.6 1.0 copy-start.1
  33.5 1.2 copy-start.2
  34.8 61.1 %copy-start.6 = (bf16[4096]{0:T(1024)(128)(2,1)S(1)}, bf16[4096]{0:T(1024)(128)(2,1)}, u32[]{:S(2)}) copy-start(bf16[4096]{0:T(1024)(128)(2,1)} %param.27) | copy-start | bytes 24580
  90.9 2.0 copy-start
  92.9 0.6 copy-start.3

commit v4 on v3

--- a/solution.py
+++ b/solution.py
@@ -207,26 +207,31 @@
 
 
 def tail_kernel(dims, o_ref, ml_ref, x_ref, gain_ref, wo_hbm, wg_hbm, wu_hbm, wd_hbm, out_ref,
-                ring, near1, nml, far1, fml, wts, comb, attn, part_o, recv_o, res, mid, act, part_d, recv_d, fin, across, near, diag,
-                ring_sem, n1s, n1r, nms, nmr, f1s, f1r, fms, fmr, os_, or_, ds_, dr_, xs_, xr_, cs_, cr_, gs_, gr_):
+                ring, near1, nml, far1, fml, wts, comb, attn, part_o, recv_o, res, mid, mid_out, mid_in, act,
+                part_d, other_d, other_in, fin, across, near, diag,
+                ring_sem, n1s, n1r, nms, nmr, f1s, f1r, fms, fmr, os_, or_, ms_, mr_, ps_, pr_, ds_, dr_, xs_, xr_, cs_, cr_, gs_, gr_):
     n_steps, heads, hd, n_chunks, exp_scale, n_slots = dims
     rows_q = n_steps * heads
     own = far1.shape[0]
     per = own // n_chunks
     tok = per * n_steps
     width = x_ref.shape[1]
+    n_tok = x_ref.shape[0]
+    hrows = n_tok // 2
     kt, nt = ring.shape[1], ring.shape[2]
-    n_o = width // nt
-    n_up = act.shape[1] // nt
-    k_up, k_dn = width // kt, act.shape[1] // kt
-    n_dn = width // nt
-    first_up = n_o
-    first_dn = n_o + 2 * k_up * n_up
-    n_loads = first_dn + k_dn * n_dn
+    inner = act.shape[1]
+    n_o, k_o = width // nt, heads * hd // kt
+    n_up, k_up = inner // nt, width // kt
+    n_dn, k_dn = width // nt, inner // kt
+    first_mlp = n_o * k_o
+    up_loads, dn_loads = 2 * k_up * n_up, k_dn * n_dn
+    mlp_loads = up_loads + dn_loads
+    n_loads = first_mlp + 2 * mlp_loads
 
     sp = lax.axis_index('sp')
     tp = lax.axis_index('tp')
-    sp_core = sp + 1 - 2 * lax.rem(sp, 2)
+    core = lax.rem(sp, 2)
+    sp_core = sp + 1 - 2 * core
     sp_chip = lax.rem(sp + 2, 4)
     sp_diag = lax.rem(sp_core + 2, 4)
     to_core = {'sp': sp_core}
@@ -253,34 +258,34 @@
         copy.start()
 
     def load(src, row, col, slot):
-        return pltpu.make_async_copy(src.at[pl.ds(pl.multiple_of(row * kt, kt), kt), pl.ds(pl.multiple_of(col * nt, nt), nt)],
+        return pltpu.make_async_copy(src.at[pl.ds(pl.multiple_of(row, kt), kt), pl.ds(pl.multiple_of(col, nt), nt)],
                                      ring.at[slot], ring_sem.at[slot])
 
     def start(idx):
         slot = lax.rem(idx, n_slots)
 
-        @pl.when(idx < first_up)
+        @pl.when(idx < first_mlp)
         def _():
-            load(wo_hbm, 0, idx, slot).start()
-
-        up = idx - first_up
-        sub = lax.rem(up + 2 * k_up, 2 * k_up)
-        col = (up - sub) // (2 * k_up)
-
-        @pl.when((idx >= first_up) & (idx < first_dn) & (sub < k_up))
+            load(wo_hbm, lax.rem(idx, k_o) * kt, (idx // k_o) * nt, slot).start()
+
+        loc = lax.rem(idx - first_mlp + mlp_loads, mlp_loads)
+        in_mlp = (idx >= first_mlp) & (idx < n_loads)
+        sub = lax.rem(loc, 2 * k_up)
+        up_col = core * inner + (loc // (2 * k_up)) * nt
+
+        @pl.when(in_mlp & (loc < up_loads) & (sub < k_up))
         def _():
-            load(wg_hbm, sub, col, slot).start()
-
-        @pl.when((idx >= first_up) & (idx < first_dn) & (sub >= k_up))
+            load(wg_hbm, sub * kt, up_col, slot).start()
+
+        @pl.when(in_mlp & (loc < up_loads) & (sub >= k_up))
         def _():
-            load(wu_hbm, sub - k_up, col, slot).start()
-
-        dn = idx - first_dn
-        dsub = lax.rem(dn, k_dn)
-
-        @pl.when((idx >= first_dn) & (idx < n_loads))
+            load(wu_hbm, (sub - k_up) * kt, up_col, slot).start()
+
+        dn = loc - up_loads
+
+        @pl.when(in_mlp & (loc >= up_loads))
         def _():
-            load(wd_hbm, dsub, (dn - dsub) // k_dn, slot).start()
+            load(wd_hbm, core * inner + lax.rem(dn, k_dn) * kt, (dn // k_dn) * nt, slot).start()
 
     def arrived(idx):
         slot = lax.rem(idx, n_slots)
@@ -354,20 +359,50 @@
         attn_in = attn[...].astype(jnp.bfloat16)
 
         def o_tile(n, carry, j=j, attn_in=attn_in):
-            if j == 0:
-                arrived(n)
-            part_o[j, :, pl.ds(pl.multiple_of(n * nt, nt), nt)] = jnp.dot(attn_in, ring[n], preferred_element_type=jnp.float32)
+            acc = None
+            for k in range(k_o):
+                if j == 0:
+                    arrived(n * k_o + k)
+                prod = jnp.dot(attn_in[:, k * kt:(k + 1) * kt], ring[n * k_o + k], preferred_element_type=jnp.float32)
+                acc = prod if acc is None else acc + prod
+            part_o[j, :, pl.ds(pl.multiple_of(n * nt, nt), nt)] = acc
             return carry
         lax.fori_loop(0, n_o, o_tile, 0)
         tp_o.append(send(part_o.at[j], recv_o.at[j], os_.at[j], or_.at[j], to_tp))
         tp_o[j].start()
-    start_many(n_slots, n_slots + n_o)
+    start_many(n_slots, n_slots + first_mlp)
+
+    mid_x = [send(mid_out.at[j], mid_in.at[j], ms_.at[j], mr_.at[j], to_core) for j in range(n_chunks)]
+
+    def pair_d(h, t):
+        return send(other_d.at[h, t], other_in.at[h, t], ps_.at[h, t], pr_.at[h, t], to_core)
+
+    def tp_d(h, t):
+        return send(part_d.at[h, t], fin.at[h, t], ds_.at[h, t], dr_.at[h, t], to_tp)
+
+    def chip_d(h, t):
+        return send(fin.at[h, t], across.at[h, t], xs_.at[h, t], xr_.at[h, t], to_chip)
+
+    def core_d(h, t):
+        return send(fin.at[h, t], near.at[h, t], cs_.at[h, t], cr_.at[h, t], to_core)
+
+    def diag_d(h, t):
+        return send(across.at[h, t], diag.at[h, t], gs_.at[h, t], gr_.at[h, t], to_core)
+
+    def cols(t):
+        return pl.ds(t * nt if isinstance(t, int) else pl.multiple_of(t * nt, nt), nt)
+
+    def emit(who, h, t, value):
+        rows = pl.ds(pl.multiple_of(who * n_tok + h * hrows, hrows), hrows)
+        out_ref[rows, cols(t)] = value.astype(out_ref.dtype)
 
     half = 16
-    for j in range(n_chunks):
+
+    def residual(j):
         tp_o[j].wait_recv()
-
-        def norm_rows(i, carry, j=j):
+        h, low = j // 2, (j % 2) * tok
+
+        def norm_rows(i, carry):
             sub = pl.ds(pl.multiple_of(i * half, half), half)
             rows = pl.ds(pl.multiple_of(j * tok + i * half, half), half)
             summed = x_ref[rows, :].astype(jnp.float32) + (part_o[j, sub, :] + recv_o[j, sub, :])
@@ -375,93 +410,162 @@
             res[rows, :] = resid
             wide = resid.astype(jnp.float32)
             inv = lax.rsqrt(jnp.mean(wide * wide, axis=-1, keepdims=True) + NORM_EPS)
-            mid[rows, :] = (wide * inv * gain_ref[...].astype(jnp.float32)).astype(jnp.bfloat16)
+            scaled = wide * inv * gain_ref[...].astype(jnp.float32)
+            mid_out[j, sub, :] = scaled
+            mid[h, pl.ds(pl.multiple_of(low + i * half, half), half), :] = scaled.astype(jnp.bfloat16)
             return carry
         lax.fori_loop(0, tok // half, norm_rows, 0)
-
-    def up_tile(t, carry):
-        idx = first_up + 2 * k_up * t
+        mid_x[j].start()
+
+    def partner(j):
+        mid_x[j].wait_recv()
+        h, low = j // 2, hrows + (j % 2) * tok
+
+        def copy_rows(i, carry):
+            sub = pl.ds(pl.multiple_of(i * half, half), half)
+            mid[h, pl.ds(pl.multiple_of(low + i * half, half), half), :] = mid_in[j, sub, :].astype(jnp.bfloat16)
+            return carry
+        lax.fori_loop(0, tok // half, copy_rows, 0)
+
+    def up_tile(h, t):
+        idx = first_mlp + h * mlp_loads + 2 * k_up * t
         total = []
         for side in (0, 1):
             acc = None
             for k in range(k_up):
                 slot = arrived(idx + side * k_up + k)
-                prod = jnp.dot(mid[:, k * kt:(k + 1) * kt], ring[slot], preferred_element_type=jnp.float32)
+                prod = jnp.dot(mid[h, :, k * kt:(k + 1) * kt], ring[slot], preferred_element_type=jnp.float32)
                 acc = prod if acc is None else acc + prod
             total.append(acc)
         gate, up = total
-        act[:, pl.ds(pl.multiple_of(t * nt, nt), nt)] = (jax.nn.silu(gate) * up).astype(jnp.bfloat16)
+        act[:, cols(t)] = (jax.nn.silu(gate) * up).astype(jnp.bfloat16)
         for k in range(2 * k_up):
             start(idx + k + n_slots)
-        return carry
-
-    lax.fori_loop(0, n_up, up_tile, 0)
-
-    tp_d, chip_d, core_d, diag_d = [], [], [], []
-    for t in range(n_dn):
-        tp_d.append(send(part_d.at[t], recv_d.at[t], ds_.at[t], dr_.at[t], to_tp))
-        chip_d.append(send(fin.at[t], across.at[t], xs_.at[t], xr_.at[t], to_chip))
-        core_d.append(send(fin.at[t], near.at[t], cs_.at[t], cr_.at[t], to_core))
-        diag_d.append(send(across.at[t], diag.at[t], gs_.at[t], gr_.at[t], to_core))
-
-    n_tok = res.shape[0]
-
-    def emit(who, t, value):
-        rows = pl.ds(pl.multiple_of(who * n_tok, n_tok), n_tok)
-        out_ref[rows, t * nt:(t + 1) * nt] = value.astype(out_ref.dtype)
-
-    def down(t):
+
+    def down(h, t):
+        idx = first_mlp + h * mlp_loads + up_loads + k_dn * t
         acc = None
         for k in range(k_dn):
-            slot = arrived(first_dn + k_dn * t + k)
+            slot = arrived(idx + k)
             prod = jnp.dot(act[:, k * kt:(k + 1) * kt], ring[slot], preferred_element_type=jnp.float32)
             acc = prod if acc is None else acc + prod
-        part_d[t] = acc
-        tp_d[t].start()
+        part_d[h, t] = acc[:hrows]
+        other_d[h, t] = acc[hrows:]
+        pair_d(h, t).start()
         for k in range(k_dn):
-            start(jnp.int32(first_dn + k_dn * t + k + n_slots))
-
-    def finish(t):
-        tp_d[t].wait_recv()
-        fin[t] = res[:, t * nt:(t + 1) * nt].astype(jnp.float32) + (part_d[t] + recv_d[t])
-        chip_d[t].start()
-        core_d[t].start()
-        emit(sp, t, fin[t])
-
-    def forward(t):
-        chip_d[t].wait_recv()
-        diag_d[t].start()
-        emit(sp_chip, t, across[t])
-        core_d[t].wait_recv()
-        emit(sp_core, t, near[t])
-
-    for t in range(n_dn):
-        down(t)
-        if t == 5:
-            finish(0)
-    for t in range(1, n_dn):
-        finish(t)
-        forward(t - 1)
-    forward(n_dn - 1)
-    for t in range(n_dn):
-        diag_d[t].wait_recv()
-        emit(sp_diag, t, diag[t])
-    for copy in near_o + [near_ml] + far_o + far_ml + tp_o + tp_d + chip_d + core_d + diag_d:
+            start(idx + k + n_slots)
+
+    def reduce(h, t):
+        pair_d(h, t).wait_recv()
+        part_d[h, t] = part_d[h, t] + other_in[h, t]
+        tp_d(h, t).start()
+
+    def finish(h, t):
+        tp_d(h, t).wait_recv()
+        fin[h, t] = res[h * hrows:(h + 1) * hrows, cols(t)].astype(jnp.float32) + (part_d[h, t] + fin[h, t])
+        chip_d(h, t).start()
+        core_d(h, t).start()
+        emit(sp, h, t, fin[h, t])
+
+    def forward(h, t):
+        chip_d(h, t).wait_recv()
+        diag_d(h, t).start()
+        emit(sp_chip, h, t, across[h, t])
+        core_d(h, t).wait_recv()
+        emit(sp_core, h, t, near[h, t])
+
+    def collect(h, t):
+        diag_d(h, t).wait_recv()
+        emit(sp_diag, h, t, diag[h, t])
+
+    def loop(lo, hi, fn):
+        def one(t, carry):
+            fn(t)
+            return carry
+        lax.fori_loop(lo, hi, one, 0)
+
+    def down_then_reduce(h):
+        def one(t):
+            down(h, t)
+            reduce(h, t - 1)
+        return one
+
+    for j in (0, 1):
+        residual(j)
+    for j in (0, 1):
+        partner(j)
+    loop(0, n_up, lambda t: up_tile(0, t))
+    down(0, 0)
+    loop(1, n_dn, down_then_reduce(0))
+    reduce(0, n_dn - 1)
+
+    for j in (2, 3):
+        residual(j)
+    for j in (2, 3):
+        partner(j)
+    up_tile(1, 0)
+
+    def up_then_finish(t):
+        up_tile(1, t)
+        finish(0, t - 1)
+
+    loop(1, n_up, up_then_finish)
+    down(1, 0)
+    finish(0, n_up - 1)
+
+    def down_more(t):
+        down(1, t)
+        reduce(1, t - 1)
+
+    loop(1, 3, down_more)
+    finish(0, n_up)
+    loop(3, 5, down_more)
+    finish(0, n_up + 1)
+    loop(5, n_dn, down_more)
+    reduce(1, n_dn - 1)
+    loop(0, n_dn // 2, lambda t: forward(0, t))
+
+    def wind_a(t):
+        finish(1, t)
+        forward(0, t + n_dn // 2)
+
+    loop(0, n_dn // 2, wind_a)
+
+    def wind_b(t):
+        finish(1, t)
+        forward(1, t - n_dn // 2)
+        collect(0, t - n_dn // 2)
+
+    loop(n_dn // 2, n_dn, wind_b)
+
+    def wind_c(t):
+        collect(0, t)
+        forward(1, t)
+        collect(1, t - n_dn // 2)
+
+    loop(n_dn // 2, n_dn, wind_c)
+    loop(n_dn // 2, n_dn, lambda t: collect(1, t))
+
+    for copy in near_o + [near_ml] + far_o + far_ml + tp_o + mid_x:
         copy.wait_send()
+    for h in (0, 1):
+        for build in (pair_d, tp_d, chip_d, core_d, diag_d):
+            loop(0, n_dn, lambda t, h=h, build=build: build(h, t).wait_send())
 
 
 def finish_layer(o_part, ml, x_own, norm, w_o, w_gate, w_up, w_down, n_steps, heads, exp_scale):
     n_batch, rows_q, hd = o_part.shape
     tokens, width = x_own.shape
     own = tokens // n_steps
-    inner = w_gate.shape[1]
-    n_chunks, n_slots, kt, nt = 4, 12, 2048, 512
+    inner = w_gate.shape[1] // 2
+    n_chunks, n_slots, kt, nt = 4, 20, 1024, 512
     per = own // n_chunks
     n_dn = width // nt
     vmem = pl.BlockSpec(memory_space=pltpu.VMEM)
     hbm = pl.BlockSpec(memory_space=pl.ANY)
     f32, bf16 = jnp.float32, jnp.bfloat16
-    tiles = pltpu.VMEM((n_dn, tokens, nt), f32)
+    tiles = pltpu.VMEM((2, n_dn, tokens // 2, nt), f32)
+    chunk = pltpu.VMEM((n_chunks, per * n_steps, width), f32)
     dma = pltpu.SemaphoreType.DMA
     return pl.pallas_call(
         functools.partial(tail_kernel, (n_steps, heads, hd, n_chunks, exp_scale, n_slots)),
@@ -473,12 +577,13 @@
                         pltpu.VMEM((own, rows_q, hd), f32), pltpu.VMEM((own, 2 * rows_q), f32),
                         pltpu.VMEM((2, per, 2 * rows_q), f32), pltpu.VMEM((per * rows_q, hd), f32),
                         pltpu.VMEM((per * n_steps, heads * hd), f32),
-                        pltpu.VMEM((n_chunks, per * n_steps, width), f32), pltpu.VMEM((n_chunks, per * n_steps, width), f32),
-                        pltpu.VMEM((tokens, width), bf16), pltpu.VMEM((tokens, width), bf16), pltpu.VMEM((tokens, inner), bf16),
-                        tiles, tiles, tiles, tiles, tiles, tiles,
+                        chunk, chunk,
+                        pltpu.VMEM((tokens, width), bf16), pltpu.VMEM((2, tokens, width), bf16), chunk, chunk,
+                        pltpu.VMEM((tokens, inner), bf16),
+                        tiles, tiles, tiles, tiles, tiles, tiles, tiles,
                         dma((n_slots,)), dma((2 * n_chunks,)), dma((2 * n_chunks,)), dma((1,)), dma((1,)),
                         dma((n_chunks,)), dma((n_chunks,)), dma((n_chunks,)), dma((n_chunks,)), dma((n_chunks,)), dma((n_chunks,)),
-                        dma((n_dn,)), dma((n_dn,)), dma((n_dn,)), dma((n_dn,)), dma((n_dn,)), dma((n_dn,)), dma((n_dn,)), dma((n_dn,))],
+                        dma((n_chunks,)), dma((n_chunks,))] + [dma((2, n_dn))] * 10,
         compiler_params=pltpu.CompilerParams(collective_id=0, has_side_effects=True, vmem_limit_bytes=63 * 2**20),
         name="finish_layer",
     )(o_part, ml, x_own, norm.reshape(1, width), w_o, w_gate, w_up, w_down)

time: 258 us -> 230 us (0.89)
  Pallas kernels: 240 us -> 211 us
    pallas_call x1, Pallas kernels: 156 us -> 127 us  [finish_layer(): pl.pallas_call(functools.partial(tail_kernel, (n_steps, heads, hd, n_chun...]
where the time goes in v4:
time: 230 us; the launch traced here: 229 us
  Pallas kernels  211 us (92%)
  local copies, waits for them, and re-layouts  14.6 us (6%)
    pallas_call x1, Pallas kernels, finish_layer(): pl.pallas_call(functools.partial(tail_kernel, (n_steps, heads, hd, n_chun...  127 us
    pallas_call x1, Pallas kernels, attention(): pl.pallas_call(functools.partial(attn_kernel, dims), grid_spec=pltpu.Pref...  56.1 us
    pallas_call x1, Pallas kernels, project_qkv(): pl.pallas_call(functools.partial(qkv_kernel, (heads, kv_heads, hd, unit,...  27.7 us
    unnamed x16, local copies, waits for them, and re-layouts  6.13 us
    transpose x1, local copies, waits for them, and re-layouts, shard_body(): flat_out.reshape(4 * n_chunks, n_steps, per_chunk, width)  4.7 us

profile of v4, /device:TPU:0, one launch (start us, length us, event | category | flops | bytes accessed | tf_op | source)
XLA Modules:
  0.0 228.7 jit_solution(11433412810139901362)
XLA Ops:
  0.7 0.1 add_multiply_fusion
  0.7 0.1 iota_add_fusion
  0.8 0.1 add.64.order_ref
  0.9 0.7 convert_bitcast_fusion
  1.6 1.0 fusion
  2.6 0.2 pad_maximum_fusion
  2.8 0.7 reshape.118.norm_ref
  3.5 0.0 copy-start.4
  3.5 0.6 copy-done.4
  4.2 0.0 copy-start.5
  4.2 0.7 copy-done.5
  4.8 0.0 copy-start.7
  4.8 27.7 %project_qkv.1 = (bf16[8192,128]{1,0:T(8,128)(2,1)S(1)}, f32[2048,128]{1,0:T(8,128)S(1)}, f32[2048,128]{1,0:T(8,128)S(1)}) custom-call(bf16[512,4096]{1,0:T(8,128)(2,1)} %bitcast.39, bf16[1,4096]{1,0:T(2,128)(2,1)S(1)} %reshape.118.norm_ref, f32[512,128]{1,0:T(8,128)S(1)} %get-tuple-element.20.cos_ref, f32[512,128]{1,0:T(8,128)S(1)} %get-tuple-element.21.sin_ref, ...), custom_call_target="tpu_custom_call" | custom-call | flops 12884901888 | bytes 25165824 | tf_op jit(solution)/shard_map/project_qkv/pallas_call | solution.py:124
  32.6 0.0 copy-start.1
  32.6 1.0 copy-done.1
  33.5 0.0 copy-done.7
  33.5 0.0 copy-start.2
  33.5 1.2 copy-done.2
  34.8 0.0 copy-start.6
  34.8 56.1 %decode_attention.1 = (bf16[128,1024,128]{2,1,0:T(8,128)(2,1)}, bf16[128,1024,128]{2,1,0:T(8,128)(2,1)}, f32[128,64,128]{2,1,0:T(8,128)S(1)}, f32[128,1,128]{2,1,0:T(1,128)S(1)}) custom-call(s32[32]{0:T(128)S(1)} %add.64.order_ref, s32[128]{0:T(128)S(1)} %broadcast_subtract_fusion.rel_ref, bf16[4,128,16,128]{3,2,1,0:T(8,128)(2,1)S(1)} %bitcast.28, ...), custom_call_target="tpu_custom_call" | custom-call | flops 4294967296 | bytes 134217728 | tf_op jit(solution)/shard_map/decode_attention/pallas_call | solution.py:188
  90.9 0.0 copy-start
  90.9 2.0 copy-done
  92.9 0.0 copy-start.3
  92.9 0.6 copy-done.3
  93.5 1.3 dynamic-slice_bitcast_fusion
  94.8 1.0 copy.19
  95.8 0.0 copy-done.6
  95.8 0.6 reshape.129.gain_ref
  96.5 127.5 %finish_layer.1 = bf16[512,4096]{1,0:T(8,128)(2,1)} custom-call(f32[128,64,128]{2,1,0:T(8,128)} %copy-done, f32[128,128]{1,0:T(8,128)} %bitcast.31, bf16[128,4096]{1,0:T(8,128)(2,1)} %bitcast.37, bf16[1,4096]{1,0:T(2,128)(2,1)} %reshape.129.gain_ref, bf16[2048,4096]{1,0:T(8,128)(2,1)} %wo_hbm.1, bf16[4096,6144]{1,0:T(8,128)(2,1)} %wg_hbm.1, ...), custom_call_target="tpu_custom_call" | custom-call | tf_op jit(solution)/shard_map/finish_layer/pallas_call | solution.py:570
  224.0 4.7 %copy.22 = bf16[4,16,8,4096]{3,2,1,0:T(8,128)(2,1)} copy(bf16[4,16,8,4096]{3,2,0,1:T(8,128)(2,1)} %bitcast.36) | data formatting | bytes 8388608 | tf_op jit(solution)/shard_map/transpose | solution.py:633
  (2 shorter events, 0.0 us)
Async XLA Ops:
  3.5 0.7 copy-start.4
  4.2 0.7 copy-start.5
  4.8 28.7 %copy-start.7 = (s32[128]{0:T(128)S(1)}, s32[128]{0:T(128)}, u32[]{:S(2)}) copy-start(s32[128]{0:T(128)} %param.16) | copy-start | bytes 1540
  32.6 1.0 copy-start.1
  33.5 1.2 copy-start.2
  34.8 61.1 %copy-start.6 = (bf16[4096]{0:T(1024)(128)(2,1)S(1)}, bf16[4096]{0:T(1024)(128)(2,1)}, u32[]{:S(2)}) copy-start(bf16[4096]{0:T(1024)(128)(2,1)} %param.27) | copy-start | bytes 24580
  90.9 2.0 copy-start
  92.9 0.6 copy-start.3

commit v5 on v4

--- a/solution.py
+++ b/solution.py
@@ -30,7 +30,7 @@
 
 
 def qkv_kernel(dims, x_ref, norm_ref, cos_ref, sin_ref, qg_ref, kg_ref, wq_hbm, wk_hbm, wv_hbm, q_ref, k_ref, v_ref,
-               n_ref, y_ref, qf_ref, wbuf, sems):
+               n_ref, ya_ref, yb_ref, qf_ref, wbuf, sems):
     heads, kv_heads, hd, unit, n_buf = dims
     tokens = x_ref.shape[0]
     rows_blk = 64
@@ -38,26 +38,16 @@
     n_q, n_kv = heads // per, kv_heads // per
     total = n_q + 2 * n_kv
 
-    def fetch(hbm, col, slot):
-        return pltpu.make_async_copy(hbm.at[:, pl.ds(pl.multiple_of(col * unit, unit), unit)], wbuf.at[slot], sems.at[slot])
-
-    def start(g):
-        slot = lax.rem(g, n_buf)
-
-        @pl.when(g < n_q)
-        def _():
-            fetch(wq_hbm, g, slot).start()
-
-        @pl.when((g >= n_q) & (g < n_q + n_kv))
-        def _():
-            fetch(wk_hbm, g - n_q, slot).start()
-
-        @pl.when((g >= n_q + n_kv) & (g < total))
-        def _():
-            fetch(wv_hbm, g - n_q - n_kv, slot).start()
+    units = [(wk_hbm, g, k_ref, kg_ref) for g in range(n_kv)] + [(wv_hbm, g, v_ref, None) for g in range(n_kv)]
+    units += [(wq_hbm, g, qf_ref, qg_ref) for g in range(n_q)]
+
+    def fetch(g):
+        hbm, col, _, _ = units[g]
+        slot = g % n_buf
+        return pltpu.make_async_copy(hbm.at[:, pl.ds(col * unit, unit)], wbuf.at[slot], sems.at[slot])
 
     for g in range(n_buf - 1):
-        start(jnp.int32(g))
+        fetch(g).start()
 
     def norm_rows(i, carry):
         rows = pl.ds(pl.multiple_of(i * rows_blk, rows_blk), rows_blk)
@@ -68,42 +58,35 @@
 
     lax.fori_loop(0, tokens // rows_blk, norm_rows, 0)
 
-    def project(g):
-        slot = lax.rem(g, n_buf)
-        start(g + n_buf - 1)
-        fetch(wq_hbm, 0, slot).wait()
-        y_ref[...] = jnp.dot(n_ref[...], wbuf[slot], preferred_element_type=jnp.float32)
-
-    def rotate(vec, gain_ref):
+    def rotate(vec, rows, gain_ref):
         inv = lax.rsqrt(jnp.mean(vec * vec, axis=-1, keepdims=True) + NORM_EPS)
         vec = vec * inv * gain_ref[...].astype(jnp.float32)
-        return vec * cos_ref[...] + pltpu.roll(vec, hd // 2, 1) * sin_ref[...]
-
-    def q_unit(g, carry):
-        project(g)
-        for h in range(per):
-            qf_ref[pl.ds(g * per + h, tokens, stride=heads), :] = rotate(y_ref[:, h * hd:(h + 1) * hd], qg_ref)
-        return carry
-
-    lax.fori_loop(0, n_q, q_unit, 0)
-
-    def k_unit(g, carry):
-        project(n_q + g)
-        for h in range(per):
-            row = rotate(y_ref[:, h * hd:(h + 1) * hd], kg_ref).astype(jnp.bfloat16)
-            k_ref[pl.ds(g * per + h, tokens, stride=kv_heads), :] = row.astype(jnp.float32)
-        return carry
-
-    lax.fori_loop(0, n_kv, k_unit, 0)
-
-    def v_unit(g, carry):
-        project(n_q + n_kv + g)
-        for h in range(per):
-            row = y_ref[:, h * hd:(h + 1) * hd].astype(jnp.bfloat16)
-            v_ref[pl.ds(g * per + h, tokens, stride=kv_heads), :] = row.astype(jnp.float32)
-        return carry
-
-    lax.fori_loop(0, n_kv, v_unit, 0)
+        return vec * cos_ref[rows, :] + pltpu.roll(vec, hd // 2, 1) * sin_ref[rows, :]
+
+    def store(g):
+        _, col, dst, gain_ref = units[g]
+        y_ref = (ya_ref, yb_ref)[g % 2]
+        n_heads = heads if dst is qf_ref else kv_heads
+        step = 64
+        for low in range(0, tokens, step):
+            for h in range(per):
+                vec = y_ref[low:low + step, h * hd:(h + 1) * hd]
+                if gain_ref is not None:
+                    vec = rotate(vec, slice(low, low + step), gain_ref)
+                if dst is not qf_ref:
+                    vec = vec.astype(jnp.bfloat16).astype(jnp.float32)
+                dst[pl.ds(low * n_heads + col * per + h, step, stride=n_heads), :] = vec
+
+    for g in range(total):
+        fetch(g).wait()
+        for low in range(0, tokens, tokens // 2):
+            rows = slice(low, low + tokens // 2)
+            (ya_ref, yb_ref)[g % 2][rows, :] = jnp.dot(n_ref[rows, :], wbuf[g % n_buf], preferred_element_type=jnp.float32)
+        if g > 0:
+            store(g - 1)
+        if g + n_buf - 1 < total:
+            fetch(g + n_buf - 1).start()
+    store(total - 1)
 
     def cast_rows(i, carry):
         rows = pl.ds(pl.multiple_of(i * 512, 512), 512)
@@ -130,6 +113,7 @@
                    jax.ShapeDtypeStruct((tokens * kv_heads, hd), jnp.float32)],
         scratch_shapes=[pltpu.VMEM((tokens, width), jnp.bfloat16),
                         pltpu.VMEM((tokens, unit), jnp.float32),
+                        pltpu.VMEM((tokens, unit), jnp.float32),
                         pltpu.VMEM((tokens * heads, hd), jnp.float32),
                         pltpu.VMEM((n_buf, width, unit), jnp.bfloat16),
                         pltpu.SemaphoreType.DMA((n_buf,))],
@@ -139,24 +123,29 @@
     )(x, norm.reshape(1, width), cos_tab, sin_tab, q_gain.reshape(1, hd), k_gain.reshape(1, hd), w_q, w_k, w_v)
 
 
-def attn_kernel(dims, order_ref, rel_ref, q_ref, kn_ref, vn_ref, k_ref, v_ref, ko_ref, vo_ref, o_ref, ml_ref):
+def attn_kernel(dims, order_ref, rel_ref, q_ref, kn_ref, vn_ref, k_ref, v_ref, ko_ref, vo_ref, o_ref, ml_ref,
+                lag_ref, sa_ref, sb_ref, pa_ref, pb_ref):
     n_req, n_steps, heads, kv_heads, groups, rows_c, hd, exp_scale = dims
     rows_q = n_steps * heads
     new_rows = n_steps * kv_heads
+    step_rows = 16
     blk = order_ref[pl.program_id(0)]
 
-    col = lax.broadcasted_iota(jnp.int32, (rows_q, rows_c), 1)
-    row = lax.broadcasted_iota(jnp.int32, (rows_q, rows_c), 0)
-    same_head = (col % kv_heads) == ((row % heads) // groups)
-    lag = jnp.where(same_head, col // kv_heads - row // heads, jnp.int32(1 << 30))
+    @pl.when(pl.program_id(0) == 0)
+    def _():
+        col = lax.broadcasted_iota(jnp.int32, (rows_q, rows_c), 1)
+        row = lax.broadcasted_iota(jnp.int32, (rows_q, rows_c), 0)
+        same_head = (col % kv_heads) == ((row % heads) // groups)
+        lag_ref[...] = jnp.where(same_head, col // kv_heads - row // heads, jnp.int32(1 << 30))
+
     win_row = lax.broadcasted_iota(jnp.int32, (2 * new_rows, hd), 0)
-    ml_lane = lax.broadcasted_iota(jnp.int32, (rows_q, 2 * rows_q), 1)
-    ml_row = lax.broadcasted_iota(jnp.int32, (rows_q, 2 * rows_q), 0)
+    ml_lane = lax.broadcasted_iota(jnp.int32, (step_rows, 2 * rows_q), 1)
+    ml_row = lax.broadcasted_iota(jnp.int32, (step_rows, 2 * rows_q), 0)
     pad = jnp.zeros((new_rows, hd), jnp.float32)
-
-    for j in range(n_req):
-        rel = rel_ref[blk * n_req + j]
-        first = rel * kv_heads
+    rels = [rel_ref[blk * n_req + j] for j in range(n_req)]
+
+    def insert(j):
+        first = rels[j] * kv_heads
         base = pl.multiple_of(jnp.clip((first >> 4) << 4, 0, rows_c - 2 * new_rows), 16)
         off = first - base
         inside = (win_row >= off) & (win_row < off + new_rows)
@@ -166,15 +155,34 @@
             rolled = pltpu.roll(jnp.concatenate(fresh + [pad], axis=0), off & (2 * new_rows - 1), 0)
             window = src[j, pl.ds(base, 2 * new_rows), :].astype(jnp.float32)
             dst[j, pl.ds(base, 2 * new_rows), :] = jnp.where(inside, rolled, window).astype(dst.dtype)
+
+    def score(j):
         query = q_ref[:, j].reshape(rows_q, hd)
-        scores = lax.dot_general(query, ko_ref[j], (((1,), (1,)), ((), ())), preferred_element_type=jnp.float32)
-        scores = jnp.where(lag <= rel, scores, MASKED)
-        top = jnp.maximum(jnp.max(scores, axis=1, keepdims=True), FLOOR)
-        probs = jnp.exp2((scores - top) * exp_scale)
-        total = jnp.sum(probs, axis=1, keepdims=True)
-        o_ref[j] = lax.dot_general(probs.astype(jnp.bfloat16), vo_ref[j], (((1,), (0,)), ((), ())), preferred_element_type=jnp.float32)
-        packed = jnp.where(ml_lane == ml_row, top, jnp.where(ml_lane == ml_row + rows_q, total, 0.0))
-        ml_ref[j] = jnp.sum(packed, axis=0, keepdims=True)
+        (sa_ref, sb_ref)[j % 2][...] = lax.dot_general(query, ko_ref[j], (((1,), (1,)), ((), ())),
+                                                       preferred_element_type=jnp.float32)
+
+    def attend(j):
+        s_ref, p_ref = ((sa_ref, pa_ref), (sb_ref, pb_ref))[j % 2]
+        stats = jnp.zeros((1, 2 * rows_q), jnp.float32)
+        for low in range(0, rows_q, step_rows):
+            rows = slice(low, low + step_rows)
+            scores = jnp.where(lag_ref[rows, :] <= rels[j], s_ref[rows, :], MASKED)
+            top = jnp.maximum(jnp.max(scores, axis=1, keepdims=True), FLOOR)
+            probs = jnp.exp2((scores - top) * exp_scale)
+            total = jnp.sum(probs, axis=1, keepdims=True)
+            p_ref[rows, :] = probs.astype(jnp.bfloat16)
+            packed = jnp.where(ml_lane == ml_row + low, top, jnp.where(ml_lane == ml_row + (low + rows_q), total, 0.0))
+            stats = stats + jnp.sum(packed, axis=0, keepdims=True)
+        ml_ref[j] = stats
+        o_ref[j] = lax.dot_general(p_ref[...], vo_ref[j], (((1,), (0,)), ((), ())), preferred_element_type=jnp.float32)
+
+    for j in range(n_req):
+        insert(j)
+    score(0)
+    for j in range(n_req):
+        if j + 1 < n_req:
+            score(j + 1)
+        attend(j)
 
 
 def attention(order, rel, q, k_new, v_new, k_cache, v_cache, kv_heads, exp_scale, n_req=4):
@@ -195,6 +203,8 @@
             out_specs=[cache_blk, cache_blk,
                        pl.BlockSpec((n_req, rows_q, hd), lambda i, order, rel: (i, 0, 0)),
                        pl.BlockSpec((n_req, 1, 2 * rows_q), lambda i, order, rel: (i, 0, 0))],
+            scratch_shapes=[pltpu.VMEM((rows_q, rows_c), jnp.int32)] + [pltpu.VMEM((rows_q, rows_c), jnp.float32)] * 2
+                           + [pltpu.VMEM((rows_q, rows_c), jnp.bfloat16)] * 2,
         ),
         out_shape=[cache_shape, cache_shape,
                    jax.ShapeDtypeStruct((n_batch, rows_q, hd), jnp.float32),
@@ -207,7 +217,7 @@
 
 
 def tail_kernel(dims, o_ref, ml_ref, x_ref, gain_ref, wo_hbm, wg_hbm, wu_hbm, wd_hbm, out_ref,
-                ring, near1, nml, far1, fml, wts, comb, attn, part_o, recv_o, res, mid, mid_out, mid_in, act,
+                ring, near1, nml, far1, fml, comb, attn, part_o, recv_o, res, mid, mid_out, mid_in, act,
                 part_d, other_d, other_in, fin, across, near, diag,
                 ring_sem, n1s, n1r, nms, nmr, f1s, f1r, fms, fmr, os_, or_, ms_, mr_, ps_, pr_, ds_, dr_, xs_, xr_, cs_, cr_, gs_, gr_):
     n_steps, heads, hd, n_chunks, exp_scale, n_slots = dims
@@ -317,14 +327,9 @@
         base = piece * own + j * per
         near_o[piece * n_chunks + j].wait_recv()
         wt_a, wt_b, stat = weights(nml[base:base + per, :], ml_ref[2 * own + base:2 * own + base + per, :])
-        wts[0] = wt_a
-        wts[1] = wt_b
         nml[base:base + per, :] = stat
-
-        def one(i, carry):
-            near1[base + i] = column(wts[0, pl.ds(i, 1), :]) * near1[base + i] + column(wts[1, pl.ds(i, 1), :]) * o_ref[2 * own + base + i]
-            return carry
-        lax.fori_loop(0, per, one, 0)
+        for i in range(per):
+            near1[base + i] = column(wt_a[i:i + 1]) * near1[base + i] + column(wt_b[i:i + 1]) * o_ref[2 * own + base + i]
 
     near_ml.wait_recv()
     far_o, far_ml = [], []
@@ -345,14 +350,10 @@
         far_o[j].wait_recv()
         wt_a, wt_b, stat = weights(nml[own + base:own + base + per, :], fml[base:base + per, :])
         inv = pltpu.roll(1.0 / stat, rows_q, 1)
-        wts[0] = wt_a * inv
-        wts[1] = wt_b * inv
-
-        def one(i, carry, base=base):
-            rows = pl.ds(pl.multiple_of(i * rows_q, rows_q), rows_q)
-            comb[rows, :] = column(wts[0, pl.ds(i, 1), :]) * near1[own + base + i] + column(wts[1, pl.ds(i, 1), :]) * far1[base + i]
-            return carry
-        lax.fori_loop(0, per, one, 0)
+        wt_a, wt_b = wt_a * inv, wt_b * inv
+        for i in range(per):
+            comb[i * rows_q:(i + 1) * rows_q, :] = (column(wt_a[i:i + 1]) * near1[own + base + i]
+                                                    + column(wt_b[i:i + 1]) * far1[base + i])
         for step in range(n_steps):
             for h in range(heads):
                 attn[step * per:(step + 1) * per, h * hd:(h + 1) * hd] = comb[pl.ds(step * heads + h, per, stride=rows_q), :]
@@ -575,7 +576,7 @@
         scratch_shapes=[pltpu.VMEM((n_slots, kt, nt), bf16),
                         pltpu.VMEM((2 * own, rows_q, hd), f32), pltpu.VMEM((2 * own, 2 * rows_q), f32),
                         pltpu.VMEM((own, rows_q, hd), f32), pltpu.VMEM((own, 2 * rows_q), f32),
-                        pltpu.VMEM((2, per, 2 * rows_q), f32), pltpu.VMEM((per * rows_q, hd), f32),
+                        pltpu.VMEM((per * rows_q, hd), f32),
                         pltpu.VMEM((per * n_steps, heads * hd), f32),
                         chunk, chunk,
                         pltpu.VMEM((tokens, width), bf16), pltpu.VMEM((2, tokens, width), bf16), chunk, chunk,

time: 230 us -> 225 us (0.978)
  Pallas kernels: 211 us -> 207 us
    pallas_call x1, Pallas kernels: 27.7 us -> 23.8 us  [project_qkv(): pl.pallas_call(functools.partial(qkv_kernel, (heads, kv_heads, hd, unit,...]
where the time goes in v5:
time: 225 us; the launch traced here: 224 us
  Pallas kernels  207 us (92%)
  local copies, waits for them, and re-layouts  14.6 us (6%)
    pallas_call x1, Pallas kernels, finish_layer(): pl.pallas_call(functools.partial(tail_kernel, (n_steps, heads, hd, n_chun...  126 us
    pallas_call x1, Pallas kernels, attention(): pl.pallas_call(functools.partial(attn_kernel, dims), grid_spec=pltpu.Pref...  56.7 us
    pallas_call x1, Pallas kernels, project_qkv(): pl.pallas_call(functools.partial(qkv_kernel, (heads, kv_heads, hd, unit,...  23.8 us
    unnamed x16, local copies, waits for them, and re-layouts  6.13 us
    transpose x1, local copies, waits for them, and re-layouts, shard_body(): flat_out.reshape(4 * n_chunks, n_steps, per_chunk, width)  4.7 us

profile of v5, /device:TPU:0, one launch (start us, length us, event | category | flops | bytes accessed | tf_op | source)
XLA Modules:
  0.0 224.3 jit_solution(7276903518891113769)
XLA Ops:
  0.7 0.1 add_multiply_fusion
  0.7 0.1 iota_add_fusion
  0.8 0.1 add.64.order_ref
  0.9 0.7 convert_bitcast_fusion
  1.6 1.0 fusion
  2.6 0.2 pad_maximum_fusion
  2.8 0.7 reshape.118.norm_ref
  3.5 0.0 copy-start.4
  3.5 0.6 copy-done.4
  4.2 0.0 copy-start.5
  4.2 0.7 copy-done.5
  4.8 0.0 copy-start.7
  4.8 23.8 %project_qkv.1 = (bf16[8192,128]{1,0:T(8,128)(2,1)S(1)}, f32[2048,128]{1,0:T(8,128)S(1)}, f32[2048,128]{1,0:T(8,128)S(1)}) custom-call(bf16[512,4096]{1,0:T(8,128)(2,1)} %bitcast.39, bf16[1,4096]{1,0:T(2,128)(2,1)S(1)} %reshape.118.norm_ref, f32[512,128]{1,0:T(8,128)S(1)} %get-tuple-element.20.cos_ref, f32[512,128]{1,0:T(8,128)S(1)} %get-tuple-element.21.sin_ref, ...), custom_call_target="tpu_custom_call" | custom-call | flops 12884901888 | bytes 25165824 | tf_op jit(solution)/shard_map/project_qkv/pallas_call | solution.py:107
  28.6 0.0 copy-start.1
  28.6 1.0 copy-done.1
  29.6 0.0 copy-done.7
  29.6 0.0 copy-start.2
  29.6 1.2 copy-done.2
  30.8 0.0 copy-start.6
  30.8 56.7 %decode_attention.1 = (bf16[128,1024,128]{2,1,0:T(8,128)(2,1)}, bf16[128,1024,128]{2,1,0:T(8,128)(2,1)}, f32[128,64,128]{2,1,0:T(8,128)S(1)}, f32[128,1,128]{2,1,0:T(1,128)S(1)}) custom-call(s32[32]{0:T(128)S(1)} %add.64.order_ref, s32[128]{0:T(128)S(1)} %broadcast_subtract_fusion.rel_ref, bf16[4,128,16,128]{3,2,1,0:T(8,128)(2,1)S(1)} %bitcast.28, ...), custom_call_target="tpu_custom_call" | custom-call | flops 4294967296 | bytes 134217728 | tf_op jit(solution)/shard_map/decode_attention/pallas_call | solution.py:196
  87.6 0.0 copy-start
  87.6 2.0 copy-done
  89.6 0.0 copy-start.3
  89.6 0.6 copy-done.3
  90.2 1.3 dynamic-slice_bitcast_fusion
  91.5 1.0 copy.19
  92.5 0.0 copy-done.6
  92.5 0.6 reshape.129.gain_ref
  93.1 126.4 %finish_layer.1 = bf16[512,4096]{1,0:T(8,128)(2,1)} custom-call(f32[128,64,128]{2,1,0:T(8,128)} %copy-done, f32[128,128]{1,0:T(8,128)} %bitcast.31, bf16[128,4096]{1,0:T(8,128)(2,1)} %bitcast.37, bf16[1,4096]{1,0:T(2,128)(2,1)} %reshape.129.gain_ref, bf16[2048,4096]{1,0:T(8,128)(2,1)} %wo_hbm.1, bf16[4096,6144]{1,0:T(8,128)(2,1)} %wg_hbm.1, ...), custom_call_target="tpu_custom_call" | custom-call | tf_op jit(solution)/shard_map/finish_layer/pallas_call | solution.py:571
  219.6 4.7 %copy.22 = bf16[4,16,8,4096]{3,2,1,0:T(8,128)(2,1)} copy(bf16[4,16,8,4096]{3,2,0,1:T(8,128)(2,1)} %bitcast.36) | data formatting | bytes 8388608 | tf_op jit(solution)/shard_map/transpose | solution.py:634
  (2 shorter events, 0.0 us)
Async XLA Ops:
  3.5 0.7 copy-start.4
  4.2 0.7 copy-start.5
  4.8 24.8 %copy-start.7 = (s32[128]{0:T(128)S(1)}, s32[128]{0:T(128)}, u32[]{:S(2)}) copy-start(s32[128]{0:T(128)} %param.16) | copy-start | bytes 1540
  28.6 1.0 copy-start.1
  29.6 1.2 copy-start.2
  30.8 61.7 %copy-start.6 = (bf16[4096]{0:T(1024)(128)(2,1)S(1)}, bf16[4096]{0:T(1024)(128)(2,1)}, u32[]{:S(2)}) copy-start(bf16[4096]{0:T(1024)(128)(2,1)} %param.27) | copy-start | bytes 24580
  87.6 2.0 copy-start
  89.6 0.6 copy-start.3

commit v6 on v5

--- a/solution.py
+++ b/solution.py
@@ -120,7 +120,7 @@
         compiler_params=pltpu.CompilerParams(vmem_limit_bytes=48 * 2**20),
         cost_estimate=pl.CostEstimate(flops=2 * tokens * width * cols, bytes_accessed=2 * width * cols, transcendentals=0),
         name="project_qkv",
-    )(x, norm.reshape(1, width), cos_tab, sin_tab, q_gain.reshape(1, hd), k_gain.reshape(1, hd), w_q, w_k, w_v)
+    )(x, norm, cos_tab, sin_tab, q_gain.reshape(1, hd), k_gain.reshape(1, hd), w_q, w_k, w_v)
 
 
 def attn_kernel(dims, order_ref, rel_ref, q_ref, kn_ref, vn_ref, k_ref, v_ref, ko_ref, vo_ref, o_ref, ml_ref,
@@ -209,24 +209,23 @@
         out_shape=[cache_shape, cache_shape,
                    jax.ShapeDtypeStruct((n_batch, rows_q, hd), jnp.float32),
                    jax.ShapeDtypeStruct((n_batch, 1, 2 * rows_q), jnp.float32)],
-        compiler_params=pltpu.CompilerParams(dimension_semantics=("arbitrary",), vmem_limit_bytes=40 * 2**20),
+        compiler_params=pltpu.CompilerParams(dimension_semantics=("arbitrary",), vmem_limit_bytes=62 * 2**20),
         cost_estimate=pl.CostEstimate(flops=4 * n_batch * rows_q * rows_c * hd, bytes_accessed=8 * n_batch * rows_c * hd,
                                       transcendentals=n_batch * rows_q * rows_c),
         name="decode_attention",
     )(order, rel, q, k_new, v_new, k_cache, v_cache)
 
 
-def tail_kernel(dims, o_ref, ml_ref, x_ref, gain_ref, wo_hbm, wg_hbm, wu_hbm, wd_hbm, out_ref,
-                ring, near1, nml, far1, fml, comb, attn, part_o, recv_o, res, mid, mid_out, mid_in, act,
+def tail_kernel(dims, o_hbm, ml_hbm, x_hbm, gain_ref, wo_hbm, wg_hbm, wu_hbm, wd_hbm, out_ref,
+                ring, o_ref, ml_ref, x_ref, near1, nml, far1, fml, comb, attn, part_o, recv_o, res, mid, mid_out, mid_in, act,
                 part_d, other_d, other_in, fin, across, near, diag,
-                ring_sem, n1s, n1r, nms, nmr, f1s, f1r, fms, fmr, os_, or_, ms_, mr_, ps_, pr_, ds_, dr_, xs_, xr_, cs_, cr_, gs_, gr_):
+                ring_sem, om_sem, mm_sem, x_sem, n1s, n1r, nms, nmr, f1s, f1r, fms, fmr, os_, or_, ms_, mr_, ps_, pr_, ds_, dr_, xs_, xr_, cs_, cr_, gs_, gr_):
     n_steps, heads, hd, n_chunks, exp_scale, n_slots = dims
     rows_q = n_steps * heads
     own = far1.shape[0]
     per = own // n_chunks
     tok = per * n_steps
-    width = x_ref.shape[1]
-    n_tok = x_ref.shape[0]
+    n_tok, width = res.shape
     hrows = n_tok // 2
     kt, nt = ring.shape[1], ring.shape[2]
     inner = act.shape[1]
@@ -257,15 +256,29 @@
         pl.semaphore_signal(barrier, inc=1, device_id=dev, device_id_type=pl.DeviceIdType.MESH)
     pl.semaphore_wait(barrier, 3)
 
-    near_ml = send(ml_ref.at[pl.ds(0, 2 * own)], nml, nms.at[0], nmr.at[0], to_core)
+    near_ml = send(ml_hbm.at[pl.ds(0, 2 * own)], nml, nms.at[0], nmr.at[0], to_core)
     near_ml.start()
     near_o = []
     for piece in (0, 1):
         for j in range(n_chunks):
             rows = pl.ds(piece * own + j * per, per)
-            near_o.append(send(o_ref.at[rows], near1.at[rows], n1s.at[piece * n_chunks + j], n1r.at[piece * n_chunks + j], to_core))
+            near_o.append(send(o_hbm.at[rows], near1.at[rows], n1s.at[piece * n_chunks + j], n1r.at[piece * n_chunks + j], to_core))
     for copy in near_o:
         copy.start()
+    mine_ml = pltpu.make_async_copy(ml_hbm.at[pl.ds(2 * own, 2 * own)], ml_ref, mm_sem.at[0])
+    mine_ml.start()
+    mine_o = [pltpu.make_async_copy(o_hbm.at[pl.ds((2 + piece) * own, own)], o_ref.at[pl.ds(piece * own, own)], om_sem.at[piece])
+              for piece in (0, 1)]
+    mine_o[0].start()
+    mine_o[1].start()
+
+    def load_x(j, step):
+        return pltpu.make_async_copy(x_hbm.at[step, pl.ds(pl.multiple_of(sp * own + j * per, per), per)], x_ref.at[j * n_steps + step],
+                                     x_sem.at[j * n_steps + step])
+
+    for j in range(n_chunks):
+        for step in range(n_steps):
+            load_x(j, step).start()
 
     def load(src, row, col, slot):
         return pltpu.make_async_copy(src.at[pl.ds(pl.multiple_of(row, kt), kt), pl.ds(pl.multiple_of(col, nt), nt)],
@@ -326,12 +339,14 @@
     def merge_near(piece, j):
         base = piece * own + j * per
         near_o[piece * n_chunks + j].wait_recv()
-        wt_a, wt_b, stat = weights(nml[base:base + per, :], ml_ref[2 * own + base:2 * own + base + per, :])
+        wt_a, wt_b, stat = weights(nml[base:base + per, :], ml_ref[base:base + per, :])
         nml[base:base + per, :] = stat
         for i in range(per):
-            near1[base + i] = column(wt_a[i:i + 1]) * near1[base + i] + column(wt_b[i:i + 1]) * o_ref[2 * own + base + i]
+            near1[base + i] = column(wt_a[i:i + 1]) * near1[base + i] + column(wt_b[i:i + 1]) * o_ref[base + i]
 
     near_ml.wait_recv()
+    mine_ml.wait()
+    mine_o[0].wait()
     far_o, far_ml = [], []
     for j in range(n_chunks):
         rows = pl.ds(j * per, per)
@@ -340,10 +355,13 @@
         far_o.append(send(near1.at[rows], far1.at[rows], f1s.at[j], f1r.at[j], to_chip))
         far_ml[j].start()
         far_o[j].start()
+    mine_o[1].wait()
     for j in range(n_chunks):
         merge_near(1, j)
 
-    tp_o = []
+    def tp_o(j, n):
+        return send(part_o.at[j, n], recv_o.at[j, n], os_.at[j, n], or_.at[j, n], to_tp)
+
     for j in range(n_chunks):
         base = j * per
         far_ml[j].wait_recv()
@@ -366,11 +384,10 @@
                     arrived(n * k_o + k)
                 prod = jnp.dot(attn_in[:, k * kt:(k + 1) * kt], ring[n * k_o + k], preferred_element_type=jnp.float32)
                 acc = prod if acc is None else acc + prod
-            part_o[j, :, pl.ds(pl.multiple_of(n * nt, nt), nt)] = acc
+            part_o[j, n] = acc
+            tp_o(j, n).start()
             return carry
         lax.fori_loop(0, n_o, o_tile, 0)
-        tp_o.append(send(part_o.at[j], recv_o.at[j], os_.at[j], or_.at[j], to_tp))
-        tp_o[j].start()
     start_many(n_slots, n_slots + first_mlp)
 
     mid_x = [send(mid_out.at[j], mid_in.at[j], ms_.at[j], mr_.at[j], to_core) for j in range(n_chunks)]
@@ -394,19 +411,32 @@
         return pl.ds(t * nt if isinstance(t, int) else pl.multiple_of(t * nt, nt), nt)
 
     def emit(who, h, t, value):
-        rows = pl.ds(pl.multiple_of(who * n_tok + h * hrows, hrows), hrows)
-        out_ref[rows, cols(t)] = value.astype(out_ref.dtype)
+        for c in (0, 1):
+            for step in range(n_steps):
+                low = c * tok + step * per
+                out_ref[step * 4 * n_chunks + who * n_chunks + 2 * h + c, :, cols(t)] = value[low:low + per].astype(out_ref.dtype)
+
+    def loop(lo, hi, fn):
+        def one(t, carry):
+            fn(t)
+            return carry
+        lax.fori_loop(lo, hi, one, 0)
 
     half = 16
 
     def residual(j):
-        tp_o[j].wait_recv()
+        for step in range(n_steps):
+            load_x(j, step).wait()
+        loop(0, n_o, lambda n: tp_o(j, n).wait_recv())
         h, low = j // 2, (j % 2) * tok
 
         def norm_rows(i, carry):
             sub = pl.ds(pl.multiple_of(i * half, half), half)
             rows = pl.ds(pl.multiple_of(j * tok + i * half, half), half)
-            summed = x_ref[rows, :].astype(jnp.float32) + (part_o[j, sub, :] + recv_o[j, sub, :])
+            base = j * n_steps + i * (half // per)
+            x_rows = jnp.concatenate([x_ref[base + g].astype(jnp.float32) for g in range(half // per)], axis=0)
+            proj = jnp.concatenate([part_o[j, n, sub, :] + recv_o[j, n, sub, :] for n in range(n_o)], axis=1)
+            summed = x_rows + proj
             resid = summed.astype(jnp.bfloat16)
             res[rows, :] = resid
             wide = resid.astype(jnp.float32)
@@ -479,12 +509,6 @@
         diag_d(h, t).wait_recv()
         emit(sp_diag, h, t, diag[h, t])
 
-    def loop(lo, hi, fn):
-        def one(t, carry):
-            fn(t)
-            return carry
-        lax.fori_loop(lo, hi, one, 0)
-
     def down_then_reduce(h):
         def one(t):
             down(h, t)
@@ -547,17 +571,20 @@
     loop(n_dn // 2, n_dn, wind_c)
     loop(n_dn // 2, n_dn, lambda t: collect(1, t))
 
-    for copy in near_o + [near_ml] + far_o + far_ml + tp_o + mid_x:
+    for copy in near_o + [near_ml] + far_o + far_ml + mid_x:
         copy.wait_send()
+    for j in range(n_chunks):
+        loop(0, n_o, lambda n, j=j: tp_o(j, n).wait_send())
     for h in (0, 1):
         for build in (pair_d, tp_d, chip_d, core_d, diag_d):
             loop(0, n_dn, lambda t, h=h, build=build: build(h, t).wait_send())
 
 
-def finish_layer(o_part, ml, x_own, norm, w_o, w_gate, w_up, w_down, n_steps, heads, exp_scale):
+def finish_layer(o_part, ml, hidden, norm, w_o, w_gate, w_up, w_down, heads, exp_scale):
     n_batch, rows_q, hd = o_part.shape
-    tokens, width = x_own.shape
-    own = tokens // n_steps
+    n_steps, _, width = hidden.shape
+    own = n_batch // 4
+    tokens = own * n_steps
     inner = w_gate.shape[1] // 2
     n_chunks, n_slots, kt, nt = 4, 20, 1024, 512
     per = own // n_chunks
@@ -567,27 +594,31 @@
     f32, bf16 = jnp.float32, jnp.bfloat16
     tiles = pltpu.VMEM((2, n_dn, tokens // 2, nt), f32)
     chunk = pltpu.VMEM((n_chunks, per * n_steps, width), f32)
+    o_tiles = pltpu.VMEM((n_chunks, n_dn, per * n_steps, nt), f32)
     dma = pltpu.SemaphoreType.DMA
     return pl.pallas_call(
         functools.partial(tail_kernel, (n_steps, heads, hd, n_chunks, exp_scale, n_slots)),
-        in_specs=[vmem] * 4 + [hbm] * 4,
+        in_specs=[hbm] * 3 + [vmem] + [hbm] * 4,
         out_specs=vmem,
-        out_shape=jax.ShapeDtypeStruct((4 * tokens, width), bf16),
+        out_shape=jax.ShapeDtypeStruct((n_steps * n_batch // per, per, width), bf16),
         scratch_shapes=[pltpu.VMEM((n_slots, kt, nt), bf16),
+                        pltpu.VMEM((2 * own, rows_q, hd), f32), pltpu.VMEM((2 * own, 2 * rows_q), f32),
+                        pltpu.VMEM((n_chunks * n_steps, per, width), bf16),
                         pltpu.VMEM((2 * own, rows_q, hd), f32), pltpu.VMEM((2 * own, 2 * rows_q), f32),
                         pltpu.VMEM((own, rows_q, hd), f32), pltpu.VMEM((own, 2 * rows_q), f32),
                         pltpu.VMEM((per * rows_q, hd), f32),
                         pltpu.VMEM((per * n_steps, heads * hd), f32),
-                        chunk, chunk,
+                        o_tiles, o_tiles,
                         pltpu.VMEM((tokens, width), bf16), pltpu.VMEM((2, tokens, width), bf16), chunk, chunk,
                         pltpu.VMEM((tokens, inner), bf16),
                         tiles, tiles, tiles, tiles, tiles, tiles, tiles,
-                        dma((n_slots,)), dma((2 * n_chunks,)), dma((2 * n_chunks,)), dma((1,)), dma((1,)),
-                        dma((n_chunks,)), dma((n_chunks,)), dma((n_chunks,)), dma((n_chunks,)), dma((n_chunks,)), dma((n_chunks,)),
+                        dma((n_slots,)), dma((2,)), dma((1,)), dma((n_chunks * n_steps,)),
+                        dma((2 * n_chunks,)), dma((2 * n_chunks,)), dma((1,)), dma((1,)),
+                        dma((n_chunks,)), dma((n_chunks,)), dma((n_chunks,)), dma((n_chunks,)), dma((n_chunks, n_dn)), dma((n_chunks, n_dn)),
                         dma((n_chunks,)), dma((n_chunks,))] + [dma((2, n_dn))] * 10,
         compiler_params=pltpu.CompilerParams(collective_id=0, has_side_effects=True, vmem_limit_bytes=63 * 2**20),
         name="finish_layer",
-    )(o_part, ml, x_own, norm.reshape(1, width), w_o, w_gate, w_up, w_down)
+    )(o_part, ml, hidden, norm, w_o, w_gate, w_up, w_down)
 
 
 def solution(mesh):
@@ -610,13 +641,14 @@
 
         tok_pos = (start_pos[None, :] + jnp.arange(n_steps, dtype=jnp.int32)[:, None]).reshape(-1)
         cos_tab, sin_tab = rope_tables(tok_pos, hd)
-        q_rows, k_rows, v_rows = project_qkv(hidden.reshape(n_steps * n_batch, width), attn_norm, cos_tab, sin_tab,
+        norms = jnp.stack([attn_norm, mlp_norm]).astype(jnp.float32)
+        q_rows, k_rows, v_rows = project_qkv(hidden.reshape(n_steps * n_batch, width), norms[:1], cos_tab, sin_tab,
                                              q_gain, k_gain, w_q, w_k, w_v)
         q_rot = q_rows.reshape(n_steps, n_batch, heads, hd)
         k_rows = k_rows.reshape(n_steps, n_batch * kv_heads, hd)
         v_rows = v_rows.reshape(n_steps, n_batch * kv_heads, hd)
 
-        n_req = 4
+        n_req = 8
         per = own // n_req
         part = jnp.stack([(1 - chip) * 2 + (1 - core), chip * 2 + (1 - core), (1 - chip) * 2 + core, chip * 2 + core])
         order = (part[:, None] * per + jnp.arange(per)[None, :]).reshape(-1).astype(jnp.int32)
@@ -625,13 +657,8 @@
         k_out, v_out, o_part, ml = attention(order, rel, q_rot, k_rows, v_rows, k_cache.reshape(flat), v_cache.reshape(flat),
                                              kv_heads, exp_scale, n_req)
 
-        n_chunks = 4
-        per_chunk = own // n_chunks
-        x_own = lax.dynamic_slice_in_dim(hidden, sp * own, own, axis=1).reshape(n_steps, n_chunks, per_chunk, width)
-        x_own = x_own.transpose(1, 0, 2, 3).reshape(n_steps * own, width)
-        flat_out = finish_layer(o_part, ml.reshape(n_batch, 2 * rows_q), x_own, mlp_norm, w_o, w_gate, w_up, w_down,
-                                n_steps, heads, exp_scale)
-        hid_out = flat_out.reshape(4 * n_chunks, n_steps, per_chunk, width).transpose(1, 0, 2, 3).reshape(n_steps, n_batch, width)
+        hid_out = finish_layer(o_part, ml.reshape(n_batch, 2 * rows_q), hidden, norms[1:], w_o, w_gate, w_up, w_down,
+                               heads, exp_scale).reshape(hidden.shape)
         return hid_out, k_out.reshape(k_cache.shape), v_out.reshape(v_cache.shape)
 
     return jax.shard_map(shard_body, mesh=mesh, in_specs=in_specs, out_specs=out_specs, check_vma=False)

time: 225 us -> 222 us (0.987)
  local copies, waits for them, and re-layouts: 14.6 us -> 11.9 us
    transpose x3 -> x0, local copies, waits for them, and re-layouts: 7.03 us -> none  [the longest x1 4.7 us: shard_body(): flat_out.reshape(4 * n_chunks, n_steps, per_chunk, width)]
    pallas_call x1, Pallas kernels: 126 us -> 123 us  [finish_layer(): pl.pallas_call(functools.partial(tail_kernel, (n_steps, heads, hd, n_chun...]
    unnamed x16 -> x11, local copies, waits for them, and re-layouts: 6.13 us -> 9.31 us
    pallas_call x1, Pallas kernels: 56.7 us -> 59.1 us  [attention(): pl.pallas_call(functools.partial(attn_kernel, dims), grid_spec=pltpu.Pref...]
where the time goes in v6:
time: 222 us; the launch traced here: 221 us
  Pallas kernels  206 us (93%)
  local copies, waits for them, and re-layouts  11.9 us (5%)
  other arithmetic  3.23 us (1%)
    pallas_call x1, Pallas kernels, finish_layer(): pl.pallas_call(functools.partial(tail_kernel, (n_steps, heads, hd, n_chun...  123 us
    pallas_call x1, Pallas kernels, attention(): pl.pallas_call(functools.partial(attn_kernel, dims), grid_spec=pltpu.Pref...  59.1 us
    pallas_call x1, Pallas kernels, project_qkv(): pl.pallas_call(functools.partial(qkv_kernel, (heads, kv_heads, hd, unit,...  23.6 us
    unnamed x11, local copies, waits for them, and re-layouts  9.31 us

profile of v6, /device:TPU:0, one launch (start us, length us, event | category | flops | bytes accessed | tf_op | source)
XLA Modules:
  0.0 221.5 jit_solution(18267489135596842817)
XLA Ops:
  0.7 0.1 add_multiply_fusion
  0.7 1.2 broadcast_subtract_fusion.rel_ref
  1.9 0.1 iota_add_fusion
  2.0 0.6 add.61.order_ref
  2.6 0.7 convert_bitcast_fusion
  3.2 0.7 stack.29
  3.9 0.7 stack.30
  4.7 0.6 fusion.1
  5.3 1.0 fusion
  6.3 0.2 pad_maximum_fusion
  6.5 0.0 copy-start.3
  6.5 0.6 copy-done.3
  7.2 0.0 copy-start.4
  7.2 0.7 copy-done.4
  7.8 23.6 %project_qkv.1 = (bf16[8192,128]{1,0:T(8,128)(2,1)S(1)}, f32[2048,128]{1,0:T(8,128)S(1)}, f32[2048,128]{1,0:T(8,128)S(1)}) custom-call(bf16[512,4096]{1,0:T(8,128)(2,1)} %bitcast.26, f32[1,4096]{1,0:T(1,128)S(1)} %get-tuple-element.18.norm_ref, f32[512,128]{1,0:T(8,128)S(1)} %get-tuple-element.22.cos_ref, f32[512,128]{1,0:T(8,128)S(1)} %get-tuple-element.23.sin_ref, ...), custom_call_target="tpu_custom_call" | custom-call | flops 12884901888 | bytes 25165824 | tf_op jit(solution)/shard_map/project_qkv/pallas_call | solution.py:107
  31.5 0.0 copy-start
  31.5 1.3 copy-done
  32.8 0.0 copy-start.1
  32.8 1.0 copy-done.1
  33.8 0.0 copy-start.2
  33.8 1.0 copy-done.2
  34.8 59.1 %decode_attention.1 = (bf16[128,1024,128]{2,1,0:T(8,128)(2,1)}, bf16[128,1024,128]{2,1,0:T(8,128)(2,1)}, f32[128,64,128]{2,1,0:T(8,128)}, f32[128,1,128]{2,1,0:T(1,128)}) custom-call(s32[16]{0:T(128)} %add.61.order_ref, s32[128]{0:T(128)} %broadcast_subtract_fusion.rel_ref, bf16[4,128,16,128]{3,2,1,0:T(8,128)(2,1)} %bitcast.18, f32[4,512,128]{2,1,0:T(8,128)} %bitcast.19, ...), custom_call_target="tpu_custom_call" | custom-call | flops 4294967296 | bytes 134217728 | tf_op jit(solution)/shard_map/decode_attention/pallas_call | solution.py:196
  93.9 122.9 %finish_layer.1 = bf16[64,8,4096]{2,1,0:T(8,128)(2,1)} custom-call(f32[128,64,128]{2,1,0:T(8,128)} %get-tuple-element.13.o_hbm, f32[128,128]{1,0:T(8,128)} %bitcast.27, bf16[4,128,4096]{2,1,0:T(8,128)(2,1)} %x_hbm.1, f32[1,4096]{1,0:T(1,128)} %get-tuple-element.17.gain_ref, bf16[2048,4096]{1,0:T(8,128)(2,1)} %wo_hbm.1, bf16[4096,6144]{1,0:T(8,128)(2,1)} %wg_hbm.1, ...), custom_call_target="tpu_custom_call" | custom-call | tf_op jit(solution)/shard_map/finish_layer/pallas_call | solution.py:599
  216.8 4.7 %copy.19 = bf16[4,128,4096]{2,1,0:T(8,128)(2,1)} copy(bf16[4,128,4096]{2,1,0:T(8,128)(2,1)} %bitcast.25) | data formatting | bytes 8388608
  (2 shorter events, 0.1 us)
Async XLA Ops:
  6.5 0.7 copy-start.3
  7.2 0.7 copy-start.4
  31.5 1.3 copy-start
  32.8 1.0 copy-start.1
  33.8 1.0 copy-start.2

commit v7 on v6

--- a/solution.py
+++ b/solution.py
@@ -117,19 +117,43 @@
                         pltpu.VMEM((tokens * heads, hd), jnp.float32),
                         pltpu.VMEM((n_buf, width, unit), jnp.bfloat16),
                         pltpu.SemaphoreType.DMA((n_buf,))],
-        compiler_params=pltpu.CompilerParams(vmem_limit_bytes=48 * 2**20),
+        compiler_params=pltpu.CompilerParams(vmem_limit_bytes=62 * 2**20),
         cost_estimate=pl.CostEstimate(flops=2 * tokens * width * cols, bytes_accessed=2 * width * cols, transcendentals=0),
         name="project_qkv",
     )(x, norm, cos_tab, sin_tab, q_gain.reshape(1, hd), k_gain.reshape(1, hd), w_q, w_k, w_v)
 
 
-def attn_kernel(dims, order_ref, rel_ref, q_ref, kn_ref, vn_ref, k_ref, v_ref, ko_ref, vo_ref, o_ref, ml_ref,
-                lag_ref, sa_ref, sb_ref, pa_ref, pb_ref):
+def attn_kernel(dims, order_ref, rel_ref, q_ref, kn_ref, vn_ref, k_hbm, v_hbm, ko_ref, vo_ref, o_ref, ml_ref,
+                lag_ref, sa_ref, sb_ref, pa_ref, pb_ref, k_buf, v_buf, sems):
     n_req, n_steps, heads, kv_heads, groups, rows_c, hd, exp_scale = dims
     rows_q = n_steps * heads
     new_rows = n_steps * kv_heads
     step_rows = 16
-    blk = order_ref[pl.program_id(0)]
+    n_buf = k_buf.shape[0]
+    here = pl.program_id(0)
+    last = pl.num_programs(0)
+    blk = order_ref[here]
+    k_ref, v_ref = k_buf.at[lax.rem(here, n_buf)], v_buf.at[lax.rem(here, n_buf)]
+
+    def fetch(step):
+        slot = lax.rem(step, n_buf)
+        reqs = pl.ds(order_ref[step] * n_req, n_req)
+        return (pltpu.make_async_copy(k_hbm.at[reqs], k_buf.at[slot], sems.at[0, slot]),
+                pltpu.make_async_copy(v_hbm.at[reqs], v_buf.at[slot], sems.at[1, slot]))
+
+    def begin(step):
+        for copy in fetch(step):
+            copy.start()
+
+    @pl.when(here == 0)
+    def _():
+        for step in range(n_buf - 1):
+            begin(jnp.int32(step))
+
+    @pl.when(here + n_buf - 1 < last)
+    def _():
+        begin(here + n_buf - 1)
+
 
     @pl.when(pl.program_id(0) == 0)
     def _():
@@ -176,6 +200,8 @@
         ml_ref[j] = stats
         o_ref[j] = lax.dot_general(p_ref[...], vo_ref[j], (((1,), (0,)), ((), ())), preferred_element_type=jnp.float32)
 
+    for copy in fetch(here):
+        copy.wait()
     for j in range(n_req):
         insert(j)
     score(0)
@@ -191,6 +217,9 @@
     rows_q = n_steps * heads
     dims = (n_req, n_steps, heads, kv_heads, heads // kv_heads, rows_c, hd, exp_scale)
     cache_blk = pl.BlockSpec((n_req, rows_c, hd), lambda i, order, rel: (order[i], 0, 0))
+    cache_in = pl.BlockSpec(memory_space=pl.ANY)
+    n_buf = 4
+    cache_buf = pltpu.VMEM((n_buf, n_req, rows_c, hd), k_cache.dtype)
     new_blk = pl.BlockSpec((n_steps, n_req * kv_heads, hd), lambda i, order, rel: (0, order[i], 0))
     cache_shape = jax.ShapeDtypeStruct(k_cache.shape, k_cache.dtype)
     return pl.pallas_call(
@@ -199,12 +228,13 @@
             num_scalar_prefetch=2,
             grid=(n_batch // n_req,),
             in_specs=[pl.BlockSpec((n_steps, n_req, heads, hd), lambda i, order, rel: (0, order[i], 0, 0)),
-                      new_blk, new_blk, cache_blk, cache_blk],
+                      new_blk, new_blk, cache_in, cache_in],
             out_specs=[cache_blk, cache_blk,
                        pl.BlockSpec((n_req, rows_q, hd), lambda i, order, rel: (i, 0, 0)),
                        pl.BlockSpec((n_req, 1, 2 * rows_q), lambda i, order, rel: (i, 0, 0))],
             scratch_shapes=[pltpu.VMEM((rows_q, rows_c), jnp.int32)] + [pltpu.VMEM((rows_q, rows_c), jnp.float32)] * 2
-                           + [pltpu.VMEM((rows_q, rows_c), jnp.bfloat16)] * 2,
+                           + [pltpu.VMEM((rows_q, rows_c), jnp.bfloat16)] * 2
+                           + [cache_buf, cache_buf, pltpu.SemaphoreType.DMA((2, n_buf))],
         ),
         out_shape=[cache_shape, cache_shape,
                    jax.ShapeDtypeStruct((n_batch, rows_q, hd), jnp.float32),
@@ -641,14 +671,13 @@
 
         tok_pos = (start_pos[None, :] + jnp.arange(n_steps, dtype=jnp.int32)[:, None]).reshape(-1)
         cos_tab, sin_tab = rope_tables(tok_pos, hd)
-        norms = jnp.stack([attn_norm, mlp_norm]).astype(jnp.float32)
-        q_rows, k_rows, v_rows = project_qkv(hidden.reshape(n_steps * n_batch, width), norms[:1], cos_tab, sin_tab,
+        q_rows, k_rows, v_rows = project_qkv(hidden.reshape(n_steps * n_batch, width), attn_norm.reshape(1, width), cos_tab, sin_tab,
                                              q_gain, k_gain, w_q, w_k, w_v)
         q_rot = q_rows.reshape(n_steps, n_batch, heads, hd)
         k_rows = k_rows.reshape(n_steps, n_batch * kv_heads, hd)
         v_rows = v_rows.reshape(n_steps, n_batch * kv_heads, hd)
 
-        n_req = 8
+        n_req = 4
         per = own // n_req
         part = jnp.stack([(1 - chip) * 2 + (1 - core), chip * 2 + (1 - core), (1 - chip) * 2 + core, chip * 2 + core])
         order = (part[:, None] * per + jnp.arange(per)[None, :]).reshape(-1).astype(jnp.int32)
@@ -657,7 +686,7 @@
         k_out, v_out, o_part, ml = attention(order, rel, q_rot, k_rows, v_rows, k_cache.reshape(flat), v_cache.reshape(flat),
                                              kv_heads, exp_scale, n_req)
 
-        hid_out = finish_layer(o_part, ml.reshape(n_batch, 2 * rows_q), hidden, norms[1:], w_o, w_gate, w_up, w_down,
+        hid_out = finish_layer(o_part, ml.reshape(n_batch, 2 * rows_q), hidden, mlp_norm.reshape(1, width), w_o, w_gate, w_up, w_down,
                                heads, exp_scale).reshape(hidden.shape)
         return hid_out, k_out.reshape(k_cache.shape), v_out.reshape(v_cache.shape)
 

time: 222 us -> 212 us (0.955)
  Pallas kernels: 206 us -> 200 us
  local copies, waits for them, and re-layouts: 11.9 us -> 7.21 us
    pallas_call x1, Pallas kernels: 59.1 us -> 51 us  [attention(): pl.pallas_call(functools.partial(attn_kernel, dims), grid_spec=pltpu.Pref...]
    unnamed x11 -> x5, local copies, waits for them, and re-layouts: 9.31 us -> 4.71 us
    pallas_call x1, Pallas kernels: 23.6 us -> 25.9 us  [project_qkv(): pl.pallas_call(functools.partial(qkv_kernel, (heads, kv_heads, hd, unit,...]
where the time goes in v7:
time: 212 us; the launch traced here: 211 us
  Pallas kernels  200 us (94%)
  local copies, waits for them, and re-layouts  7.21 us (3%)
  other arithmetic  3.39 us (2%)
    pallas_call x1, Pallas kernels, finish_layer(): pl.pallas_call(functools.partial(tail_kernel, (n_steps, heads, hd, n_chun...  123 us
    pallas_call x1, Pallas kernels, attention(): pl.pallas_call(functools.partial(attn_kernel, dims), grid_spec=pltpu.Pref...  51 us
    pallas_call x1, Pallas kernels, project_qkv(): pl.pallas_call(functools.partial(qkv_kernel, (heads, kv_heads, hd, unit,...  25.9 us
    unnamed x5, local copies, waits for them, and re-layouts  4.71 us

profile of v7, /device:TPU:0, one launch (start us, length us, event | category | flops | bytes accessed | tf_op | source)
XLA Modules:
  0.0 211.0 jit_solution(6047695709899669502)
XLA Ops:
  0.7 0.1 add_multiply_fusion
  0.7 0.1 iota_add_fusion
  0.8 0.6 add.61.order_ref
  1.4 0.7 convert_bitcast_fusion
  2.1 1.0 fusion
  3.1 1.0 pad_maximum_fusion
  4.1 1.3 reshape.109.norm_ref
  5.4 0.0 copy-start.1
  5.4 25.9 %project_qkv.1 = (bf16[8192,128]{1,0:T(8,128)(2,1)}, f32[2048,128]{1,0:T(8,128)}, f32[2048,128]{1,0:T(8,128)}) custom-call(bf16[512,4096]{1,0:T(8,128)(2,1)} %bitcast.21, bf16[1,4096]{1,0:T(2,128)(2,1)} %reshape.109.norm_ref, f32[512,128]{1,0:T(8,128)} %get-tuple-element.20.cos_ref, f32[512,128]{1,0:T(8,128)} %get-tuple-element.21.sin_ref, ...), custom_call_target="tpu_custom_call" | custom-call | flops 12884901888 | bytes 25165824 | tf_op jit(solution)/shard_map/project_qkv/pallas_call | solution.py:107
  31.3 0.0 copy-done.1
  31.3 0.6 broadcast_subtract_fusion.rel_ref
  31.9 0.0 copy-start
  31.9 51.0 %decode_attention.1 = (bf16[128,1024,128]{2,1,0:T(8,128)(2,1)}, bf16[128,1024,128]{2,1,0:T(8,128)(2,1)}, f32[128,64,128]{2,1,0:T(8,128)}, f32[128,1,128]{2,1,0:T(1,128)}) custom-call(s32[32]{0:T(128)} %add.61.order_ref, s32[128]{0:T(128)} %broadcast_subtract_fusion.rel_ref, bf16[4,128,16,128]{3,2,1,0:T(8,128)(2,1)} %bitcast.22, f32[4,512,128]{2,1,0:T(8,128)} %bitcast.23, ...), custom_call_target="tpu_custom_call" | custom-call | flops 4294967296 | bytes 134217728 | tf_op jit(solution)/shard_map/decode_attention/pallas_call | solution.py:225
  82.9 0.0 copy-done
  82.9 0.6 reshape.118.gain_ref
  83.5 122.8 %finish_layer.1 = bf16[64,8,4096]{2,1,0:T(8,128)(2,1)} custom-call(f32[128,64,128]{2,1,0:T(8,128)} %get-tuple-element.13.o_hbm, f32[128,128]{1,0:T(8,128)} %bitcast.25, bf16[4,128,4096]{2,1,0:T(8,128)(2,1)} %x_hbm.1, bf16[1,4096]{1,0:T(2,128)(2,1)} %reshape.118.gain_ref, bf16[2048,4096]{1,0:T(8,128)(2,1)} %wo_hbm.1, bf16[4096,6144]{1,0:T(8,128)(2,1)} %wg_hbm.1, ...), custom_call_target="tpu_custom_call" | custom-call | tf_op jit(solution)/shard_map/finish_layer/pallas_call | solution.py:629
  206.3 4.7 %copy.19 = bf16[4,128,4096]{2,1,0:T(8,128)(2,1)} copy(bf16[4,128,4096]{2,1,0:T(8,128)(2,1)} %bitcast.20) | data formatting | bytes 8388608
  (1 shorter events, 0.0 us)
Async XLA Ops:
  5.4 25.9 %copy-start.1 = (s32[128]{0:T(128)S(1)}, s32[128]{0:T(128)}, u32[]{:S(2)}) copy-start(s32[128]{0:T(128)} %param.16) | copy-start | bytes 1540
  31.9 51.0 %copy-start = (bf16[4096]{0:T(1024)(128)(2,1)S(1)}, bf16[4096]{0:T(1024)(128)(2,1)}, u32[]{:S(2)}) copy-start(bf16[4096]{0:T(1024)(128)(2,1)} %param.27) | copy-start | bytes 24580
